TPU v7x, 128 devices: a whole 4x4x4 slice. The times are simulated.
128 devices in a mesh: dp: 8 (over x, z_lo), rep: 16 (over z_hi, y, core).
Axes of the slice: x: 4, y: 4, z: 4 (z_hi: 2, z_lo: 2; z = z_hi * 2 + z_lo), core: 2. Of those that a mesh axis runs over, the one named last changes fastest.
Arguments:
- queries: bfloat16 [65536, 2048], P(('dp', 'rep')), may hold values from -32 to 32
- key_rows: bfloat16 [65536, 2048], P(('dp', 'rep')), may hold values from -32 to 32
- values: bfloat16 [65536, 2048], P(('dp', 'rep')), may hold values from -6 to 6
- upstream: bfloat16 [65536, 2048], P(('dp', 'rep')), may hold values from -24 to 24
- out_weight: bfloat16 [2048, 2048], P(('dp', 'rep')), may hold values from -0.125 to 0.125
- sample_ids: int32 [128, 512], P(('dp', 'rep')), may hold values from 0 to 3, as said below
Outputs:
- grad_queries: bfloat16 [65536, 2048], P(('dp', 'rep'))
- grad_keys: bfloat16 [65536, 2048], P(('dp', 'rep'))
- grad_values: bfloat16 [65536, 2048], P(('dp', 'rep'))
- grad_weight: float32 [2048, 2048], P(('dp', 'rep'))
Inputs may be any that keep to these rules, and one draw needn't show every extreme that they name: `sample_ids`: within a row the ids never fall, every row starts with 0 and ends with 3, and the tokens of one sample are contiguous.
All inputs are finite; a program needn't handle non-finite values.
Results may differ from a plain program's by a relative error of at most 0.015.
Values may be sent and summed in bfloat16 or wider, within the bound.
No kernel may reach another device: no remote copies, remote signals or barrier semaphores. Data moves between devices by JAX's collectives and lax.ppermute only.
A program may use at most 192 MiB of HBM per device.

v0:
```python
import math

import jax
import jax.numpy as jnp
from jax import lax
from jax.experimental import pallas as pl
from jax.experimental.pallas import tpu as pltpu
from jax.sharding import Mesh
from jax.sharding import PartitionSpec as P


DH = 128
HALF = 8
STEP_HEADS = 4
LIMIT = 50
FLOPS_4US = 2 << 30
FLOPS_6US = 3 << 30
SCALE = 1.0 / math.sqrt(DH)
LOG2E = math.log2(math.e)
BF = jnp.bfloat16
F32 = jnp.float32
CLASSES = ((1, 0), (0, 1), (1, 1))


def coords(i):
    return (i // 32, (i // 2) % 4, 2 * ((i // 8) % 2) + (i // 16) % 2, i % 2)


def device_at(x, y, z, core):
    x, y, z = x % 4, y % 4, z % 4
    return x * 32 + (z % 2) * 16 + (z // 2) * 8 + y * 2 + core


COSETS = [
    [
        device_at((kx + z) % 2 + 2 * i, (ky + z) % 2 + 2 * j, z, core)
        for z in range(4)
        for i in range(2)
        for j in range(2)
        for core in range(2)
    ]
    for kx in range(2)
    for ky in range(2)
]
CORE_SWAP = [(i, i ^ 1) for i in range(128)]


def shift(axis, by):
    pairs = []
    for i in range(128):
        place = list(coords(i))
        place[axis] += by
        pairs.append((i, device_at(*place)))
    return pairs


def exchange(pieces):
    return lax.all_to_all(pieces, "d", 0, 0, axis_index_groups=COSETS, tiled=True)


def grid_params():
    return pltpu.CompilerParams(
        dimension_semantics=("arbitrary",), vmem_limit_bytes=LIMIT * 1024 * 1024
    )


def whole_params(mib):
    return pltpu.CompilerParams(vmem_limit_bytes=mib * 1024 * 1024)


def forward_kernel(base, q_ref, k_ref, v_ref, ids_ref, att_ref, prob_ref, bias_ref):
    rows = q_ref.shape[0]

    @pl.when(pl.program_id(0) == 0)
    def _():
        t = lax.broadcasted_iota(jnp.int32, (rows, rows), 0)
        u = lax.broadcasted_iota(jnp.int32, (rows, rows), 1)
        ids = ids_ref[...].astype(F32)
        own = jnp.broadcast_to(ids, (DH, rows)).T[:, :1]
        bias_ref[...] = jnp.where(jnp.logical_and(u <= t, own == ids), 0.0, -1e30)

    block = 256

    def cut(h, i):
        return slice(h * DH, (h + 1) * DH), i * block, (i + 1) * block

    def scores_of(h, i):
        cols, lo, hi = cut(h, i)
        return lax.dot_general(
            q_ref[lo:hi, cols],
            k_ref[:hi, cols],
            (((1,), (1,)), ((), ())),
            preferred_element_type=F32,
        )

    def softmax_of(h, i, scores):
        _, lo, hi = cut(h, i)
        scores = scores * (SCALE * LOG2E) + bias_ref[lo:hi, :hi]
        raised = jnp.exp2(scores - jnp.max(scores, axis=1, keepdims=True))
        total = jnp.sum(raised, axis=1, keepdims=True)
        probs = (raised * (1.0 / total)).astype(BF)
        prob_ref[h, lo:hi, :hi] = probs
        return probs

    def attend(h, i, probs):
        cols, lo, hi = cut(h, i)
        att_ref[lo:hi, cols] = jnp.dot(
            probs, v_ref[:hi, cols], preferred_element_type=F32
        ).astype(BF)

    jobs = [(h, i) for h in range(STEP_HEADS) for i in range(rows // block)]
    ready = scores_of(*jobs[0])
    waiting = None
    for n, job in enumerate(jobs):
        scores = ready
        if n + 1 < len(jobs):
            ready = scores_of(*jobs[n + 1])
        probs = softmax_of(*job, scores)
        if waiting is not None:
            attend(*waiting)
        waiting = (*job, probs)
    attend(*waiting)


def attend_forward(base, queries, keys, values, ids):
    rows = queries.shape[0]
    head = pl.BlockSpec((rows, DH * STEP_HEADS), lambda i, b: (0, b[0] + i))
    return pl.pallas_call(
        forward_kernel,
        grid_spec=pltpu.PrefetchScalarGridSpec(
            num_scalar_prefetch=1,
            grid=(HALF // STEP_HEADS,),
            in_specs=[head, head, head, pl.BlockSpec((1, rows), lambda i, b: (0, 0))],
            out_specs=[
                pl.BlockSpec((rows, DH * STEP_HEADS), lambda i, b: (0, i)),
                pl.BlockSpec((STEP_HEADS, rows, rows), lambda i, b: (i, 0, 0)),
            ],
            scratch_shapes=[pltpu.VMEM((rows, rows), F32)],
        ),
        out_shape=[
            jax.ShapeDtypeStruct((rows, HALF * DH), BF),
            jax.ShapeDtypeStruct((HALF, rows, rows), BF),
        ],
        compiler_params=grid_params(),
        cost_estimate=pl.CostEstimate(
            flops=FLOPS_6US, bytes_accessed=9 << 20, transcendentals=1 << 20
        ),
        name="attend_forward",
    )(base, queries, keys, values, ids)


def backward_kernel(base, q_ref, k_ref, v_ref, g_ref, att_ref, prob_ref, *refs):
    dq_ref, dk_ref, dv_ref = refs[-3:]
    rows = q_ref.shape[0]
    block = 256
    count = rows // block
    inner, grad_t, query_t, sums = {}, {}, {}, {}

    def cut(h, i):
        return slice(h * DH, (h + 1) * DH), i * block, (i + 1) * block

    def prepare(h):
        cols = cut(h, 0)[0]
        grad = g_ref[:, cols]
        inner[h] = jnp.sum(
            grad.astype(F32) * att_ref[:, cols].astype(F32), axis=1, keepdims=True
        )
        grad_t[h] = grad.T
        query_t[h] = q_ref[:, cols].T
        sums[h] = []

    def grad_probs_of(h, i):
        cols, lo, hi = cut(h, i)
        return lax.dot_general(
            g_ref[lo:hi, cols],
            v_ref[:hi, cols],
            (((1,), (1,)), ((), ())),
            preferred_element_type=F32,
        )

    def grad_scores_of(h, i, grad_probs):
        _, lo, hi = cut(h, i)
        probs = prob_ref[h, lo:hi, :hi].astype(F32)
        return (probs * (grad_probs - inner[h][lo:hi, :])).astype(BF)

    def finish(h, i, grad_scores):
        cols, lo, hi = cut(h, i)
        probs = prob_ref[h, lo:hi, :hi]
        dq_ref[lo:hi, cols] = (
            SCALE * jnp.dot(grad_scores, k_ref[:hi, cols], preferred_element_type=F32)
        ).astype(BF)
        sums[h].append(
            (
                jnp.dot(grad_t[h][:, lo:hi], probs, preferred_element_type=F32),
                jnp.dot(query_t[h][:, lo:hi], grad_scores, preferred_element_type=F32),
            )
        )
        if i < count - 1:
            return
        for n, (out_ref, factor) in enumerate(((dv_ref, 1.0), (dk_ref, SCALE))):
            for j in range(count):
                _, lo, hi = cut(h, j)
                total = sums[h][j][n][:, lo:hi]
                for m in range(j + 1, count):
                    total = total + sums[h][m][n][:, lo:hi]
                out_ref[lo:hi, cols] = (total * factor).astype(BF).T

    jobs = [(h, i) for h in range(STEP_HEADS) for i in range(count)]
    prepare(0)
    ready = grad_probs_of(*jobs[0])
    waiting = None
    for n, job in enumerate(jobs):
        grad_probs = ready
        if n + 1 < len(jobs):
            if jobs[n + 1][1] == 0:
                prepare(jobs[n + 1][0])
            ready = grad_probs_of(*jobs[n + 1])
        grad_scores = grad_scores_of(*job, grad_probs)
        if waiting is not None:
            finish(*waiting)
        waiting = (*job, grad_scores)
    finish(*waiting)


def attend_backward(base, queries, keys, values, grad, attended, probs, previous):
    rows = queries.shape[0]
    head = pl.BlockSpec((rows, DH * STEP_HEADS), lambda i, b: (0, b[0] + i))
    half = pl.BlockSpec((rows, DH * STEP_HEADS), lambda i, b: (0, i))
    shape = jax.ShapeDtypeStruct(queries.shape, BF)
    return pl.pallas_call(
        backward_kernel,
        grid_spec=pltpu.PrefetchScalarGridSpec(
            num_scalar_prefetch=1,
            grid=(HALF // STEP_HEADS,),
            in_specs=[head, head, head, half, half]
            + [pl.BlockSpec((STEP_HEADS, rows, rows), lambda i, b: (i, 0, 0))]
            + [pl.BlockSpec(memory_space=pl.ANY)] * len(previous),
            out_specs=[head, head, head],
        ),
        out_shape=[shape, shape, shape],
        input_output_aliases={7 + n: n for n in range(len(previous))},
        compiler_params=grid_params(),
        cost_estimate=pl.CostEstimate(
            flops=FLOPS_4US, bytes_accessed=12 << 20, transcendentals=0
        ),
        name="attend_backward",
    )(base, queries, keys, values, grad, attended, probs, *previous)


def row_of(coset, other, block):
    core, j, i, z = block % 2, (block // 2) % 2, (block // 4) % 2, block // 8
    odd_x, odd_y = (z + other[0]) % 2, (z + other[1]) % 2
    x = (1 - coset[0] if odd_x else coset[0]) + 2 * i
    y = (1 - coset[1] if odd_y else coset[1]) + 2 * j
    return 16 * (x * 32 + (z % 2) * 16 + (z // 2) * 8 + y * 2 + core)


def coset_parts():
    yield (0, 0), 0, 32
    for other in CLASSES:
        yield other, 0, 16
        yield other, 16, 32


def project_kernel(coset, up_own_ref, up_other_ref, *refs):
    pieces, (own_ref, other_ref, weight_ref) = refs[:7], refs[7:]
    place = (coset[0], coset[1])
    for ref, (other, lo, hi) in zip(pieces, coset_parts()):
        for block in range(lo, hi):
            row = pl.multiple_of(row_of(place, other, block), 16)
            weight_ref[pl.ds(row, 16), :] = ref[16 * (block - lo) : 16 * (block - lo + 1), :]
    step = 512
    for up_ref, out_ref in ((up_other_ref, other_ref), (up_own_ref, own_ref)):
        for lo in range(0, out_ref.shape[1], step):
            out_ref[:, lo : lo + step] = jnp.dot(
                up_ref[...], weight_ref[:, lo : lo + step], preferred_element_type=F32
            ).astype(BF)


SMEM = pl.BlockSpec(memory_space=pltpu.SMEM)
VMEM = pl.BlockSpec(memory_space=pltpu.VMEM)


def project(coset, up_own, up_other, pieces):
    rows, width = up_own.shape
    cols = pieces[0].shape[1]
    return pl.pallas_call(
        project_kernel,
        in_specs=[SMEM] + [VMEM] * (2 + len(pieces)),
        out_specs=[VMEM] * 2,
        out_shape=[jax.ShapeDtypeStruct((rows, cols), BF)] * 2,
        scratch_shapes=[pltpu.VMEM((width, cols), BF)],
        compiler_params=whole_params(20),
        cost_estimate=pl.CostEstimate(
            flops=FLOPS_4US, bytes_accessed=10 << 20, transcendentals=0
        ),
        name="project",
    )(coset, up_own, up_other, *pieces)


def weight_kernel(coset, up_own_ref, up_other_ref, att_own_ref, att_other_ref, *refs):
    outs, sums_ref = refs[:7], refs[7]
    width = up_own_ref.shape[1]
    place = (coset[0], coset[1])
    step, cut = 256, 512

    def strip(lo):
        return jnp.concatenate(
            [up_own_ref[:, lo : lo + step].T, up_other_ref[:, lo : lo + step].T], axis=1
        )

    ready = strip(0)
    for lo in range(0, width, step):
        up_t = ready
        if lo + step < width:
            ready = strip(lo + step)
        for col in range(0, sums_ref.shape[1], cut):
            attended = jnp.concatenate(
                [att_own_ref[:, col : col + cut], att_other_ref[:, col : col + cut]], axis=0
            )
            sums_ref[lo : lo + step, col : col + cut] = jnp.dot(
                up_t, attended, preferred_element_type=F32
            ).astype(BF)
    for ref, (other, lo, hi) in zip(outs, coset_parts()):
        for block in range(lo, hi):
            row = pl.multiple_of(row_of(place, other, block), 16)
            ref[16 * (block - lo) : 16 * (block - lo + 1), :] = sums_ref[pl.ds(row, 16), :]


def weight_sums(coset, up_own, up_other, att_own, att_other):
    width = up_own.shape[1]
    cols = att_own.shape[1]
    sizes = [16 * (hi - lo) for _, lo, hi in coset_parts()]
    return pl.pallas_call(
        weight_kernel,
        in_specs=[SMEM] + [VMEM] * 4,
        out_specs=[VMEM] * len(sizes),
        out_shape=[jax.ShapeDtypeStruct((size, cols), BF) for size in sizes],
        scratch_shapes=[pltpu.VMEM((width, cols), BF)],
        compiler_params=whole_params(20),
        cost_estimate=pl.CostEstimate(
            flops=FLOPS_4US, bytes_accessed=10 << 20, transcendentals=0
        ),
        name="weight_sums",
    )(coset, up_own, up_other, att_own, att_other)


def spread_kernel(weight_ref, out_ref):
    cols = out_ref.shape[2]
    for n in range(out_ref.shape[0]):
        out_ref[n] = weight_ref[:, cols * (n % 2) : cols * (n % 2 + 1)]


def gather_weight(weight):
    rows, cols = weight.shape[0], weight.shape[1] // 2
    pieces = pl.pallas_call(
        spread_kernel,
        in_specs=[VMEM],
        out_specs=VMEM,
        out_shape=jax.ShapeDtypeStruct((32, rows, cols), BF),
        compiler_params=whole_params(8),
        name="spread",
    )(weight)
    return exchange(pieces).reshape(32 * rows, cols)


def gather_cosets(block):
    half = block.shape[0] // 2
    parts = (block[:half], block[half:])
    result = [block]
    for axis in range(3):
        for half in range(2):
            result.append(lax.ppermute(parts[half], "d", shift(axis, 2 * half - 1)))
    return result


def add_kernel(own_ref, *refs):
    received, out_ref = refs[:6], refs[6]
    rows = received[0].shape[0]
    for half in range(2):
        for lo in range(0, rows, 16):
            total = own_ref[rows * half + lo : rows * half + lo + 16, :].astype(F32)
            for axis in range(3):
                total = total + received[2 * axis + half][lo : lo + 16, :].astype(F32)
            out_ref[rows * half + lo : rows * half + lo + 16, :] = total.astype(BF)


def reduce_cosets(pieces):
    received = []
    for n, piece in enumerate(pieces[1:]):
        received.append(lax.ppermute(piece, "d", shift(n // 2, 1 - 2 * (n % 2))))
    return received


def add_received(own, received):
    return pl.pallas_call(
        add_kernel,
        in_specs=[VMEM] * 7,
        out_specs=VMEM,
        out_shape=jax.ShapeDtypeStruct(own.shape, BF),
        compiler_params=whole_params(8),
        cost_estimate=pl.CostEstimate(flops=1 << 28, bytes_accessed=5 << 20, transcendentals=0),
        name="add_received",
    )(own, *received)


def own_rows(rows_in, total_tokens):
    rows = rows_in.reshape(16, 2, *rows_in.shape[1:]).astype(F32)
    sums = jnp.sum(rows, axis=0) * (1.0 / math.sqrt(total_tokens))
    return jnp.concatenate([sums[0], sums[1]], axis=1)


def shards(queries, keys, values, upstream, weight, sample_ids):
    rows = queries.shape[0]
    me = lax.axis_index("d")
    core = jnp.bitwise_and(me, 1)
    z = jnp.bitwise_and(jnp.right_shift(me, 4), 1)
    kx = jnp.bitwise_and(jnp.right_shift(me, 5) + z, 1)
    ky = jnp.bitwise_and(jnp.right_shift(me, 1) + z, 1)
    coset = jnp.stack([kx, ky]).astype(jnp.int32)
    steps = HALF // STEP_HEADS
    base_own = (steps * core).astype(jnp.int32).reshape(1)
    base_other = (steps * (1 - core)).astype(jnp.int32).reshape(1)

    up_other = lax.ppermute(upstream, "d", CORE_SWAP)
    mine = gather_weight(weight)
    att_a, prob_a = attend_forward(base_other, queries, keys, values, sample_ids)
    att_other = lax.ppermute(att_a, "d", CORE_SWAP)
    att_b, prob_b = attend_forward(base_own, queries, keys, values, sample_ids)
    sums = weight_sums(coset, upstream, up_other, att_b, att_other)
    received = reduce_cosets(sums)
    mine, _ = lax.optimization_barrier((mine, sums[0]))
    gathered = gather_cosets(mine)
    reduced = add_received(sums[0], received)
    rows_in = exchange(reduced.reshape(32, -1, reduced.shape[1]))
    grad_own, grad_sent = project(coset, upstream, up_other, gathered)
    grad_other = lax.ppermute(grad_sent, "d", CORE_SWAP)
    outs = attend_backward(base_own, queries, keys, values, grad_own, att_b, prob_b, ())
    outs = attend_backward(
        base_other, queries, keys, values, grad_other, att_a, prob_a, tuple(outs)
    )
    grad_weight = own_rows(rows_in, rows * lax.axis_size("d"))
    return (*outs, grad_weight)


def solution(mesh):
    flat = Mesh(mesh.devices.reshape(-1), ("d",))
    return jax.shard_map(
        shards,
        mesh=flat,
        in_specs=(P("d", None),) * 6,
        out_specs=(P("d", None),) * 4,
        check_vma=False,
    )
```

profile of v0, /device:TPU:1, one launch (start us, length us, event | category | flops | bytes accessed | tf_op | source)
XLA Modules:
  0.0 128.7 jit_solution(18046117958534556910)
XLA Ops:
  0.6 1.5 %collective-permute-start = (bf16[512,2048]{1,0:T(8,128)(2,1)}, bf16[512,2048]{1,0:T(8,128)(2,1)}, u32[]{:S(2)}, u32[]{:S(2)}) collective-permute-start(bf16[512,2048]{1,0:T(8,128)(2,1)} %up_own_ref.3), channel_id=1, source_target_pairs={{0,1},{1,0},{2,3},{3,2},{4,5},{5,4},{6,7},{7,6},{8,9},{9,8},{10,11... | collective-permute-start | bytes 6291464 | tf_op jit(solution)/shard_map/ppermute | solution.py:425
  2.1 0.0 copy-start
  2.1 1.6 %copy-done = bf16[512,2048]{1,0:T(8,128)(2,1)S(1)} copy-done((bf16[512,2048]{1,0:T(8,128)(2,1)S(1)}, bf16[512,2048]{1,0:T(8,128)(2,1)}, u32[]{:S(2)}) %copy-start) | copy-done | bytes 2097176
  3.7 0.7 copy-done.12
  4.4 0.0 copy-start.7
  4.4 6.4 %attend_forward.3 = (bf16[512,1024]{1,0:T(8,128)(2,1)}, bf16[8,512,512]{2,1,0:T(8,128)(2,1)}) custom-call(s32[1]{0:T(128)} %bitcast.base, bf16[512,2048]{1,0:T(8,128)(2,1)S(1)} %copy-done, bf16[512,2048]{1,0:T(8,128)(2,1)} %k_ref.7, bf16[512,2048]{1,0:T(8,128)(2,1)} %v_ref.7, s32[1,512]{1,0:T(1,128)S(1)} %copy-done.12), custom_call_target="tpu_custom_call" | custom-call | flops 3221225472 | bytes 9437184 | tf_op jit(solution)/shard_map/attend_forward/pallas_call | solution.py:128
  10.8 0.0 copy-start.1
  10.8 0.1 collective-permute-start.1
  10.9 0.0 copy-done.7
  10.9 0.1 spread.1
  11.0 0.0 copy-start.2
  11.0 1.0 copy-done.2
  11.9 11.0 %all-to-all-start = ((bf16[32,16,1024]{2,1,0:T(8,128)(2,1)}), bf16[32,16,1024]{2,1,0:T(8,128)(2,1)S(1)}, u32[]{:S(2)}, u32[]{:S(2)}) async-start(bf16[32,16,1024]{2,1,0:T(8,128)(2,1)} %copy-done.2), calls=%async_computation | async-start | bytes 2097152 | tf_op jit(solution)/shard_map/all_to_all | solution.py:58
  22.9 0.1 pad_add_fusion.coset
  23.0 0.0 copy-done.1
  23.0 0.0 copy-done.13
  23.0 6.6 %attend_forward.2 = (bf16[512,1024]{1,0:T(8,128)(2,1)S(1)}, bf16[8,512,512]{2,1,0:T(8,128)(2,1)}) custom-call(s32[1]{0:T(128)} %bitcast.4.base, bf16[512,2048]{1,0:T(8,128)(2,1)S(1)} %copy-done.1, bf16[512,2048]{1,0:T(8,128)(2,1)} %k_ref.7, bf16[512,2048]{1,0:T(8,128)(2,1)} %v_ref.7, s32[1,512]{1,0:T(1,128)S(1)} %copy-done.13), custom_call_target="tpu_custom_call" | custom-call | flops 3221225472 | bytes 9437184 | tf_op jit(solution)/shard_map/attend_forward/pallas_call | solution.py:128
  29.6 0.0 collective-permute-done.1.att_other_ref
  29.6 0.0 collective-permute-done.up_other_ref
  29.6 0.0 copy-done.3
  29.6 8.0 %weight_sums.1 = (bf16[512,1024]{1,0:T(8,128)(2,1)S(1)}, bf16[256,1024]{1,0:T(8,128)(2,1)}, bf16[256,1024]{1,0:T(8,128)(2,1)}, bf16[256,1024]{1,0:T(8,128)(2,1)S...) custom-call(s32[2]{0:T(128)S(1)} %pad_add_fusion.coset, ...), custom_call_target="tpu_custom_call" | custom-call | flops 2147483648 | bytes 10485760 | tf_op jit(solution)/shard_map/weight_sums/pallas_call | solution.py:334
  37.6 0.0 copy-done.5
  37.6 0.8 copy-done.8
  38.4 0.8 copy-done.9
  39.3 0.8 copy-done.10
  40.0 0.8 copy-done.11
  40.8 0.3 collective-permute-start.9
  41.1 2.4 %collective-permute-start.10 = (bf16[256,1024]{1,0:T(8,128)(2,1)}, bf16[256,1024]{1,0:T(8,128)(2,1)S(1)}, u32[]{:S(2)}, u32[]{:S(2)}) collective-permute-start(bf16[256,1024]{1,0:T(8,128)(2,1)} %get-tuple-element.39), channel_id=1, source_target_pairs={{0,96},{1,97},{2,98},{3,99},{4,100},{5,101},{6,102},{7,103},{8,104... | collective-permute-start | bytes 1572872 | tf_op jit(solution)/shard_map/ppermute | solution.py:391
  43.5 0.0 all-to-all-done
  43.5 0.4 collective-permute-start.11
  43.9 2.3 %collective-permute-start.12 = (bf16[256,1024]{1,0:T(8,128)(2,1)}, bf16[256,1024]{1,0:T(8,128)(2,1)S(1)}, u32[]{:S(2)}, u32[]{:S(2)}) collective-permute-start(bf16[256,1024]{1,0:T(8,128)(2,1)} %copy-done.10), channel_id=1, source_target_pairs={{0,6},{1,7},{2,0},{3,1},{4,2},{5,3},{6,4},{7,5},{8,14},{9,15},{10,... | collective-permute-start | bytes 1572872 | tf_op jit(solution)/shard_map/ppermute | solution.py:391
  46.2 1.5 %collective-permute-start.13 = (bf16[256,1024]{1,0:T(8,128)(2,1)}, bf16[256,1024]{1,0:T(8,128)(2,1)S(1)}, u32[]{:S(2)}, u32[]{:S(2)}) collective-permute-start(bf16[256,1024]{1,0:T(8,128)(2,1)} %copy-done.9), channel_id=1, source_target_pairs={{0,16},{1,17},{2,18},{3,19},{4,20},{5,21},{6,22},{7,23},{8,24},{9,... | collective-permute-start | bytes 1572872 | tf_op jit(solution)/shard_map/ppermute | solution.py:391
  47.7 7.8 %collective-permute-done.9.refs_0_ = bf16[256,1024]{1,0:T(8,128)(2,1)S(1)} collective-permute-done((bf16[256,1024]{1,0:T(8,128)(2,1)}, bf16[256,1024]{1,0:T(8,128)(2,1)S(1)}, u32[]{:S(2)}, u32[]{:S(2)}) %collective-permute-start.9) | collective-permute-done | bytes 524320 | tf_op jit(solution)/shard_map/ppermute | solution.py:391
  55.5 2.6 %collective-permute-start.14 = (bf16[256,1024]{1,0:T(8,128)(2,1)}, bf16[256,1024]{1,0:T(8,128)(2,1)S(1)}, u32[]{:S(2)}, u32[]{:S(2)}) collective-permute-start(bf16[256,1024]{1,0:T(8,128)(2,1)} %copy-done.8), channel_id=1, source_target_pairs={{0,24},{1,25},{2,26},{3,27},{4,28},{5,29},{6,30},{7,31},{8,16},{9,... | collective-permute-start | bytes 1572872 | tf_op jit(solution)/shard_map/ppermute | solution.py:391
  58.1 1.0 fusion
  59.1 0.0 collective-permute-done.10.refs_1_
  59.1 0.0 collective-permute-start.7
  59.1 0.0 collective-permute-done.11.refs_2_
  59.1 0.0 collective-permute-done.12.refs_3_
  59.2 0.7 collective-permute-done.13.refs_4_
  59.9 8.5 %collective-permute-done.14.refs_5_ = bf16[256,1024]{1,0:T(8,128)(2,1)S(1)} collective-permute-done((bf16[256,1024]{1,0:T(8,128)(2,1)}, bf16[256,1024]{1,0:T(8,128)(2,1)S(1)}, u32[]{:S(2)}, u32[]{:S(2)}) %collective-permute-start.14) | collective-permute-done | bytes 524320 | tf_op jit(solution)/shard_map/ppermute | solution.py:391
  68.5 1.5 %add_received.1 = bf16[512,1024]{1,0:T(8,128)(2,1)} custom-call(bf16[512,1024]{1,0:T(8,128)(2,1)S(1)} %get-tuple-element.26.own_ref, bf16[256,1024]{1,0:T(8,128)(2,1)S(1)} %collective-permute-done.9.refs_0_, bf16[256,1024]{1,0:T(8,128)(2,1)S(1)} %collective-permute-done.10.refs_1_, bf16[256,1024]{1,0:T(8,128)(2,1)S(1)} %collective-permute-done.11.refs_2_, ...), custom_call_target="tpu_custom_call" | custom-call | flops 268435456 | bytes 5242880 | tf_op jit(solution)/shard_map/add_received/pallas_call | solution.py:396
  70.0 10.2 %all-to-all-start.1 = ((bf16[32,16,1024]{2,1,0:T(8,128)(2,1)}), bf16[32,16,1024]{2,1,0:T(8,128)(2,1)}, u32[]{:S(2)}, u32[]{:S(2)}) async-start(bf16[32,16,1024]{2,1,0:T(8,128)(2,1)} %bitcast.5), calls=%async_computation.1 | async-start | bytes 2097152 | tf_op jit(solution)/shard_map/all_to_all | solution.py:58
  80.2 0.1 collective-permute-start.5
  80.3 0.4 collective-permute-start.3
  80.6 4.6 %collective-permute-start.6 = (bf16[256,1024]{1,0:T(8,128)(2,1)}, bf16[256,1024]{1,0:T(8,128)(2,1)S(1)}, u32[]{:S(2)}, u32[]{:S(2)}) collective-permute-start(bf16[256,1024]{1,0:T(8,128)(2,1)} %get-tuple-element.45), channel_id=1, source_target_pairs={{0,24},{1,25},{2,26},{3,27},{4,28},{5,29},{6,30},{7,31},{8,16},{9,... | collective-permute-start | bytes 1572872 | tf_op jit(solution)/shard_map/ppermute | solution.py:373
  85.2 1.3 %collective-permute-start.4 = (bf16[256,1024]{1,0:T(8,128)(2,1)}, bf16[256,1024]{1,0:T(8,128)(2,1)S(1)}, u32[]{:S(2)}, u32[]{:S(2)}) collective-permute-start(bf16[256,1024]{1,0:T(8,128)(2,1)} %get-tuple-element.45), channel_id=1, source_target_pairs={{0,6},{1,7},{2,0},{3,1},{4,2},{5,3},{6,4},{7,5},{8,14},{9,15},{10,... | collective-permute-start | bytes 1572872 | tf_op jit(solution)/shard_map/ppermute | solution.py:373
  86.5 0.0 collective-permute-done.7.refs_6_
  86.5 1.5 %collective-permute-start.2 = (bf16[256,1024]{1,0:T(8,128)(2,1)}, bf16[256,1024]{1,0:T(8,128)(2,1)S(1)}, u32[]{:S(2)}, u32[]{:S(2)}) collective-permute-start(bf16[256,1024]{1,0:T(8,128)(2,1)} %get-tuple-element.45), channel_id=1, source_target_pairs={{0,96},{1,97},{2,98},{3,99},{4,100},{5,101},{6,102},{7,103},{8,104... | collective-permute-start | bytes 1572872 | tf_op jit(solution)/shard_map/ppermute | solution.py:373
  88.0 18.3 %collective-permute-done.5.refs_4_ = bf16[256,1024]{1,0:T(8,128)(2,1)S(1)} collective-permute-done((bf16[256,1024]{1,0:T(8,128)(2,1)}, bf16[256,1024]{1,0:T(8,128)(2,1)S(1)}, u32[]{:S(2)}, u32[]{:S(2)}) %collective-permute-start.5) | collective-permute-done | bytes 524320 | tf_op jit(solution)/shard_map/ppermute | solution.py:373
  106.3 0.0 collective-permute-done.3.refs_2_
  106.3 0.0 collective-permute-done.6.refs_5_
  106.3 0.0 collective-permute-done.4.refs_3_
  106.4 0.0 collective-permute-done.2.refs_1_
  106.4 0.0 copy-done.4
  106.4 6.5 %project.1 = (bf16[512,1024]{1,0:T(8,128)(2,1)S(1)}, bf16[512,1024]{1,0:T(8,128)(2,1)}) custom-call(s32[2]{0:T(128)S(1)} %pad_add_fusion.coset, bf16[512,2048]{1,0:T(8,128)(2,1)S(1)} %copy-done.4, bf16[512,2048]{1,0:T(8,128)(2,1)} %collective-permute-done.up_other_ref, bf16[512,1024]{1,0:T(8,128)(2,1)S(1)} %bitcast.13, ...), custom_call_target="tpu_custom_call" | custom-call | flops 2147483648 | bytes 10485760 | tf_op jit(solution)/shard_map/project/pallas_call | solution.py:287
  112.9 0.7 collective-permute-start.8
  113.6 0.0 copy-done.6
  113.6 6.4 %attend_backward.2 = (bf16[512,2048]{1,0:T(8,128)(2,1)}, bf16[512,2048]{1,0:T(8,128)(2,1)}, bf16[512,2048]{1,0:T(8,128)(2,1)}) custom-call(s32[1]{0:T(128)} %bitcast.4.base, bf16[512,2048]{1,0:T(8,128)(2,1)} %q_ref.7, bf16[512,2048]{1,0:T(8,128)(2,1)} %k_ref.7, bf16[512,2048]{1,0:T(8,128)(2,1)} %v_ref.7, bf16[512,1024]{1,0:T(8,128)(2,1)S(1)} %get-tuple-element.30.g_ref, ...), custom_call_target="tpu_custom_call" | custom-call | flops 2147483648 | bytes 12582912 | tf_op jit(solution)/shard_map/attend_backward/pallas_call | solution.py:230
  120.0 0.0 all-to-all-done.1
  120.0 1.4 %convert_reduce_fusion = f32[2,16,1024]{2,1,0:T(8,128)S(1)} fusion(bf16[16,2,16,1024]{3,2,1,0:T(8,128)(2,1)} %bitcast.9), kind=kLoop, calls=%fused_computation | loop fusion | flops 1015808 | bytes 1179648 | tf_op jit(solution)/shard_map/reduce_sum | solution.py:409
  121.5 0.7 pad_maximum_fusion
  122.1 0.0 collective-permute-done.8.g_ref
  122.2 6.6 %attend_backward.3 = (bf16[512,2048]{1,0:T(8,128)(2,1)}, bf16[512,2048]{1,0:T(8,128)(2,1)}, bf16[512,2048]{1,0:T(8,128)(2,1)}) custom-call(s32[1]{0:T(128)} %bitcast.base, bf16[512,2048]{1,0:T(8,128)(2,1)} %q_ref.7, bf16[512,2048]{1,0:T(8,128)(2,1)} %k_ref.7, bf16[512,2048]{1,0:T(8,128)(2,1)} %v_ref.7, ...), custom_call_target="tpu_custom_call", output_to_operand_aliasing={{0}: (7, {}), {1}: (8, {}), {2}: (9, {})} | custom-call | flops 2147483648 | bytes 12582912 | tf_op jit(solution)/shard_map/attend_backward/pallas_call | solution.py:230
  (12 shorter events, 0.0 us)
Async XLA Ops:
  0.6 29.0 %collective-permute-start = (bf16[512,2048]{1,0:T(8,128)(2,1)}, bf16[512,2048]{1,0:T(8,128)(2,1)}, u32[]{:S(2)}, u32[]{:S(2)}) collective-permute-start(bf16[512,2048]{1,0:T(8,128)(2,1)} %up_own_ref.3), channel_id=1, source_target_pairs={{0,1},{1,0},{2,3},{3,2},{4,5},{5,4},{6,7},{7,6},{8,9},{9,8},{10,11... | collective-permute-start | bytes 6291464 | tf_op jit(solution)/shard_map/ppermute | solution.py:425
  2.1 1.6 %copy-start = (bf16[512,2048]{1,0:T(8,128)(2,1)S(1)}, bf16[512,2048]{1,0:T(8,128)(2,1)}, u32[]{:S(2)}) copy-start(bf16[512,2048]{1,0:T(8,128)(2,1)} %q_ref.7) | copy-start | bytes 6291460
  3.7 0.7 copy-start.12
  4.4 6.5 %copy-start.7 = (bf16[16,2048]{1,0:T(8,128)(2,1)S(1)}, bf16[16,2048]{1,0:T(8,128)(2,1)}, u32[]{:S(2)}) copy-start(bf16[16,2048]{1,0:T(8,128)(2,1)} %weight_ref.1) | copy-start | bytes 196612
  10.8 12.2 %copy-start.1 = (bf16[512,2048]{1,0:T(8,128)(2,1)S(1)}, bf16[512,2048]{1,0:T(8,128)(2,1)}, u32[]{:S(2)}) copy-start(bf16[512,2048]{1,0:T(8,128)(2,1)} %q_ref.7) | copy-start | bytes 6291460
  10.8 12.2 %copy-start.13 = (s32[1,512]{1,0:T(1,128)S(1)}, s32[1,512]{1,0:T(1,128)}, u32[]{:S(2)}) copy-start(s32[1,512]{1,0:T(1,128)} %ids_ref.3) | copy-start | bytes 6148
  10.8 18.8 %collective-permute-start.1 = (bf16[512,1024]{1,0:T(8,128)(2,1)}, bf16[512,1024]{1,0:T(8,128)(2,1)}, u32[]{:S(2)}, u32[]{:S(2)}) collective-permute-start(bf16[512,1024]{1,0:T(8,128)(2,1)} %get-tuple-element.25.att_ref), channel_id=1, source_target_pairs={{0,1},{1,0},{2,3},{3,2},{4,5},{5,4},{6,7},{7,6},{8,9},{9,8},{10,11... | collective-permute-start | bytes 3145736 | tf_op jit(solution)/shard_map/ppermute | solution.py:428
  11.0 1.0 copy-start.2
  11.9 31.6 %all-to-all-start = ((bf16[32,16,1024]{2,1,0:T(8,128)(2,1)}), bf16[32,16,1024]{2,1,0:T(8,128)(2,1)S(1)}, u32[]{:S(2)}, u32[]{:S(2)}) async-start(bf16[32,16,1024]{2,1,0:T(8,128)(2,1)} %copy-done.2), calls=%async_computation | async-start | bytes 2097152 | tf_op jit(solution)/shard_map/all_to_all | solution.py:58
  23.0 6.6 %copy-start.3 = (bf16[512,2048]{1,0:T(8,128)(2,1)S(1)}, bf16[512,2048]{1,0:T(8,128)(2,1)}, u32[]{:S(2)}) copy-start(bf16[512,2048]{1,0:T(8,128)(2,1)} %up_own_ref.3) | copy-start | bytes 6291460
  29.6 8.0 %copy-start.5 = (bf16[512,1024]{1,0:T(8,128)(2,1)}, bf16[512,1024]{1,0:T(8,128)(2,1)S(1)}, u32[]{:S(2)}) copy-start(bf16[512,1024]{1,0:T(8,128)(2,1)S(1)} %get-tuple-element.24.att_own_ref.att_ref) | copy-start | bytes 3145732
  37.6 0.8 copy-start.8
  38.4 0.8 copy-start.9
  39.3 0.8 copy-start.10
  40.0 0.8 copy-start.11
  40.8 14.7 %collective-permute-start.9 = (bf16[256,1024]{1,0:T(8,128)(2,1)}, bf16[256,1024]{1,0:T(8,128)(2,1)S(1)}, u32[]{:S(2)}, u32[]{:S(2)}) collective-permute-start(bf16[256,1024]{1,0:T(8,128)(2,1)} %get-tuple-element.38), channel_id=1, source_target_pairs={{0,32},{1,33},{2,34},{3,35},{4,36},{5,37},{6,38},{7,39},{8,40},{9,... | collective-permute-start | bytes 1572872 | tf_op jit(solution)/shard_map/ppermute | solution.py:391
  41.1 18.0 %collective-permute-start.10 = (bf16[256,1024]{1,0:T(8,128)(2,1)}, bf16[256,1024]{1,0:T(8,128)(2,1)S(1)}, u32[]{:S(2)}, u32[]{:S(2)}) collective-permute-start(bf16[256,1024]{1,0:T(8,128)(2,1)} %get-tuple-element.39), channel_id=1, source_target_pairs={{0,96},{1,97},{2,98},{3,99},{4,100},{5,101},{6,102},{7,103},{8,104... | collective-permute-start | bytes 1572872 | tf_op jit(solution)/shard_map/ppermute | solution.py:391
  43.5 15.6 %collective-permute-start.11 = (bf16[256,1024]{1,0:T(8,128)(2,1)}, bf16[256,1024]{1,0:T(8,128)(2,1)S(1)}, u32[]{:S(2)}, u32[]{:S(2)}) collective-permute-start(bf16[256,1024]{1,0:T(8,128)(2,1)} %copy-done.11), channel_id=1, source_target_pairs={{0,2},{1,3},{2,4},{3,5},{4,6},{5,7},{6,0},{7,1},{8,10},{9,11},{10,... | collective-permute-start | bytes 1572872 | tf_op jit(solution)/shard_map/ppermute | solution.py:391
  43.9 15.2 %collective-permute-start.12 = (bf16[256,1024]{1,0:T(8,128)(2,1)}, bf16[256,1024]{1,0:T(8,128)(2,1)S(1)}, u32[]{:S(2)}, u32[]{:S(2)}) collective-permute-start(bf16[256,1024]{1,0:T(8,128)(2,1)} %copy-done.10), channel_id=1, source_target_pairs={{0,6},{1,7},{2,0},{3,1},{4,2},{5,3},{6,4},{7,5},{8,14},{9,15},{10,... | collective-permute-start | bytes 1572872 | tf_op jit(solution)/shard_map/ppermute | solution.py:391
  46.2 13.7 %collective-permute-start.13 = (bf16[256,1024]{1,0:T(8,128)(2,1)}, bf16[256,1024]{1,0:T(8,128)(2,1)S(1)}, u32[]{:S(2)}, u32[]{:S(2)}) collective-permute-start(bf16[256,1024]{1,0:T(8,128)(2,1)} %copy-done.9), channel_id=1, source_target_pairs={{0,16},{1,17},{2,18},{3,19},{4,20},{5,21},{6,22},{7,23},{8,24},{9,... | collective-permute-start | bytes 1572872 | tf_op jit(solution)/shard_map/ppermute | solution.py:391
  55.5 13.0 %collective-permute-start.14 = (bf16[256,1024]{1,0:T(8,128)(2,1)}, bf16[256,1024]{1,0:T(8,128)(2,1)S(1)}, u32[]{:S(2)}, u32[]{:S(2)}) collective-permute-start(bf16[256,1024]{1,0:T(8,128)(2,1)} %copy-done.8), channel_id=1, source_target_pairs={{0,24},{1,25},{2,26},{3,27},{4,28},{5,29},{6,30},{7,31},{8,16},{9,... | collective-permute-start | bytes 1572872 | tf_op jit(solution)/shard_map/ppermute | solution.py:391
  59.1 27.4 %collective-permute-start.7 = (bf16[256,1024]{1,0:T(8,128)(2,1)}, bf16[256,1024]{1,0:T(8,128)(2,1)}, u32[]{:S(2)}, u32[]{:S(2)}) collective-permute-start(bf16[256,1024]{1,0:T(8,128)(2,1)} %get-tuple-element.44), channel_id=1, source_target_pairs={{0,16},{1,17},{2,18},{3,19},{4,20},{5,21},{6,22},{7,23},{8,24},{9,... | collective-permute-start | bytes 1572872 | tf_op jit(solution)/shard_map/ppermute | solution.py:373
  70.0 36.4 %copy-start.4 = (bf16[512,2048]{1,0:T(8,128)(2,1)S(1)}, bf16[512,2048]{1,0:T(8,128)(2,1)}, u32[]{:S(2)}) copy-start(bf16[512,2048]{1,0:T(8,128)(2,1)} %up_own_ref.3) | copy-start | bytes 6291460
  70.0 50.1 %all-to-all-start.1 = ((bf16[32,16,1024]{2,1,0:T(8,128)(2,1)}), bf16[32,16,1024]{2,1,0:T(8,128)(2,1)}, u32[]{:S(2)}, u32[]{:S(2)}) async-start(bf16[32,16,1024]{2,1,0:T(8,128)(2,1)} %bitcast.5), calls=%async_computation.1 | async-start | bytes 2097152 | tf_op jit(solution)/shard_map/all_to_all | solution.py:58
  80.2 26.2 %collective-permute-start.5 = (bf16[256,1024]{1,0:T(8,128)(2,1)}, bf16[256,1024]{1,0:T(8,128)(2,1)S(1)}, u32[]{:S(2)}, u32[]{:S(2)}) collective-permute-start(bf16[256,1024]{1,0:T(8,128)(2,1)} %get-tuple-element.44), channel_id=1, source_target_pairs={{0,2},{1,3},{2,4},{3,5},{4,6},{5,7},{6,0},{7,1},{8,10},{9,11},{10,... | collective-permute-start | bytes 1572872 | tf_op jit(solution)/shard_map/ppermute | solution.py:373
  80.3 26.1 %collective-permute-start.3 = (bf16[256,1024]{1,0:T(8,128)(2,1)}, bf16[256,1024]{1,0:T(8,128)(2,1)S(1)}, u32[]{:S(2)}, u32[]{:S(2)}) collective-permute-start(bf16[256,1024]{1,0:T(8,128)(2,1)} %get-tuple-element.44), channel_id=1, source_target_pairs={{0,32},{1,33},{2,34},{3,35},{4,36},{5,37},{6,38},{7,39},{8,40},{9,... | collective-permute-start | bytes 1572872 | tf_op jit(solution)/shard_map/ppermute | solution.py:373
  80.6 33.0 %copy-start.6 = (bf16[512,1024]{1,0:T(8,128)(2,1)S(1)}, bf16[512,1024]{1,0:T(8,128)(2,1)}, u32[]{:S(2)}) copy-start(bf16[512,1024]{1,0:T(8,128)(2,1)} %copy-done.5) | copy-start | bytes 3145732
  80.6 25.7 %collective-permute-start.6 = (bf16[256,1024]{1,0:T(8,128)(2,1)}, bf16[256,1024]{1,0:T(8,128)(2,1)S(1)}, u32[]{:S(2)}, u32[]{:S(2)}) collective-permute-start(bf16[256,1024]{1,0:T(8,128)(2,1)} %get-tuple-element.45), channel_id=1, source_target_pairs={{0,24},{1,25},{2,26},{3,27},{4,28},{5,29},{6,30},{7,31},{8,16},{9,... | collective-permute-start | bytes 1572872 | tf_op jit(solution)/shard_map/ppermute | solution.py:373
  85.2 21.1 %collective-permute-start.4 = (bf16[256,1024]{1,0:T(8,128)(2,1)}, bf16[256,1024]{1,0:T(8,128)(2,1)S(1)}, u32[]{:S(2)}, u32[]{:S(2)}) collective-permute-start(bf16[256,1024]{1,0:T(8,128)(2,1)} %get-tuple-element.45), channel_id=1, source_target_pairs={{0,6},{1,7},{2,0},{3,1},{4,2},{5,3},{6,4},{7,5},{8,14},{9,15},{10,... | collective-permute-start | bytes 1572872 | tf_op jit(solution)/shard_map/ppermute | solution.py:373
  86.5 19.8 %collective-permute-start.2 = (bf16[256,1024]{1,0:T(8,128)(2,1)}, bf16[256,1024]{1,0:T(8,128)(2,1)S(1)}, u32[]{:S(2)}, u32[]{:S(2)}) collective-permute-start(bf16[256,1024]{1,0:T(8,128)(2,1)} %get-tuple-element.45), channel_id=1, source_target_pairs={{0,96},{1,97},{2,98},{3,99},{4,100},{5,101},{6,102},{7,103},{8,104... | collective-permute-start | bytes 1572872 | tf_op jit(solution)/shard_map/ppermute | solution.py:373
  112.9 9.3 %collective-permute-start.8 = (bf16[512,1024]{1,0:T(8,128)(2,1)}, bf16[512,1024]{1,0:T(8,128)(2,1)S(1)}, u32[]{:S(2)}, u32[]{:S(2)}) collective-permute-start(bf16[512,1024]{1,0:T(8,128)(2,1)} %get-tuple-element.28), channel_id=1, source_target_pairs={{0,1},{1,0},{2,3},{3,2},{4,5},{5,4},{6,7},{7,6},{8,9},{9,8},{10,11... | collective-permute-start | bytes 3145736 | tf_op jit(solution)/shard_map/ppermute | solution.py:437
where the time goes:
time: 129 us
  Pallas kernels  42 us (33%)
  starting transfers between devices  40.8 us (32%)
  waiting for transfers between devices  35.4 us (27%)
  local copies, waits for them, and re-layouts  7.5 us (6%)
  other arithmetic  2.18 us (2%)
    all_to_all x2, starting transfers between devices, exchange(): lax.all_to_all(pieces, 'd', 0, 0, axis_index_groups=COSETS, tiled=True)  21.2 us
    ppermute x6, waiting for transfers between devices, gather_cosets(): result.append(lax.ppermute(parts[half], 'd', shift(axis, 2 * half - 1)))  18.3 us
    ppermute x6, waiting for transfers between devices, reduce_cosets(): received.append(lax.ppermute(piece, 'd', shift(n // 2, 1 - 2 * (n % 2))))  17.1 us
    pallas_call x2, Pallas kernels, attend_forward(): pl.pallas_call(forward_kernel, grid_spec=pltpu.PrefetchScalarGridSpec(num...  13 us
    pallas_call x2, Pallas kernels, attend_backward(): pl.pallas_call(backward_kernel, grid_spec=pltpu.PrefetchScalarGridSpec(nu...  13 us
    ppermute x6, starting transfers between devices, reduce_cosets(): received.append(lax.ppermute(piece, 'd', shift(n // 2, 1 - 2 * (n % 2))))  9.47 us
    pallas_call x1, Pallas kernels, weight_sums(): pl.pallas_call(weight_kernel, in_specs=[SMEM] + [VMEM] * 4, out_specs=[VM...  7.98 us
    ppermute x6, starting transfers between devices, gather_cosets(): result.append(lax.ppermute(parts[half], 'd', shift(axis, 2 * half - 1)))  7.85 us
  transfers between devices with their start and end apart: 17, of which 4 were waited for; matrix products, arithmetic and copies ran while one was open for 3% of the time, Pallas kernels for 28%

commit v1 on v0

v1 whole, which is shorter than its diff:
```python
import math

import jax
import jax.numpy as jnp
from jax import lax
from jax.experimental import pallas as pl
from jax.experimental.pallas import tpu as pltpu
from jax.sharding import Mesh
from jax.sharding import PartitionSpec as P


DH = 128
HALF = 8
LIMIT = 58
LIMIT_PROJECT = 50
FLOPS_4US = 2 << 30
FLOPS_6US = 3 << 30
SCALE = 1.0 / math.sqrt(DH)
LOG2E = math.log2(math.e)
BF = jnp.bfloat16
F32 = jnp.float32
CLASSES = ((1, 0), (0, 1), (1, 1))


def coords(i):
    return (i // 32, (i // 2) % 4, 2 * ((i // 8) % 2) + (i // 16) % 2, i % 2)


def device_at(x, y, z, core):
    x, y, z = x % 4, y % 4, z % 4
    return x * 32 + (z % 2) * 16 + (z // 2) * 8 + y * 2 + core


COSETS = [
    [
        device_at((kx + z) % 2 + 2 * i, (ky + z) % 2 + 2 * j, z, core)
        for z in range(4)
        for i in range(2)
        for j in range(2)
        for core in range(2)
    ]
    for kx in range(2)
    for ky in range(2)
]
CORE_SWAP = [(i, i ^ 1) for i in range(128)]


def shift(axis, by):
    pairs = []
    for i in range(128):
        place = list(coords(i))
        place[axis] += by
        pairs.append((i, device_at(*place)))
    return pairs


def exchange(pieces):
    return lax.all_to_all(pieces, "d", 0, 0, axis_index_groups=COSETS, tiled=True)


SMEM = pl.BlockSpec(memory_space=pltpu.SMEM)
VMEM = pl.BlockSpec(memory_space=pltpu.VMEM)
HBM = pl.BlockSpec(memory_space=pltpu.HBM)


def whole_params(mib):
    return pltpu.CompilerParams(vmem_limit_bytes=mib * 1024 * 1024)


BLOCK = 256
PACKED = 3 * BLOCK
CHUNK = 2


def places(h, i):
    cols = slice(h * DH, (h + 1) * DH)
    packed = slice(0, BLOCK) if i == 0 else slice(BLOCK, PACKED)
    return cols, i * BLOCK, (i + 1) * BLOCK, packed


def chunk_copy(source, base, buffer, sem, n, chunk):
    wide = CHUNK * DH
    start = pl.multiple_of(base * (HALF * DH) + chunk * wide, DH)
    return pltpu.make_async_copy(
        source.at[:, pl.ds(start, wide)],
        buffer.at[:, chunk * wide : (chunk + 1) * wide],
        sem.at[n, chunk],
    )


def forward_kernel(base_ref, ids_ref, q_hbm, k_hbm, v_hbm, att_hbm, prob_hbm, *scratch):
    q_ref, k_ref, v_ref, att_ref, prob_ref, bias_ref, in_sem, prob_sem, att_sem = scratch
    rows = q_ref.shape[0]
    base = base_ref[0]
    loads = [
        [
            chunk_copy(source, base, buffer, in_sem, n, chunk)
            for n, (source, buffer) in enumerate(((q_hbm, q_ref), (k_hbm, k_ref), (v_hbm, v_ref)))
        ]
        for chunk in range(HALF // CHUNK)
    ]
    for group in loads:
        for copy in group:
            copy.start()

    t = lax.broadcasted_iota(jnp.int32, (rows, rows), 0)
    u = lax.broadcasted_iota(jnp.int32, (rows, rows), 1)
    ids = ids_ref[...].astype(F32)
    own = jnp.broadcast_to(ids, (DH, rows)).T[:, :1]
    bias_ref[...] = jnp.where(jnp.logical_and(u <= t, own == ids), 0.0, -1e30)

    def scores_of(h, i):
        cols, lo, hi, _ = places(h, i)
        if i == 0 and h % CHUNK == 0:
            for copy in loads[h // CHUNK]:
                copy.wait()
        return lax.dot_general(
            q_ref[lo:hi, cols],
            k_ref[:hi, cols],
            (((1,), (1,)), ((), ())),
            preferred_element_type=F32,
        )

    stores = [
        pltpu.make_async_copy(prob_ref.at[h], prob_hbm.at[h], prob_sem.at[h]) for h in range(HALF)
    ]

    def softmax_of(h, i, scores):
        _, lo, hi, packed = places(h, i)
        scores = scores * (SCALE * LOG2E) + bias_ref[lo:hi, :hi]
        raised = jnp.exp2(scores - jnp.max(scores, axis=1, keepdims=True))
        total = jnp.sum(raised, axis=1, keepdims=True)
        probs = (raised * (1.0 / total)).astype(BF)
        prob_ref[h, :, packed] = probs
        return probs

    def attend(h, i, probs):
        cols, lo, hi, _ = places(h, i)
        att_ref[lo:hi, cols] = jnp.dot(
            probs, v_ref[:hi, cols], preferred_element_type=F32
        ).astype(BF)

    jobs = [(h, i) for h in range(HALF) for i in range(rows // BLOCK)]
    ready = scores_of(*jobs[0])
    waiting = None
    for n, job in enumerate(jobs):
        scores = ready
        if n + 1 < len(jobs):
            ready = scores_of(*jobs[n + 1])
        probs = softmax_of(*job, scores)
        if waiting is not None:
            attend(*waiting)
        waiting = (*job, probs)
        if job[1] == 1:
            stores[job[0]].start()
    attend(*waiting)
    keep = pltpu.make_async_copy(att_ref, att_hbm, att_sem)
    keep.start()
    for copy in stores:
        copy.wait()
    keep.wait()


def attend_forward(base, queries, keys, values, ids):
    rows = queries.shape[0]
    cols = HALF * DH
    return pl.pallas_call(
        forward_kernel,
        in_specs=[SMEM, VMEM, HBM, HBM, HBM],
        out_specs=[HBM, HBM],
        out_shape=[
            jax.ShapeDtypeStruct((rows, cols), BF),
            jax.ShapeDtypeStruct((HALF, BLOCK, PACKED), BF),
        ],
        scratch_shapes=[pltpu.VMEM((rows, cols), BF)] * 4
        + [
            pltpu.VMEM((HALF, BLOCK, PACKED), BF),
            pltpu.VMEM((rows, rows), F32),
            pltpu.SemaphoreType.DMA((3, HALF // CHUNK)),
            pltpu.SemaphoreType.DMA((HALF,)),
            pltpu.SemaphoreType.DMA,
        ],
        compiler_params=whole_params(LIMIT),
        cost_estimate=pl.CostEstimate(
            flops=FLOPS_6US, bytes_accessed=9 << 20, transcendentals=1 << 20
        ),
        name="attend_forward",
    )(base, ids, queries, keys, values)


def backward_kernel(base_ref, g_ref, q_hbm, k_hbm, v_hbm, att_hbm, prob_hbm, *refs):
    dq_hbm, dk_hbm, dv_hbm = refs[-13:-10]
    q_ref, k_ref, v_ref, att_ref, prob_ref, dq_ref, dk_ref, dv_ref = refs[-10:-2]
    in_sem, out_sem = refs[-2:]
    rows = q_ref.shape[0]
    base = base_ref[0]
    count = rows // BLOCK
    loads = []
    for chunk in range(HALF // CHUNK):
        group = [
            chunk_copy(source, base, buffer, in_sem, n, chunk)
            for n, (source, buffer) in enumerate(((q_hbm, q_ref), (k_hbm, k_ref), (v_hbm, v_ref)))
        ]
        group.append(chunk_copy(att_hbm, 0, att_ref, in_sem, 3, chunk))
        heads = slice(chunk * CHUNK, (chunk + 1) * CHUNK)
        group.append(
            pltpu.make_async_copy(prob_hbm.at[heads], prob_ref.at[heads], in_sem.at[4, chunk])
        )
        loads.append(group)
    for group in loads:
        for copy in group:
            copy.start()
    wide = CHUNK * DH
    stores = [
        [
            pltpu.make_async_copy(
                buffer.at[:, chunk * wide : (chunk + 1) * wide],
                target.at[
                    :, pl.ds(pl.multiple_of(base * (HALF * DH) + chunk * wide, DH), wide)
                ],
                out_sem.at[n, chunk],
            )
            for n, (buffer, target) in enumerate(
                ((dq_ref, dq_hbm), (dk_ref, dk_hbm), (dv_ref, dv_hbm))
            )
        ]
        for chunk in range(HALF // CHUNK)
    ]
    inner, grad_t, query_t, sums = {}, {}, {}, {}

    def prepare(h):
        cols = places(h, 0)[0]
        if h % CHUNK == 0:
            for copy in loads[h // CHUNK]:
                copy.wait()
        grad = g_ref[:, cols]
        inner[h] = jnp.sum(
            grad.astype(F32) * att_ref[:, cols].astype(F32), axis=1, keepdims=True
        )
        grad_t[h] = grad.T
        query_t[h] = q_ref[:, cols].T
        sums[h] = []

    def grad_probs_of(h, i):
        cols, lo, hi, _ = places(h, i)
        return lax.dot_general(
            g_ref[lo:hi, cols],
            v_ref[:hi, cols],
            (((1,), (1,)), ((), ())),
            preferred_element_type=F32,
        )

    def grad_scores_of(h, i, grad_probs):
        _, lo, hi, packed = places(h, i)
        probs = prob_ref[h, :, packed].astype(F32)
        return (probs * (grad_probs - inner[h][lo:hi, :])).astype(BF)

    def finish(h, i, grad_scores):
        cols, lo, hi, packed = places(h, i)
        probs = prob_ref[h, :, packed]
        dq_ref[lo:hi, cols] = (
            SCALE * jnp.dot(grad_scores, k_ref[:hi, cols], preferred_element_type=F32)
        ).astype(BF)
        sums[h].append(
            (
                jnp.dot(grad_t[h][:, lo:hi], probs, preferred_element_type=F32),
                jnp.dot(query_t[h][:, lo:hi], grad_scores, preferred_element_type=F32),
            )
        )
        if i < count - 1:
            return
        for n, (out_ref, factor) in enumerate(((dv_ref, 1.0), (dk_ref, SCALE))):
            for j in range(count):
                _, lo, hi, _ = places(h, j)
                total = sums[h][j][n][:, lo:hi]
                for m in range(j + 1, count):
                    total = total + sums[h][m][n][:, lo:hi]
                out_ref[lo:hi, cols] = (total * factor).astype(BF).T
        if h % CHUNK == CHUNK - 1:
            for copy in stores[h // CHUNK]:
                copy.start()

    jobs = [(h, i) for h in range(HALF) for i in range(count)]
    prepare(0)
    ready = grad_probs_of(*jobs[0])
    waiting = None
    for n, job in enumerate(jobs):
        grad_probs = ready
        if n + 1 < len(jobs):
            if jobs[n + 1][1] == 0:
                prepare(jobs[n + 1][0])
            ready = grad_probs_of(*jobs[n + 1])
        grad_scores = grad_scores_of(*job, grad_probs)
        if waiting is not None:
            finish(*waiting)
        waiting = (*job, grad_scores)
    finish(*waiting)
    for group in stores:
        for copy in group:
            copy.wait()


def attend_backward(base, queries, keys, values, grad, attended, probs, previous):
    rows = queries.shape[0]
    cols = HALF * DH
    shape = jax.ShapeDtypeStruct(queries.shape, BF)
    chunks = HALF // CHUNK
    half = pltpu.VMEM((rows, cols), BF)
    return pl.pallas_call(
        backward_kernel,
        in_specs=[SMEM, VMEM] + [HBM] * (5 + len(previous)),
        out_specs=[HBM] * 3,
        out_shape=[shape, shape, shape],
        scratch_shapes=[half] * 4
        + [pltpu.VMEM((HALF, BLOCK, PACKED), BF)]
        + [half] * 3
        + [pltpu.SemaphoreType.DMA((5, chunks)), pltpu.SemaphoreType.DMA((3, chunks))],
        input_output_aliases={7 + n: n for n in range(len(previous))},
        compiler_params=whole_params(LIMIT),
        cost_estimate=pl.CostEstimate(
            flops=FLOPS_4US, bytes_accessed=12 << 20, transcendentals=0
        ),
        name="attend_backward",
    )(base, grad, queries, keys, values, attended, probs, *previous)


def row_of(coset, other, block):
    core, j, i, z = block % 2, (block // 2) % 2, (block // 4) % 2, block // 8
    odd_x, odd_y = (z + other[0]) % 2, (z + other[1]) % 2
    x = (1 - coset[0] if odd_x else coset[0]) + 2 * i
    y = (1 - coset[1] if odd_y else coset[1]) + 2 * j
    return 16 * (x * 32 + (z % 2) * 16 + (z // 2) * 8 + y * 2 + core)


def coset_parts():
    yield (0, 0), 0, 32
    for other in CLASSES:
        yield other, 0, 16
        yield other, 16, 32


def project_kernel(coset, up_own_hbm, up_other_hbm, *refs):
    pieces, (own_hbm, other_hbm) = refs[:7], refs[7:9]
    weight_ref, up_ref, out_ref, up_sem, out_sem = refs[9:]
    cols = weight_ref.shape[1]
    place = (coset[0], coset[1])
    ups = []
    for n, source in enumerate((up_other_hbm, up_own_hbm)):
        ups.append(pltpu.make_async_copy(source, up_ref.at[n], up_sem.at[n]))
        ups[n].start()
    for piece, (other, lo, hi) in zip(pieces, coset_parts()):
        for block in range(lo, hi):
            row = pl.multiple_of(row_of(place, other, block), 16)
            weight_ref[pl.ds(row, 16), :] = piece[16 * (block - lo) : 16 * (block - lo + 1), :]
    step = 512
    stores = []
    for n, target in enumerate((other_hbm, own_hbm)):
        ups[n].wait()
        for lo in range(0, cols, step):
            out_ref[n, :, lo : lo + step] = jnp.dot(
                up_ref[n], weight_ref[:, lo : lo + step], preferred_element_type=F32
            ).astype(BF)
        stores.append(pltpu.make_async_copy(out_ref.at[n], target, out_sem.at[n]))
        stores[n].start()
    for copy in stores:
        copy.wait()


def project(coset, up_own, up_other, pieces):
    rows, width = up_own.shape
    cols = pieces[0].shape[1]
    return pl.pallas_call(
        project_kernel,
        in_specs=[SMEM, HBM, HBM] + [VMEM] * len(pieces),
        out_specs=[HBM] * 2,
        out_shape=[jax.ShapeDtypeStruct((rows, cols), BF)] * 2,
        scratch_shapes=[
            pltpu.VMEM((width, cols), BF),
            pltpu.VMEM((2, rows, width), BF),
            pltpu.VMEM((2, rows, cols), BF),
            pltpu.SemaphoreType.DMA((2,)),
            pltpu.SemaphoreType.DMA((2,)),
        ],
        compiler_params=whole_params(LIMIT_PROJECT),
        cost_estimate=pl.CostEstimate(
            flops=FLOPS_4US, bytes_accessed=10 << 20, transcendentals=0
        ),
        name="project",
    )(coset, up_own, up_other, *pieces)


def weight_kernel(coset, up_other_ref, up_own_hbm, att_own_hbm, att_other_hbm, *refs):
    outs, stages = refs[:7], refs[7:14]
    up_ref, att_ref, up_t_ref, first_ref, second_ref, up_sem, att_sem, out_sem = refs[14:]
    rows, width = up_own_hbm.shape
    place = (coset[0], coset[1])
    step, cut = 256, 512
    att_loads, up_loads = [], []
    for col in range(2):
        att_loads.append(
            [
                pltpu.make_async_copy(
                    source.at[:, col * cut : (col + 1) * cut],
                    att_ref.at[n * rows : (n + 1) * rows, col * cut : (col + 1) * cut],
                    att_sem.at[n, col],
                )
                for n, source in enumerate((att_own_hbm, att_other_hbm))
            ]
        )
    for m in range(width // step):
        up_loads.append(
            pltpu.make_async_copy(
                up_own_hbm.at[:, m * step : (m + 1) * step],
                up_ref.at[:, m * step : (m + 1) * step],
                up_sem.at[m],
            )
        )
    for copy in [*att_loads[0], *up_loads, *att_loads[1]]:
        copy.start()

    def turn(m):
        up_loads[m].wait()
        strip = slice(m * step, (m + 1) * step)
        for n, source in enumerate((up_ref, up_other_ref)):
            up_t_ref[strip, n * rows : (n + 1) * rows] = source[:, strip].T

    turn(0)
    stores = []
    for col, sums_ref in enumerate((first_ref, second_ref)):
        for copy in att_loads[col]:
            copy.wait()
        cols = slice(col * cut, (col + 1) * cut)
        for m in range(width // step):
            if col == 0 and (m + 1) * step < width:
                turn(m + 1)
            sums_ref[m * step : (m + 1) * step, :] = jnp.dot(
                up_t_ref[m * step : (m + 1) * step, :],
                att_ref[:, cols],
                preferred_element_type=F32,
            ).astype(BF)
        for k, (out, stage, (other, lo, hi)) in enumerate(zip(outs, stages, coset_parts())):
            for block in range(lo, hi):
                row = pl.multiple_of(row_of(place, other, block), 16)
                stage[col, 16 * (block - lo) : 16 * (block - lo + 1), :] = sums_ref[
                    pl.ds(row, 16), :
                ]
            copy = pltpu.make_async_copy(stage.at[col], out.at[:, cols], out_sem.at[col, k])
            copy.start()
            stores.append(copy)
    for copy in stores:
        copy.wait()


def weight_sums(coset, up_own, up_other, att_own, att_other):
    rows, width = up_own.shape
    cols = att_own.shape[1]
    sizes = [16 * (hi - lo) for _, lo, hi in coset_parts()]
    return pl.pallas_call(
        weight_kernel,
        in_specs=[SMEM, VMEM] + [HBM] * 3,
        out_specs=[HBM] * len(sizes),
        out_shape=[jax.ShapeDtypeStruct((size, cols), BF) for size in sizes],
        scratch_shapes=[pltpu.VMEM((2, size, cols // 2), BF) for size in sizes]
        + [
            pltpu.VMEM((rows, width), BF),
            pltpu.VMEM((2 * rows, cols), BF),
            pltpu.VMEM((width, 2 * rows), BF),
            pltpu.VMEM((width, cols // 2), BF),
            pltpu.VMEM((width, cols // 2), BF),
            pltpu.SemaphoreType.DMA((width // 256,)),
            pltpu.SemaphoreType.DMA((2, 2)),
            pltpu.SemaphoreType.DMA((2, len(sizes))),
        ],
        compiler_params=whole_params(LIMIT),
        cost_estimate=pl.CostEstimate(
            flops=FLOPS_4US, bytes_accessed=10 << 20, transcendentals=0
        ),
        name="weight_sums",
    )(coset, up_other, up_own, att_own, att_other)


def spread_kernel(weight_ref, out_hbm, sem):
    cols = out_hbm.shape[2]
    copies = [
        pltpu.make_async_copy(
            weight_ref.at[:, cols * (n % 2) : cols * (n % 2 + 1)], out_hbm.at[n], sem.at[n]
        )
        for n in range(out_hbm.shape[0])
    ]
    for copy in copies:
        copy.start()
    for copy in copies:
        copy.wait()


def gather_weight(weight):
    rows, cols = weight.shape[0], weight.shape[1] // 2
    pieces = pl.pallas_call(
        spread_kernel,
        in_specs=[VMEM],
        out_specs=HBM,
        out_shape=jax.ShapeDtypeStruct((32, rows, cols), BF),
        scratch_shapes=[pltpu.SemaphoreType.DMA((32,))],
        compiler_params=whole_params(LIMIT),
        name="spread",
    )(weight)
    return exchange(pieces).reshape(32 * rows, cols)


def gather_cosets(block):
    half = block.shape[0] // 2
    parts = (block[:half], block[half:])
    result = [block]
    for axis in range(3):
        for half in range(2):
            result.append(lax.ppermute(parts[half], "d", shift(axis, 2 * half - 1)))
    return result


def add_kernel(own_ref, *refs):
    received, out_ref = refs[:6], refs[6]
    rows = received[0].shape[0]
    for half in range(2):
        for lo in range(0, rows, 16):
            total = own_ref[rows * half + lo : rows * half + lo + 16, :].astype(F32)
            for axis in range(3):
                total = total + received[2 * axis + half][lo : lo + 16, :].astype(F32)
            out_ref[rows * half + lo : rows * half + lo + 16, :] = total.astype(BF)


def reduce_cosets(pieces):
    received = []
    for n, piece in enumerate(pieces[1:]):
        received.append(lax.ppermute(piece, "d", shift(n // 2, 1 - 2 * (n % 2))))
    return received


def add_received(own, received):
    return pl.pallas_call(
        add_kernel,
        in_specs=[VMEM] * 7,
        out_specs=VMEM,
        out_shape=jax.ShapeDtypeStruct(own.shape, BF),
        compiler_params=whole_params(8),
        cost_estimate=pl.CostEstimate(flops=1 << 28, bytes_accessed=5 << 20, transcendentals=0),
        name="add_received",
    )(own, *received)


def own_rows(rows_in, total_tokens):
    rows = rows_in.reshape(16, 2, *rows_in.shape[1:]).astype(F32)
    sums = jnp.sum(rows, axis=0) * (1.0 / math.sqrt(total_tokens))
    return jnp.concatenate([sums[0], sums[1]], axis=1)


def shards(queries, keys, values, upstream, weight, sample_ids):
    rows = queries.shape[0]
    me = lax.axis_index("d")
    core = jnp.bitwise_and(me, 1)
    z = jnp.bitwise_and(jnp.right_shift(me, 4), 1)
    kx = jnp.bitwise_and(jnp.right_shift(me, 5) + z, 1)
    ky = jnp.bitwise_and(jnp.right_shift(me, 1) + z, 1)
    coset = jnp.stack([kx, ky]).astype(jnp.int32)
    base_own = core.astype(jnp.int32).reshape(1)
    base_other = (1 - core).astype(jnp.int32).reshape(1)

    up_other = lax.ppermute(upstream, "d", CORE_SWAP)
    mine = gather_weight(weight)
    att_a, prob_a = attend_forward(base_other, queries, keys, values, sample_ids)
    att_other = lax.ppermute(att_a, "d", CORE_SWAP)
    att_b, prob_b = attend_forward(base_own, queries, keys, values, sample_ids)
    sums = weight_sums(coset, upstream, up_other, att_b, att_other)
    received = reduce_cosets(sums)
    mine, _ = lax.optimization_barrier((mine, sums[0]))
    gathered = gather_cosets(mine)
    reduced = add_received(sums[0], received)
    rows_in = exchange(reduced.reshape(32, -1, reduced.shape[1]))
    grad_own, grad_sent = project(coset, upstream, up_other, gathered)
    grad_other = lax.ppermute(grad_sent, "d", CORE_SWAP)
    outs = attend_backward(
        base_own, queries, keys, values, grad_own, att_b, prob_b, ()
    )
    outs = attend_backward(
        base_other, queries, keys, values, grad_other, att_a, prob_a, tuple(outs)
    )
    grad_weight = own_rows(rows_in, rows * lax.axis_size("d"))
    return (*outs, grad_weight)


def solution(mesh):
    flat = Mesh(mesh.devices.reshape(-1), ("d",))
    return jax.shard_map(
        shards,
        mesh=flat,
        in_specs=(P("d", None),) * 6,
        out_specs=(P("d", None),) * 4,
        check_vma=False,
    )
```

time: 129 us -> 135 us (1.047)
  Pallas kernels: 42 us -> 52.3 us
  local copies, waits for them, and re-layouts: 7.5 us -> 4.68 us
    pallas_call x7, Pallas kernels: 40.5 us -> 50.8 us  [the longest x2 15.9 us: attend_backward(): pl.pallas_call(backward_kernel, in_specs=[SMEM, VMEM] + [HBM] * (5 + len(...]
    unnamed x28 -> x10, local copies, waits for them, and re-layouts: 6.45 us -> 2.6 us
  transfers between devices with their start and end apart: 17 -> 17, of which waited for: 4 -> 3; matrix products, arithmetic and copies ran while one was open for 3% -> 3% of each run, Pallas kernels for 28% -> 33%
where the time goes in v1:
time: 135 us
  Pallas kernels  52.3 us (39%)
  starting transfers between devices  41.2 us (31%)
  waiting for transfers between devices  34.2 us (25%)
  local copies, waits for them, and re-layouts  4.68 us (3%)
  other arithmetic  1.43 us (1%)
    all_to_all x2, starting transfers between devices, exchange(): lax.all_to_all(pieces, 'd', 0, 0, axis_index_groups=COSETS, tiled=True)  21.3 us
    ppermute x6, waiting for transfers between devices, gather_cosets(): result.append(lax.ppermute(parts[half], 'd', shift(axis, 2 * half - 1)))  18.3 us
    pallas_call x2, Pallas kernels, attend_backward(): pl.pallas_call(backward_kernel, in_specs=[SMEM, VMEM] + [HBM] * (5 + len(...  15.9 us
    ppermute x6, waiting for transfers between devices, reduce_cosets(): received.append(lax.ppermute(piece, 'd', shift(n // 2, 1 - 2 * (n % 2))))  15.8 us
    pallas_call x2, Pallas kernels, attend_forward(): pl.pallas_call(forward_kernel, in_specs=[SMEM, VMEM, HBM, HBM, HBM], out_...  13.4 us
    pallas_call x1, Pallas kernels, weight_sums(): pl.pallas_call(weight_kernel, in_specs=[SMEM, VMEM] + [HBM] * 3, out_spec...  10.7 us
    ppermute x6, starting transfers between devices, reduce_cosets(): received.append(lax.ppermute(piece, 'd', shift(n // 2, 1 - 2 * (n % 2))))  9.73 us
    pallas_call x1, Pallas kernels, project(): pl.pallas_call(project_kernel, in_specs=[SMEM, HBM, HBM] + [VMEM] * len(p...  8.74 us
  transfers between devices with their start and end apart: 17, of which 3 were waited for; matrix products, arithmetic and copies ran while one was open for 3% of the time, Pallas kernels for 33%

profile of v1, /device:TPU:1, one launch (start us, length us, event | category | flops | bytes accessed | tf_op | source)
XLA Modules:
  0.0 134.8 jit_solution(1388003723314543724)
XLA Ops:
  0.6 1.5 %collective-permute-start = (bf16[512,2048]{1,0:T(8,128)(2,1)}, bf16[512,2048]{1,0:T(8,128)(2,1)S(1)}, u32[]{:S(2)}, u32[]{:S(2)}) collective-permute-start(bf16[512,2048]{1,0:T(8,128)(2,1)} %up_own_hbm.3), channel_id=1, source_target_pairs={{0,1},{1,0},{2,3},{3,2},{4,5},{5,4},{6,7},{7,6},{8,9},{9,8},{10,11... | collective-permute-start | bytes 6291464 | tf_op jit(solution)/shard_map/ppermute | solution.py:567
  2.1 6.6 %attend_forward.3 = (bf16[512,1024]{1,0:T(8,128)(2,1)}, bf16[8,256,768]{2,1,0:T(8,128)(2,1)}) custom-call(s32[1]{0:T(128)} %bitcast.base_ref, s32[1,512]{1,0:T(1,128)} %ids_ref.3, bf16[512,2048]{1,0:T(8,128)(2,1)} %q_hbm.7, bf16[512,2048]{1,0:T(8,128)(2,1)} %k_hbm.7, bf16[512,2048]{1,0:T(8,128)(2,1)} %v_hbm.7), custom_call_target="tpu_custom_call" | custom-call | flops 3221225472 | bytes 9437184 | tf_op jit(solution)/shard_map/attend_forward/pallas_call | solution.py:167
  8.7 0.1 collective-permute-start.1
  8.8 2.1 %spread.1 = bf16[32,16,1024]{2,1,0:T(8,128)(2,1)} custom-call(bf16[16,2048]{1,0:T(8,128)(2,1)} %weight_ref.1), custom_call_target="tpu_custom_call" | custom-call | tf_op jit(solution)/shard_map/spread/pallas_call | solution.py:498
  10.9 11.1 %all-to-all-start = ((bf16[32,16,1024]{2,1,0:T(8,128)(2,1)}), bf16[32,16,1024]{2,1,0:T(8,128)(2,1)}, u32[]{:S(2)}, u32[]{:S(2)}) async-start(bf16[32,16,1024]{2,1,0:T(8,128)(2,1)} %spread.1), calls=%async_computation | async-start | bytes 2097152 | tf_op jit(solution)/shard_map/all_to_all | solution.py:58
  22.0 0.6 pad_add_fusion.coset
  22.6 6.7 %attend_forward.2 = (bf16[512,1024]{1,0:T(8,128)(2,1)}, bf16[8,256,768]{2,1,0:T(8,128)(2,1)}) custom-call(s32[1]{0:T(128)} %bitcast.4.base_ref, s32[1,512]{1,0:T(1,128)} %ids_ref.3, bf16[512,2048]{1,0:T(8,128)(2,1)} %q_hbm.7, bf16[512,2048]{1,0:T(8,128)(2,1)} %k_hbm.7, bf16[512,2048]{1,0:T(8,128)(2,1)} %v_hbm.7), custom_call_target="tpu_custom_call" | custom-call | flops 3221225472 | bytes 9437184 | tf_op jit(solution)/shard_map/attend_forward/pallas_call | solution.py:167
  29.3 0.0 collective-permute-done.1.att_other_hbm
  29.3 0.0 copy-start.4
  29.3 0.0 collective-permute-done.up_other_ref.up_other_hbm
  29.4 0.0 copy-start.2
  29.4 0.9 copy-done.4
  30.3 0.7 copy-done.2
  31.0 10.7 %weight_sums.1 = (bf16[512,1024]{1,0:T(8,128)(2,1)}, bf16[256,1024]{1,0:T(8,128)(2,1)}, bf16[256,1024]{1,0:T(8,128)(2,1)}, bf16[256,1024]{1,0:T(8,128)(2,1)}, bf...) custom-call(s32[2]{0:T(128)} %pad_add_fusion.coset, bf16[512,2048]{1,0:T(8,128)(2,1)} %copy-done.2, ...), custom_call_target="tpu_custom_call" | custom-call | flops 2147483648 | bytes 10485760 | tf_op jit(solution)/shard_map/weight_sums/pallas_call | solution.py:458
  41.7 0.0 copy-start
  41.7 0.4 collective-permute-start.9
  42.1 2.4 %collective-permute-start.10 = (bf16[256,1024]{1,0:T(8,128)(2,1)}, bf16[256,1024]{1,0:T(8,128)(2,1)S(1)}, u32[]{:S(2)}, u32[]{:S(2)}) collective-permute-start(bf16[256,1024]{1,0:T(8,128)(2,1)} %get-tuple-element.39), channel_id=1, source_target_pairs={{0,96},{1,97},{2,98},{3,99},{4,100},{5,101},{6,102},{7,103},{8,104... | collective-permute-start | bytes 1572872 | tf_op jit(solution)/shard_map/ppermute | solution.py:534
  44.5 0.0 all-to-all-done
  44.5 0.4 collective-permute-start.11
  44.9 2.3 %collective-permute-start.12 = (bf16[256,1024]{1,0:T(8,128)(2,1)}, bf16[256,1024]{1,0:T(8,128)(2,1)S(1)}, u32[]{:S(2)}, u32[]{:S(2)}) collective-permute-start(bf16[256,1024]{1,0:T(8,128)(2,1)} %get-tuple-element.41), channel_id=1, source_target_pairs={{0,6},{1,7},{2,0},{3,1},{4,2},{5,3},{6,4},{7,5},{8,14},{9,15},{10,... | collective-permute-start | bytes 1572872 | tf_op jit(solution)/shard_map/ppermute | solution.py:534
  47.1 1.5 %collective-permute-start.13 = (bf16[256,1024]{1,0:T(8,128)(2,1)}, bf16[256,1024]{1,0:T(8,128)(2,1)S(1)}, u32[]{:S(2)}, u32[]{:S(2)}) collective-permute-start(bf16[256,1024]{1,0:T(8,128)(2,1)} %get-tuple-element.42), channel_id=1, source_target_pairs={{0,16},{1,17},{2,18},{3,19},{4,20},{5,21},{6,22},{7,23},{8,24},{9,... | collective-permute-start | bytes 1572872 | tf_op jit(solution)/shard_map/ppermute | solution.py:534
  48.6 7.6 %collective-permute-done.9.refs_0_ = bf16[256,1024]{1,0:T(8,128)(2,1)S(1)} collective-permute-done((bf16[256,1024]{1,0:T(8,128)(2,1)}, bf16[256,1024]{1,0:T(8,128)(2,1)S(1)}, u32[]{:S(2)}, u32[]{:S(2)}) %collective-permute-start.9) | collective-permute-done | bytes 524320 | tf_op jit(solution)/shard_map/ppermute | solution.py:534
  56.2 2.8 %collective-permute-start.14 = (bf16[256,1024]{1,0:T(8,128)(2,1)}, bf16[256,1024]{1,0:T(8,128)(2,1)S(1)}, u32[]{:S(2)}, u32[]{:S(2)}) collective-permute-start(bf16[256,1024]{1,0:T(8,128)(2,1)} %get-tuple-element.43), channel_id=1, source_target_pairs={{0,24},{1,25},{2,26},{3,27},{4,28},{5,29},{6,30},{7,31},{8,16},{9,... | collective-permute-start | bytes 1572872 | tf_op jit(solution)/shard_map/ppermute | solution.py:534
  59.0 2.1 %fusion = (bf16[256,1024]{1,0:T(8,128)(2,1)}, bf16[256,1024]{1,0:T(8,128)(2,1)S(1)}) fusion(bf16[512,1024]{1,0:T(8,128)(2,1)} %bitcast.3.refs_0_), kind=kLoop, calls=%fused_computation.6 | loop fusion | bytes 2097152 | tf_op jit(solution)/shard_map/slice | solution.py:512
  61.1 0.0 collective-permute-done.10.refs_1_
  61.1 0.0 collective-permute-start.7
  61.1 0.0 collective-permute-done.11.refs_2_
  61.1 0.0 collective-permute-done.12.refs_3_
  61.1 0.0 collective-permute-done.13.refs_4_
  61.1 8.3 %collective-permute-done.14.refs_5_ = bf16[256,1024]{1,0:T(8,128)(2,1)S(1)} collective-permute-done((bf16[256,1024]{1,0:T(8,128)(2,1)}, bf16[256,1024]{1,0:T(8,128)(2,1)S(1)}, u32[]{:S(2)}, u32[]{:S(2)}) %collective-permute-start.14) | collective-permute-done | bytes 524320 | tf_op jit(solution)/shard_map/ppermute | solution.py:534
  69.4 0.0 copy-done
  69.4 1.5 %add_received.1 = bf16[512,1024]{1,0:T(8,128)(2,1)} custom-call(bf16[512,1024]{1,0:T(8,128)(2,1)S(1)} %copy-done, bf16[256,1024]{1,0:T(8,128)(2,1)S(1)} %collective-permute-done.9.refs_0_, bf16[256,1024]{1,0:T(8,128)(2,1)S(1)} %collective-permute-done.10.refs_1_, bf16[256,1024]{1,0:T(8,128)(2,1)S(1)} %collective-permute-done.11.refs_2_, ...), custom_call_target="tpu_custom_call" | custom-call | flops 268435456 | bytes 5242880 | tf_op jit(solution)/shard_map/add_received/pallas_call | solution.py:539
  70.9 0.0 copy-start.1
  70.9 10.2 %all-to-all-start.1 = ((bf16[32,16,1024]{2,1,0:T(8,128)(2,1)}), bf16[32,16,1024]{2,1,0:T(8,128)(2,1)S(1)}, u32[]{:S(2)}, u32[]{:S(2)}) async-start(bf16[32,16,1024]{2,1,0:T(8,128)(2,1)} %bitcast.5), calls=%async_computation.1 | async-start | bytes 2097152 | tf_op jit(solution)/shard_map/all_to_all | solution.py:58
  81.1 0.1 collective-permute-start.5
  81.2 0.3 collective-permute-start.3
  81.5 4.6 %collective-permute-start.6 = (bf16[256,1024]{1,0:T(8,128)(2,1)S(1)}, bf16[256,1024]{1,0:T(8,128)(2,1)S(1)}, u32[]{:S(2)}, u32[]{:S(2)}) collective-permute-start(bf16[256,1024]{1,0:T(8,128)(2,1)S(1)} %get-tuple-element.45), channel_id=1, source_target_pairs={{0,24},{1,25},{2,26},{3,27},{4,28},{5,29},{6,30},{7,31},{8,16},{9,... | collective-permute-start | bytes 1572872 | tf_op jit(solution)/shard_map/ppermute | solution.py:516
  86.1 1.3 collective-permute-start.4
  87.5 0.0 collective-permute-done.7.refs_6_
  87.5 1.5 %collective-permute-start.2 = (bf16[256,1024]{1,0:T(8,128)(2,1)S(1)}, bf16[256,1024]{1,0:T(8,128)(2,1)S(1)}, u32[]{:S(2)}, u32[]{:S(2)}) collective-permute-start(bf16[256,1024]{1,0:T(8,128)(2,1)S(1)} %get-tuple-element.45), channel_id=1, source_target_pairs={{0,96},{1,97},{2,98},{3,99},{4,100},{5,101},{6,102},{7,103},{8,104... | collective-permute-start | bytes 1572872 | tf_op jit(solution)/shard_map/ppermute | solution.py:516
  88.9 18.3 %collective-permute-done.5.refs_4_ = bf16[256,1024]{1,0:T(8,128)(2,1)S(1)} collective-permute-done((bf16[256,1024]{1,0:T(8,128)(2,1)}, bf16[256,1024]{1,0:T(8,128)(2,1)S(1)}, u32[]{:S(2)}, u32[]{:S(2)}) %collective-permute-start.5) | collective-permute-done | bytes 524320 | tf_op jit(solution)/shard_map/ppermute | solution.py:516
  107.3 0.0 collective-permute-done.3.refs_2_
  107.3 0.0 collective-permute-done.6.refs_5_
  107.3 0.0 collective-permute-done.4.refs_3_
  107.3 0.0 collective-permute-done.2.refs_1_
  107.3 0.0 copy-done.1
  107.3 8.7 %project.1 = (bf16[512,1024]{1,0:T(8,128)(2,1)}, bf16[512,1024]{1,0:T(8,128)(2,1)}) custom-call(s32[2]{0:T(128)S(1)} %copy-done.1, bf16[512,2048]{1,0:T(8,128)(2,1)} %up_own_hbm.3, bf16[512,2048]{1,0:T(8,128)(2,1)} %copy-done.2, bf16[512,1024]{1,0:T(8,128)(2,1)} %bitcast.3.refs_0_, bf16[256,1024]{1,0:T(8,128)(2,1)S(1)} %collective-permute-done.2.refs_1_, ...), custom_call_target="tpu_custom_call" | custom-call | flops 2147483648 | bytes 10485760 | tf_op jit(solution)/shard_map/project/pallas_call | solution.py:372
  116.0 0.8 collective-permute-start.8
  116.8 8.0 %attend_backward.2 = (bf16[512,2048]{1,0:T(8,128)(2,1)}, bf16[512,2048]{1,0:T(8,128)(2,1)}, bf16[512,2048]{1,0:T(8,128)(2,1)}) custom-call(s32[1]{0:T(128)} %bitcast.4.base_ref, bf16[512,1024]{1,0:T(8,128)(2,1)} %get-tuple-element.30.g_ref, bf16[512,2048]{1,0:T(8,128)(2,1)} %q_hbm.7, bf16[512,2048]{1,0:T(8,128)(2,1)} %k_hbm.7, bf16[512,2048]{1,0:T(8,128)(2,1)} %v_hbm.7, ...), custom_call_target="tpu_custom_call" | custom-call | flops 2147483648 | bytes 12582912 | tf_op jit(solution)/shard_map/attend_backward/pallas_call | solution.py:309
  124.8 0.0 all-to-all-done.1
  124.8 0.2 convert_reduce_fusion
  125.0 0.7 pad_maximum_fusion
  125.7 0.0 collective-permute-done.8.g_ref
  125.7 0.0 copy-start.3
  125.7 1.0 copy-done.3
  126.6 8.0 %attend_backward.3 = (bf16[512,2048]{1,0:T(8,128)(2,1)}, bf16[512,2048]{1,0:T(8,128)(2,1)}, bf16[512,2048]{1,0:T(8,128)(2,1)}) custom-call(s32[1]{0:T(128)} %bitcast.base_ref, bf16[512,1024]{1,0:T(8,128)(2,1)} %copy-done.3, bf16[512,2048]{1,0:T(8,128)(2,1)} %q_hbm.7, ...), custom_call_target="tpu_custom_call", output_to_operand_aliasing={{0}: (7, {}), {1}: (8, {}), {2}: (9, {})} | custom-call | flops 2147483648 | bytes 12582912 | tf_op jit(solution)/shard_map/attend_backward/pallas_call | solution.py:309
  (2 shorter events, 0.0 us)
Async XLA Ops:
  0.6 28.7 %collective-permute-start = (bf16[512,2048]{1,0:T(8,128)(2,1)}, bf16[512,2048]{1,0:T(8,128)(2,1)S(1)}, u32[]{:S(2)}, u32[]{:S(2)}) collective-permute-start(bf16[512,2048]{1,0:T(8,128)(2,1)} %up_own_hbm.3), channel_id=1, source_target_pairs={{0,1},{1,0},{2,3},{3,2},{4,5},{5,4},{6,7},{7,6},{8,9},{9,8},{10,11... | collective-permute-start | bytes 6291464 | tf_op jit(solution)/shard_map/ppermute | solution.py:567
  8.7 20.6 %collective-permute-start.1 = (bf16[512,1024]{1,0:T(8,128)(2,1)}, bf16[512,1024]{1,0:T(8,128)(2,1)S(1)}, u32[]{:S(2)}, u32[]{:S(2)}) collective-permute-start(bf16[512,1024]{1,0:T(8,128)(2,1)} %get-tuple-element.25.att_hbm), channel_id=1, source_target_pairs={{0,1},{1,0},{2,3},{3,2},{4,5},{5,4},{6,7},{7,6},{8,9},{9,8},{10,11... | collective-permute-start | bytes 3145736 | tf_op jit(solution)/shard_map/ppermute | solution.py:570
  10.9 33.5 %all-to-all-start = ((bf16[32,16,1024]{2,1,0:T(8,128)(2,1)}), bf16[32,16,1024]{2,1,0:T(8,128)(2,1)}, u32[]{:S(2)}, u32[]{:S(2)}) async-start(bf16[32,16,1024]{2,1,0:T(8,128)(2,1)} %spread.1), calls=%async_computation | async-start | bytes 2097152 | tf_op jit(solution)/shard_map/all_to_all | solution.py:58
  29.3 1.0 copy-start.4
  29.4 1.6 %copy-start.2 = (bf16[512,2048]{1,0:T(8,128)(2,1)}, bf16[512,2048]{1,0:T(8,128)(2,1)S(1)}, u32[]{:S(2)}) copy-start(bf16[512,2048]{1,0:T(8,128)(2,1)S(1)} %collective-permute-done.up_other_ref.up_other_hbm) | copy-start | bytes 6291460
  41.7 27.7 %copy-start = (bf16[512,1024]{1,0:T(8,128)(2,1)S(1)}, bf16[512,1024]{1,0:T(8,128)(2,1)}, u32[]{:S(2)}) copy-start(bf16[512,1024]{1,0:T(8,128)(2,1)} %get-tuple-element.26.own_ref) | copy-start | bytes 3145732
  41.7 14.5 %collective-permute-start.9 = (bf16[256,1024]{1,0:T(8,128)(2,1)}, bf16[256,1024]{1,0:T(8,128)(2,1)S(1)}, u32[]{:S(2)}, u32[]{:S(2)}) collective-permute-start(bf16[256,1024]{1,0:T(8,128)(2,1)} %get-tuple-element.38), channel_id=1, source_target_pairs={{0,32},{1,33},{2,34},{3,35},{4,36},{5,37},{6,38},{7,39},{8,40},{9,... | collective-permute-start | bytes 1572872 | tf_op jit(solution)/shard_map/ppermute | solution.py:534
  42.1 19.0 %collective-permute-start.10 = (bf16[256,1024]{1,0:T(8,128)(2,1)}, bf16[256,1024]{1,0:T(8,128)(2,1)S(1)}, u32[]{:S(2)}, u32[]{:S(2)}) collective-permute-start(bf16[256,1024]{1,0:T(8,128)(2,1)} %get-tuple-element.39), channel_id=1, source_target_pairs={{0,96},{1,97},{2,98},{3,99},{4,100},{5,101},{6,102},{7,103},{8,104... | collective-permute-start | bytes 1572872 | tf_op jit(solution)/shard_map/ppermute | solution.py:534
  44.5 16.6 %collective-permute-start.11 = (bf16[256,1024]{1,0:T(8,128)(2,1)}, bf16[256,1024]{1,0:T(8,128)(2,1)S(1)}, u32[]{:S(2)}, u32[]{:S(2)}) collective-permute-start(bf16[256,1024]{1,0:T(8,128)(2,1)} %get-tuple-element.40), channel_id=1, source_target_pairs={{0,2},{1,3},{2,4},{3,5},{4,6},{5,7},{6,0},{7,1},{8,10},{9,11},{10,... | collective-permute-start | bytes 1572872 | tf_op jit(solution)/shard_map/ppermute | solution.py:534
  44.9 16.2 %collective-permute-start.12 = (bf16[256,1024]{1,0:T(8,128)(2,1)}, bf16[256,1024]{1,0:T(8,128)(2,1)S(1)}, u32[]{:S(2)}, u32[]{:S(2)}) collective-permute-start(bf16[256,1024]{1,0:T(8,128)(2,1)} %get-tuple-element.41), channel_id=1, source_target_pairs={{0,6},{1,7},{2,0},{3,1},{4,2},{5,3},{6,4},{7,5},{8,14},{9,15},{10,... | collective-permute-start | bytes 1572872 | tf_op jit(solution)/shard_map/ppermute | solution.py:534
  47.1 14.0 %collective-permute-start.13 = (bf16[256,1024]{1,0:T(8,128)(2,1)}, bf16[256,1024]{1,0:T(8,128)(2,1)S(1)}, u32[]{:S(2)}, u32[]{:S(2)}) collective-permute-start(bf16[256,1024]{1,0:T(8,128)(2,1)} %get-tuple-element.42), channel_id=1, source_target_pairs={{0,16},{1,17},{2,18},{3,19},{4,20},{5,21},{6,22},{7,23},{8,24},{9,... | collective-permute-start | bytes 1572872 | tf_op jit(solution)/shard_map/ppermute | solution.py:534
  56.2 13.2 %collective-permute-start.14 = (bf16[256,1024]{1,0:T(8,128)(2,1)}, bf16[256,1024]{1,0:T(8,128)(2,1)S(1)}, u32[]{:S(2)}, u32[]{:S(2)}) collective-permute-start(bf16[256,1024]{1,0:T(8,128)(2,1)} %get-tuple-element.43), channel_id=1, source_target_pairs={{0,24},{1,25},{2,26},{3,27},{4,28},{5,29},{6,30},{7,31},{8,16},{9,... | collective-permute-start | bytes 1572872 | tf_op jit(solution)/shard_map/ppermute | solution.py:534
  61.1 26.4 %collective-permute-start.7 = (bf16[256,1024]{1,0:T(8,128)(2,1)}, bf16[256,1024]{1,0:T(8,128)(2,1)S(1)}, u32[]{:S(2)}, u32[]{:S(2)}) collective-permute-start(bf16[256,1024]{1,0:T(8,128)(2,1)} %get-tuple-element.44), channel_id=1, source_target_pairs={{0,16},{1,17},{2,18},{3,19},{4,20},{5,21},{6,22},{7,23},{8,24},{9,... | collective-permute-start | bytes 1572872 | tf_op jit(solution)/shard_map/ppermute | solution.py:516
  70.9 36.4 %copy-start.1 = (s32[2]{0:T(128)S(1)}, s32[2]{0:T(128)}, u32[]{:S(2)}) copy-start(s32[2]{0:T(128)} %pad_add_fusion.coset) | copy-start | bytes 28
  70.9 53.9 %all-to-all-start.1 = ((bf16[32,16,1024]{2,1,0:T(8,128)(2,1)}), bf16[32,16,1024]{2,1,0:T(8,128)(2,1)S(1)}, u32[]{:S(2)}, u32[]{:S(2)}) async-start(bf16[32,16,1024]{2,1,0:T(8,128)(2,1)} %bitcast.5), calls=%async_computation.1 | async-start | bytes 2097152 | tf_op jit(solution)/shard_map/all_to_all | solution.py:58
  81.1 26.2 %collective-permute-start.5 = (bf16[256,1024]{1,0:T(8,128)(2,1)}, bf16[256,1024]{1,0:T(8,128)(2,1)S(1)}, u32[]{:S(2)}, u32[]{:S(2)}) collective-permute-start(bf16[256,1024]{1,0:T(8,128)(2,1)} %get-tuple-element.44), channel_id=1, source_target_pairs={{0,2},{1,3},{2,4},{3,5},{4,6},{5,7},{6,0},{7,1},{8,10},{9,11},{10,... | collective-permute-start | bytes 1572872 | tf_op jit(solution)/shard_map/ppermute | solution.py:516
  81.2 26.1 %collective-permute-start.3 = (bf16[256,1024]{1,0:T(8,128)(2,1)}, bf16[256,1024]{1,0:T(8,128)(2,1)S(1)}, u32[]{:S(2)}, u32[]{:S(2)}) collective-permute-start(bf16[256,1024]{1,0:T(8,128)(2,1)} %get-tuple-element.44), channel_id=1, source_target_pairs={{0,32},{1,33},{2,34},{3,35},{4,36},{5,37},{6,38},{7,39},{8,40},{9,... | collective-permute-start | bytes 1572872 | tf_op jit(solution)/shard_map/ppermute | solution.py:516
  81.5 25.7 %collective-permute-start.6 = (bf16[256,1024]{1,0:T(8,128)(2,1)S(1)}, bf16[256,1024]{1,0:T(8,128)(2,1)S(1)}, u32[]{:S(2)}, u32[]{:S(2)}) collective-permute-start(bf16[256,1024]{1,0:T(8,128)(2,1)S(1)} %get-tuple-element.45), channel_id=1, source_target_pairs={{0,24},{1,25},{2,26},{3,27},{4,28},{5,29},{6,30},{7,31},{8,16},{9,... | collective-permute-start | bytes 1572872 | tf_op jit(solution)/shard_map/ppermute | solution.py:516
  86.1 21.1 %collective-permute-start.4 = (bf16[256,1024]{1,0:T(8,128)(2,1)S(1)}, bf16[256,1024]{1,0:T(8,128)(2,1)S(1)}, u32[]{:S(2)}, u32[]{:S(2)}) collective-permute-start(bf16[256,1024]{1,0:T(8,128)(2,1)S(1)} %get-tuple-element.45), channel_id=1, source_target_pairs={{0,6},{1,7},{2,0},{3,1},{4,2},{5,3},{6,4},{7,5},{8,14},{9,15},{10,... | collective-permute-start | bytes 1572872 | tf_op jit(solution)/shard_map/ppermute | solution.py:516
  87.5 19.8 %collective-permute-start.2 = (bf16[256,1024]{1,0:T(8,128)(2,1)S(1)}, bf16[256,1024]{1,0:T(8,128)(2,1)S(1)}, u32[]{:S(2)}, u32[]{:S(2)}) collective-permute-start(bf16[256,1024]{1,0:T(8,128)(2,1)S(1)} %get-tuple-element.45), channel_id=1, source_target_pairs={{0,96},{1,97},{2,98},{3,99},{4,100},{5,101},{6,102},{7,103},{8,104... | collective-permute-start | bytes 1572872 | tf_op jit(solution)/shard_map/ppermute | solution.py:516
  116.0 9.6 %collective-permute-start.8 = (bf16[512,1024]{1,0:T(8,128)(2,1)}, bf16[512,1024]{1,0:T(8,128)(2,1)S(1)}, u32[]{:S(2)}, u32[]{:S(2)}) collective-permute-start(bf16[512,1024]{1,0:T(8,128)(2,1)} %get-tuple-element.28), channel_id=1, source_target_pairs={{0,1},{1,0},{2,3},{3,2},{4,5},{5,4},{6,7},{7,6},{8,9},{9,8},{10,11... | collective-permute-start | bytes 3145736 | tf_op jit(solution)/shard_map/ppermute | solution.py:579
  125.7 1.0 copy-start.3

commit v2 on v0

--- a/solution.py
+++ b/solution.py
@@ -1,3 +1,4 @@
+import functools
 import math
 
 import jax
@@ -13,6 +14,12 @@
 HALF = 8
 STEP_HEADS = 4
 LIMIT = 50
+LIMIT_A = 60
+LIMIT_BACK = 50
+LIMIT_LAST = 50
+LIMIT_SPREAD = 58
+LIMIT_WHOLE = 20
+LIMIT_SMALL = 8
 FLOPS_4US = 2 << 30
 FLOPS_6US = 3 << 30
 SCALE = 1.0 / math.sqrt(DH)
@@ -42,6 +49,7 @@
     for kx in range(2)
     for ky in range(2)
 ]
+CHIPS = [coset[core::2] for coset in COSETS for core in range(2)]
 CORE_SWAP = [(i, i ^ 1) for i in range(128)]
 
 
@@ -58,9 +66,9 @@
     return lax.all_to_all(pieces, "d", 0, 0, axis_index_groups=COSETS, tiled=True)
 
 
-def grid_params():
+def grid_params(mib):
     return pltpu.CompilerParams(
-        dimension_semantics=("arbitrary",), vmem_limit_bytes=LIMIT * 1024 * 1024
+        dimension_semantics=("arbitrary",), vmem_limit_bytes=mib * 1024 * 1024
     )
 
 
@@ -122,7 +130,7 @@
     attend(*waiting)
 
 
-def attend_forward(base, queries, keys, values, ids):
+def attend_forward(base, queries, keys, values, ids, mib):
     rows = queries.shape[0]
     head = pl.BlockSpec((rows, DH * STEP_HEADS), lambda i, b: (0, b[0] + i))
     return pl.pallas_call(
@@ -141,7 +149,7 @@
             jax.ShapeDtypeStruct((rows, HALF * DH), BF),
             jax.ShapeDtypeStruct((HALF, rows, rows), BF),
         ],
-        compiler_params=grid_params(),
+        compiler_params=grid_params(mib),
         cost_estimate=pl.CostEstimate(
             flops=FLOPS_6US, bytes_accessed=9 << 20, transcendentals=1 << 20
         ),
@@ -222,7 +230,7 @@
     finish(*waiting)
 
 
-def attend_backward(base, queries, keys, values, grad, attended, probs, previous):
+def attend_backward(base, queries, keys, values, grad, attended, probs, previous, mib):
     rows = queries.shape[0]
     head = pl.BlockSpec((rows, DH * STEP_HEADS), lambda i, b: (0, b[0] + i))
     half = pl.BlockSpec((rows, DH * STEP_HEADS), lambda i, b: (0, i))
@@ -239,7 +247,7 @@
         ),
         out_shape=[shape, shape, shape],
         input_output_aliases={7 + n: n for n in range(len(previous))},
-        compiler_params=grid_params(),
+        compiler_params=grid_params(mib),
         cost_estimate=pl.CostEstimate(
             flops=FLOPS_4US, bytes_accessed=12 << 20, transcendentals=0
         ),
@@ -262,9 +270,9 @@
         yield other, 16, 32
 
 
-def project_kernel(coset, up_own_ref, up_other_ref, *refs):
+def project_kernel(kx_ref, ky_ref, up_own_ref, up_other_ref, *refs):
     pieces, (own_ref, other_ref, weight_ref) = refs[:7], refs[7:]
-    place = (coset[0], coset[1])
+    place = (kx_ref[0], ky_ref[0])
     for ref, (other, lo, hi) in zip(pieces, coset_parts()):
         for block in range(lo, hi):
             row = pl.multiple_of(row_of(place, other, block), 16)
@@ -286,22 +294,22 @@
     cols = pieces[0].shape[1]
     return pl.pallas_call(
         project_kernel,
-        in_specs=[SMEM] + [VMEM] * (2 + len(pieces)),
+        in_specs=[SMEM] * 2 + [VMEM] * (2 + len(pieces)),
         out_specs=[VMEM] * 2,
         out_shape=[jax.ShapeDtypeStruct((rows, cols), BF)] * 2,
         scratch_shapes=[pltpu.VMEM((width, cols), BF)],
-        compiler_params=whole_params(20),
+        compiler_params=whole_params(LIMIT_WHOLE),
         cost_estimate=pl.CostEstimate(
             flops=FLOPS_4US, bytes_accessed=10 << 20, transcendentals=0
         ),
         name="project",
-    )(coset, up_own, up_other, *pieces)
-
-
-def weight_kernel(coset, up_own_ref, up_other_ref, att_own_ref, att_other_ref, *refs):
+    )(*coset, up_own, up_other, *pieces)
+
+
+def weight_kernel(kx_ref, ky_ref, up_own_ref, up_other_ref, att_own_ref, att_other_ref, *refs):
     outs, sums_ref = refs[:7], refs[7]
     width = up_own_ref.shape[1]
-    place = (coset[0], coset[1])
+    place = (kx_ref[0], ky_ref[0])
     step, cut = 256, 512
 
     def strip(lo):
@@ -333,40 +341,62 @@
     sizes = [16 * (hi - lo) for _, lo, hi in coset_parts()]
     return pl.pallas_call(
         weight_kernel,
-        in_specs=[SMEM] + [VMEM] * 4,
+        in_specs=[SMEM] * 2 + [VMEM] * 4,
         out_specs=[VMEM] * len(sizes),
         out_shape=[jax.ShapeDtypeStruct((size, cols), BF) for size in sizes],
         scratch_shapes=[pltpu.VMEM((width, cols), BF)],
-        compiler_params=whole_params(20),
+        compiler_params=whole_params(LIMIT_WHOLE),
         cost_estimate=pl.CostEstimate(
             flops=FLOPS_4US, bytes_accessed=10 << 20, transcendentals=0
         ),
         name="weight_sums",
-    )(coset, up_own, up_other, att_own, att_other)
-
-
-def spread_kernel(weight_ref, out_ref):
-    cols = out_ref.shape[2]
+    )(*coset, up_own, up_other, att_own, att_other)
+
+
+def spread_kernel(core_ref, own_ref, other_ref, out_ref):
+    core = core_ref[0]
+    rows, cols = own_ref.shape[0], out_ref.shape[2]
+    mine = pl.ds(pl.multiple_of(core * cols, DH), cols)
+    own, other = own_ref[:, mine], other_ref[:, mine]
     for n in range(out_ref.shape[0]):
-        out_ref[n] = weight_ref[:, cols * (n % 2) : cols * (n % 2 + 1)]
-
-
-def gather_weight(weight):
+        out_ref[n, pl.ds(pl.multiple_of(core * rows, rows), rows), :] = own
+        out_ref[n, pl.ds(pl.multiple_of((1 - core) * rows, rows), rows), :] = other
+
+
+def gather_weight(core, weight, other):
     rows, cols = weight.shape[0], weight.shape[1] // 2
     pieces = pl.pallas_call(
         spread_kernel,
+        in_specs=[SMEM, VMEM, VMEM],
+        out_specs=VMEM,
+        out_shape=jax.ShapeDtypeStruct((16, 2 * rows, cols), BF),
+        compiler_params=whole_params(LIMIT_SPREAD),
+        name="spread",
+    )(core, weight, other)
+    block = lax.all_to_all(pieces, "d", 0, 0, axis_index_groups=CHIPS, tiled=True)
+    return block.reshape(32 * rows, cols)
+
+
+def split_kernel(block_ref, low_ref, high_ref):
+    half = low_ref.shape[0]
+    low_ref[...] = block_ref[:half, :]
+    high_ref[...] = block_ref[half:, :]
+
+
+def split(block):
+    half = jax.ShapeDtypeStruct((block.shape[0] // 2, block.shape[1]), BF)
+    return pl.pallas_call(
+        split_kernel,
         in_specs=[VMEM],
-        out_specs=VMEM,
-        out_shape=jax.ShapeDtypeStruct((32, rows, cols), BF),
-        compiler_params=whole_params(8),
-        name="spread",
-    )(weight)
-    return exchange(pieces).reshape(32 * rows, cols)
+        out_specs=[VMEM] * 2,
+        out_shape=[half] * 2,
+        compiler_params=whole_params(4),
+        name="split",
+    )(block)
 
 
 def gather_cosets(block):
-    half = block.shape[0] // 2
-    parts = (block[:half], block[half:])
+    parts = split(block)
     result = [block]
     for axis in range(3):
         for half in range(2):
@@ -398,16 +428,31 @@
         in_specs=[VMEM] * 7,
         out_specs=VMEM,
         out_shape=jax.ShapeDtypeStruct(own.shape, BF),
-        compiler_params=whole_params(8),
+        compiler_params=whole_params(LIMIT_SMALL),
         cost_estimate=pl.CostEstimate(flops=1 << 28, bytes_accessed=5 << 20, transcendentals=0),
         name="add_received",
     )(own, *received)
 
 
+def own_rows_kernel(in_ref, out_ref, *, factor):
+    cols = in_ref.shape[2]
+    for half in range(2):
+        total = in_ref[half].astype(F32)
+        for n in range(1, in_ref.shape[0] // 2):
+            total = total + in_ref[2 * n + half].astype(F32)
+        out_ref[:, half * cols : (half + 1) * cols] = total * factor
+
+
 def own_rows(rows_in, total_tokens):
-    rows = rows_in.reshape(16, 2, *rows_in.shape[1:]).astype(F32)
-    sums = jnp.sum(rows, axis=0) * (1.0 / math.sqrt(total_tokens))
-    return jnp.concatenate([sums[0], sums[1]], axis=1)
+    _, rows, cols = rows_in.shape
+    return pl.pallas_call(
+        functools.partial(own_rows_kernel, factor=1.0 / math.sqrt(total_tokens)),
+        in_specs=[VMEM],
+        out_specs=VMEM,
+        out_shape=jax.ShapeDtypeStruct((rows, 2 * cols), F32),
+        compiler_params=whole_params(LIMIT_SMALL),
+        name="own_rows",
+    )(rows_in)
 
 
 def shards(queries, keys, values, upstream, weight, sample_ids):
@@ -417,16 +462,19 @@
     z = jnp.bitwise_and(jnp.right_shift(me, 4), 1)
     kx = jnp.bitwise_and(jnp.right_shift(me, 5) + z, 1)
     ky = jnp.bitwise_and(jnp.right_shift(me, 1) + z, 1)
-    coset = jnp.stack([kx, ky]).astype(jnp.int32)
+    coset = (kx.astype(jnp.int32).reshape(1), ky.astype(jnp.int32).reshape(1))
     steps = HALF // STEP_HEADS
     base_own = (steps * core).astype(jnp.int32).reshape(1)
     base_other = (steps * (1 - core)).astype(jnp.int32).reshape(1)
 
     up_other = lax.ppermute(upstream, "d", CORE_SWAP)
-    mine = gather_weight(weight)
-    att_a, prob_a = attend_forward(base_other, queries, keys, values, sample_ids)
+    other = lax.ppermute(weight, "d", CORE_SWAP)
+    mine = gather_weight(core.astype(jnp.int32).reshape(1), weight, other)
+    att_a, prob_a = attend_forward(
+        base_other, queries, keys, values, sample_ids, LIMIT_A
+    )
     att_other = lax.ppermute(att_a, "d", CORE_SWAP)
-    att_b, prob_b = attend_forward(base_own, queries, keys, values, sample_ids)
+    att_b, prob_b = attend_forward(base_own, queries, keys, values, sample_ids, LIMIT)
     sums = weight_sums(coset, upstream, up_other, att_b, att_other)
     received = reduce_cosets(sums)
     mine, _ = lax.optimization_barrier((mine, sums[0]))
@@ -435,9 +483,11 @@
     rows_in = exchange(reduced.reshape(32, -1, reduced.shape[1]))
     grad_own, grad_sent = project(coset, upstream, up_other, gathered)
     grad_other = lax.ppermute(grad_sent, "d", CORE_SWAP)
-    outs = attend_backward(base_own, queries, keys, values, grad_own, att_b, prob_b, ())
     outs = attend_backward(
-        base_other, queries, keys, values, grad_other, att_a, prob_a, tuple(outs)
+        base_own, queries, keys, values, grad_own, att_b, prob_b, (), LIMIT_BACK
+    )
+    outs = attend_backward(
+        base_other, queries, keys, values, grad_other, att_a, prob_a, tuple(outs), LIMIT_LAST
     )
     grad_weight = own_rows(rows_in, rows * lax.axis_size("d"))
     return (*outs, grad_weight)

time: 129 us -> 125 us (0.969)
  waiting for transfers between devices: 35.4 us -> 31.3 us
  other arithmetic: 2.18 us -> 0 us
  Pallas kernels: 42 us -> 43.5 us
    all_to_all x2 -> x1, waiting for transfers between devices: 0.01 us -> 12.7 us  [exchange(): lax.all_to_all(pieces, 'd', 0, 0, axis_index_groups=COSETS, tiled=True)]
    all_to_all x2 -> x1, starting transfers between devices: 21.2 us -> 8.72 us  [exchange(): lax.all_to_all(pieces, 'd', 0, 0, axis_index_groups=COSETS, tiled=True)]
    ppermute x6, waiting for transfers between devices: 17.1 us -> 6.68 us  [reduce_cosets(): received.append(lax.ppermute(piece, 'd', shift(n // 2, 1 - 2 * (n % 2))))]
    all_to_all x0 -> x1, starting transfers between devices: none -> 10.2 us  [gather_weight(): lax.all_to_all(pieces, 'd', 0, 0, axis_index_groups=CHIPS, tiled=True)]
    ppermute x6, waiting for transfers between devices: 18.3 us -> 9.38 us  [gather_cosets(): result.append(lax.ppermute(parts[half], 'd', shift(axis, 2 * half - 1)))]
    ppermute x1, starting transfers between devices: 0.74 us -> 4.22 us  [shards(): grad_other = lax.ppermute(grad_sent, 'd', CORE_SWAP)]
    ppermute x6, starting transfers between devices: 9.47 us -> 6.61 us  [reduce_cosets(): received.append(lax.ppermute(piece, 'd', shift(n // 2, 1 - 2 * (n % 2))))]
    ppermute x0 -> x1, waiting for transfers between devices: none -> 2.49 us  [shards(): other = lax.ppermute(weight, 'd', CORE_SWAP)]
  transfers between devices with their start and end apart: 17 -> 18, of which waited for: 4 -> 7; matrix products, arithmetic and copies ran while one was open for 3% -> 0% of each run, Pallas kernels for 28% -> 30%
where the time goes in v2:
time: 125 us; the launch traced here: 124 us
  Pallas kernels  43.5 us (35%)
  starting transfers between devices  39.9 us (32%)
  waiting for transfers between devices  31.3 us (25%)
  local copies, waits for them, and re-layouts  8.64 us (7%)
    pallas_call x2, Pallas kernels, attend_forward(): pl.pallas_call(forward_kernel, grid_spec=pltpu.PrefetchScalarGridSpec(num...  13.1 us
    pallas_call x2, Pallas kernels, attend_backward(): pl.pallas_call(backward_kernel, grid_spec=pltpu.PrefetchScalarGridSpec(nu...  12.9 us
    all_to_all x1, waiting for transfers between devices, exchange(): lax.all_to_all(pieces, 'd', 0, 0, axis_index_groups=COSETS, tiled=True)  12.7 us
    all_to_all x1, starting transfers between devices, gather_weight(): lax.all_to_all(pieces, 'd', 0, 0, axis_index_groups=CHIPS, tiled=True)  10.2 us
    ppermute x6, waiting for transfers between devices, gather_cosets(): result.append(lax.ppermute(parts[half], 'd', shift(axis, 2 * half - 1)))  9.38 us
    all_to_all x1, starting transfers between devices, exchange(): lax.all_to_all(pieces, 'd', 0, 0, axis_index_groups=COSETS, tiled=True)  8.72 us
    unnamed x38, local copies, waits for them, and re-layouts  8.64 us
    ppermute x6, starting transfers between devices, gather_cosets(): result.append(lax.ppermute(parts[half], 'd', shift(axis, 2 * half - 1)))  8.12 us
  transfers between devices with their start and end apart: 18, of which 7 were waited for; matrix products, arithmetic and copies ran while one was open for 0% of the time, Pallas kernels for 30%

profile of v2, /device:TPU:1, one launch (start us, length us, event | category | flops | bytes accessed | tf_op | source)
XLA Modules:
  0.0 124.1 jit_solution(54612686898163510)
XLA Ops:
  0.6 1.5 %collective-permute-start = (bf16[512,2048]{1,0:T(8,128)(2,1)}, bf16[512,2048]{1,0:T(8,128)(2,1)}, u32[]{:S(2)}, u32[]{:S(2)}) collective-permute-start(bf16[512,2048]{1,0:T(8,128)(2,1)} %up_own_ref.3), channel_id=1, source_target_pairs={{0,1},{1,0},{2,3},{3,2},{4,5},{5,4},{6,7},{7,6},{8,9},{9,8},{10,11... | collective-permute-start | bytes 6291464 | tf_op jit(solution)/shard_map/ppermute | solution.py:470
  2.1 6.5 %attend_forward.3 = (bf16[512,1024]{1,0:T(8,128)(2,1)}, bf16[8,512,512]{2,1,0:T(8,128)(2,1)}) custom-call(s32[1]{0:T(128)} %bitcast.base, bf16[512,2048]{1,0:T(8,128)(2,1)} %q_ref.7, bf16[512,2048]{1,0:T(8,128)(2,1)} %k_ref.7, bf16[512,2048]{1,0:T(8,128)(2,1)} %v_ref.7, s32[1,512]{1,0:T(1,128)} %ids_ref.3), custom_call_target="tpu_custom_call" | custom-call | flops 3221225472 | bytes 9437184 | tf_op jit(solution)/shard_map/attend_forward/pallas_call | solution.py:136
  8.6 0.1 collective-permute-start.2
  8.7 0.0 copy-done.17
  8.7 0.5 collective-permute-start.1
  9.2 2.5 %collective-permute-done.1.other_ref = bf16[16,2048]{1,0:T(8,128)(2,1)S(1)} collective-permute-done((bf16[16,2048]{1,0:T(8,128)(2,1)S(1)}, bf16[16,2048]{1,0:T(8,128)(2,1)S(1)}, u32[]{:S(2)}, u32[]{:S(2)}) %collective-permute-start.1) | collective-permute-done | bytes 65568 | tf_op jit(solution)/shard_map/ppermute | solution.py:471
  11.7 0.6 copy-done.18
  12.3 1.9 %spread.1 = bf16[16,32,1024]{2,1,0:T(8,128)(2,1)} custom-call(s32[1]{0:T(128)} %bitcast.3.core_ref, bf16[16,2048]{1,0:T(8,128)(2,1)} %own_ref.1, bf16[16,2048]{1,0:T(8,128)(2,1)} %copy-done.18), custom_call_target="tpu_custom_call" | custom-call | tf_op jit(solution)/shard_map/spread/pallas_call | solution.py:368
  14.2 10.2 %all-to-all-start = ((bf16[16,32,1024]{2,1,0:T(8,128)(2,1)}), bf16[16,32,1024]{2,1,0:T(8,128)(2,1)S(1)}, u32[]{:S(2)}, u32[]{:S(2)}) async-start(bf16[16,32,1024]{2,1,0:T(8,128)(2,1)} %spread.1), calls=%async_computation | async-start | bytes 2097152 | tf_op jit(solution)/shard_map/all_to_all | solution.py:376
  24.5 0.0 copy-done
  24.5 0.0 copy-done.16
  24.5 0.0 copy-start.1
  24.5 6.6 %attend_forward.2 = (bf16[512,1024]{1,0:T(8,128)(2,1)S(1)}, bf16[8,512,512]{2,1,0:T(8,128)(2,1)}) custom-call(s32[1]{0:T(128)} %bitcast.5.base, bf16[512,2048]{1,0:T(8,128)(2,1)S(1)} %copy-done, bf16[512,2048]{1,0:T(8,128)(2,1)} %k_ref.7, bf16[512,2048]{1,0:T(8,128)(2,1)} %v_ref.7, s32[1,512]{1,0:T(1,128)S(1)} %copy-done.16), custom_call_target="tpu_custom_call" | custom-call | flops 3221225472 | bytes 9437184 | tf_op jit(solution)/shard_map/attend_forward/pallas_call | solution.py:136
  31.1 0.0 collective-permute-done.2.att_other_ref
  31.1 0.0 collective-permute-done.up_other_ref
  31.1 0.0 copy-start.2
  31.1 6.8 %weight_sums.1 = (bf16[512,1024]{1,0:T(8,128)(2,1)S(1)}, bf16[256,1024]{1,0:T(8,128)(2,1)S(1)}, bf16[256,1024]{1,0:T(8,128)(2,1)S(1)}, bf16[256,1024]{1,0:T(8,12...) custom-call(s32[1]{0:T(128)} %bitcast.1.kx_ref, ...), custom_call_target="tpu_custom_call" | custom-call | flops 2147483648 | bytes 10485760 | tf_op jit(solution)/shard_map/weight_sums/pallas_call | solution.py:342
  37.9 0.0 copy-start.3
  38.0 1.0 copy-done.3
  38.9 1.0 copy-done.5
  39.9 0.8 copy-done.10
  40.7 0.8 copy-done.11
  41.5 0.8 copy-done.12
  42.3 0.8 copy-done.13
  43.1 0.8 copy-done.14
  43.9 0.8 copy-done.15
  44.7 0.0 all-to-all-done
  44.7 0.3 collective-permute-start.10
  45.0 0.1 split.1
  45.1 3.6 %collective-permute-start.7 = (bf16[256,1024]{1,0:T(8,128)(2,1)S(1)}, bf16[256,1024]{1,0:T(8,128)(2,1)S(1)}, u32[]{:S(2)}, u32[]{:S(2)}) collective-permute-start(bf16[256,1024]{1,0:T(8,128)(2,1)S(1)} %get-tuple-element.30), channel_id=1, source_target_pairs={{0,24},{1,25},{2,26},{3,27},{4,28},{5,29},{6,30},{7,31},{8,16},{9,... | collective-permute-start | bytes 1572872 | tf_op jit(solution)/shard_map/ppermute | solution.py:403
  48.7 2.3 %collective-permute-start.5 = (bf16[256,1024]{1,0:T(8,128)(2,1)S(1)}, bf16[256,1024]{1,0:T(8,128)(2,1)S(1)}, u32[]{:S(2)}, u32[]{:S(2)}) collective-permute-start(bf16[256,1024]{1,0:T(8,128)(2,1)S(1)} %get-tuple-element.30), channel_id=1, source_target_pairs={{0,6},{1,7},{2,0},{3,1},{4,2},{5,3},{6,4},{7,5},{8,14},{9,15},{10,... | collective-permute-start | bytes 1572872 | tf_op jit(solution)/shard_map/ppermute | solution.py:403
  51.0 1.5 %collective-permute-start.3 = (bf16[256,1024]{1,0:T(8,128)(2,1)S(1)}, bf16[256,1024]{1,0:T(8,128)(2,1)S(1)}, u32[]{:S(2)}, u32[]{:S(2)}) collective-permute-start(bf16[256,1024]{1,0:T(8,128)(2,1)S(1)} %get-tuple-element.30), channel_id=1, source_target_pairs={{0,96},{1,97},{2,98},{3,99},{4,100},{5,101},{6,102},{7,103},{8,104... | collective-permute-start | bytes 1572872 | tf_op jit(solution)/shard_map/ppermute | solution.py:403
  52.5 0.0 collective-permute-start.8
  52.5 6.7 %collective-permute-done.10.refs_0_ = bf16[256,1024]{1,0:T(8,128)(2,1)S(1)} collective-permute-done((bf16[256,1024]{1,0:T(8,128)(2,1)}, bf16[256,1024]{1,0:T(8,128)(2,1)S(1)}, u32[]{:S(2)}, u32[]{:S(2)}) %collective-permute-start.10) | collective-permute-done | bytes 524320 | tf_op jit(solution)/shard_map/ppermute | solution.py:421
  59.2 0.4 collective-permute-start.6
  59.6 0.0 collective-permute-done.7.refs_5_
  59.6 0.3 collective-permute-start.4
  59.9 1.1 collective-permute-done.5.refs_3_
  61.0 1.5 %collective-permute-start.11 = (bf16[256,1024]{1,0:T(8,128)(2,1)}, bf16[256,1024]{1,0:T(8,128)(2,1)S(1)}, u32[]{:S(2)}, u32[]{:S(2)}) collective-permute-start(bf16[256,1024]{1,0:T(8,128)(2,1)} %copy-done.14), channel_id=1, source_target_pairs={{0,96},{1,97},{2,98},{3,99},{4,100},{5,101},{6,102},{7,103},{8,104... | collective-permute-start | bytes 1572872 | tf_op jit(solution)/shard_map/ppermute | solution.py:421
  62.6 0.4 collective-permute-done.3.refs_1_
  63.0 1.2 collective-permute-start.12
  64.1 1.3 %collective-permute-done.8.refs_6_ = bf16[256,1024]{1,0:T(8,128)(2,1)S(1)} collective-permute-done((bf16[256,1024]{1,0:T(8,128)(2,1)S(1)}, bf16[256,1024]{1,0:T(8,128)(2,1)S(1)}, u32[]{:S(2)}, u32[]{:S(2)}) %collective-permute-start.8) | collective-permute-done | bytes 524320 | tf_op jit(solution)/shard_map/ppermute | solution.py:403
  65.4 0.6 collective-permute-start.13
  66.0 6.6 %collective-permute-done.6.refs_4_ = bf16[256,1024]{1,0:T(8,128)(2,1)S(1)} collective-permute-done((bf16[256,1024]{1,0:T(8,128)(2,1)S(1)}, bf16[256,1024]{1,0:T(8,128)(2,1)S(1)}, u32[]{:S(2)}, u32[]{:S(2)}) %collective-permute-start.6) | collective-permute-done | bytes 524320 | tf_op jit(solution)/shard_map/ppermute | solution.py:403
  72.6 0.9 collective-permute-start.14
  73.5 0.0 collective-permute-done.4.refs_2_
  73.5 2.0 %collective-permute-start.15 = (bf16[256,1024]{1,0:T(8,128)(2,1)}, bf16[256,1024]{1,0:T(8,128)(2,1)S(1)}, u32[]{:S(2)}, u32[]{:S(2)}) collective-permute-start(bf16[256,1024]{1,0:T(8,128)(2,1)} %copy-done.10), channel_id=1, source_target_pairs={{0,24},{1,25},{2,26},{3,27},{4,28},{5,29},{6,30},{7,31},{8,16},{9,... | collective-permute-start | bytes 1572872 | tf_op jit(solution)/shard_map/ppermute | solution.py:421
  75.6 6.4 %project.1 = (bf16[512,1024]{1,0:T(8,128)(2,1)S(1)}, bf16[512,1024]{1,0:T(8,128)(2,1)}) custom-call(s32[1]{0:T(128)} %bitcast.1.kx_ref, s32[1]{0:T(128)} %bitcast.2.ky_ref, bf16[512,2048]{1,0:T(8,128)(2,1)S(1)} %copy-done.2, bf16[512,2048]{1,0:T(8,128)(2,1)} %collective-permute-done.up_other_ref, bf16[512,1024]{1,0:T(8,128)(2,1)S(1)} %bitcast.8, ...), custom_call_target="tpu_custom_call" | custom-call | flops 2147483648 | bytes 10485760 | tf_op jit(solution)/shard_map/project/pallas_call | solution.py:295
  81.9 0.0 copy-start.7
  82.0 0.0 collective-permute-done.11.refs_1_
  82.0 4.2 %collective-permute-start.9 = (bf16[512,1024]{1,0:T(8,128)(2,1)}, bf16[512,1024]{1,0:T(8,128)(2,1)}, u32[]{:S(2)}, u32[]{:S(2)}) collective-permute-start(bf16[512,1024]{1,0:T(8,128)(2,1)} %get-tuple-element.32), channel_id=1, source_target_pairs={{0,1},{1,0},{2,3},{3,2},{4,5},{5,4},{6,7},{7,6},{8,9},{9,8},{10,11... | collective-permute-start | bytes 3145736 | tf_op jit(solution)/shard_map/ppermute | solution.py:485
  86.2 0.0 collective-permute-done.12.refs_2_
  86.2 0.0 collective-permute-done.13.refs_3_
  86.2 0.0 collective-permute-done.14.refs_4_
  86.2 0.0 collective-permute-done.15.refs_5_
  86.2 1.5 %add_received.1 = bf16[512,1024]{1,0:T(8,128)(2,1)} custom-call(bf16[512,1024]{1,0:T(8,128)(2,1)S(1)} %copy-done.6, bf16[256,1024]{1,0:T(8,128)(2,1)S(1)} %collective-permute-done.10.refs_0_, bf16[256,1024]{1,0:T(8,128)(2,1)S(1)} %collective-permute-done.11.refs_1_, bf16[256,1024]{1,0:T(8,128)(2,1)S(1)} %collective-permute-done.12.refs_2_, ...), custom_call_target="tpu_custom_call" | custom-call | flops 268435456 | bytes 5242880 | tf_op jit(solution)/shard_map/add_received/pallas_call | solution.py:426
  87.7 0.0 copy-done.7
  87.7 8.7 %all-to-all-start.1 = ((bf16[32,16,1024]{2,1,0:T(8,128)(2,1)}), bf16[32,16,1024]{2,1,0:T(8,128)(2,1)S(1)}, u32[]{:S(2)}, u32[]{:S(2)}) async-start(bf16[32,16,1024]{2,1,0:T(8,128)(2,1)} %bitcast.6), calls=%async_computation.1 | async-start | bytes 2097152 | tf_op jit(solution)/shard_map/all_to_all | solution.py:66
  96.5 6.4 %attend_backward.2 = (bf16[512,2048]{1,0:T(8,128)(2,1)}, bf16[512,2048]{1,0:T(8,128)(2,1)}, bf16[512,2048]{1,0:T(8,128)(2,1)}) custom-call(s32[1]{0:T(128)} %bitcast.5.base, bf16[512,2048]{1,0:T(8,128)(2,1)} %q_ref.7, bf16[512,2048]{1,0:T(8,128)(2,1)} %k_ref.7, bf16[512,2048]{1,0:T(8,128)(2,1)} %v_ref.7, bf16[512,1024]{1,0:T(8,128)(2,1)S(1)} %copy-done.8, ...), custom_call_target="tpu_custom_call" | custom-call | flops 2147483648 | bytes 12582912 | tf_op jit(solution)/shard_map/attend_backward/pallas_call | solution.py:238
  102.9 12.7 %all-to-all-done.1.in_ref = bf16[32,16,1024]{2,1,0:T(8,128)(2,1)S(1)} async-done(((bf16[32,16,1024]{2,1,0:T(8,128)(2,1)}), bf16[32,16,1024]{2,1,0:T(8,128)(2,1)S(1)}, u32[]{:S(2)}, u32[]{:S(2)}) %all-to-all-start.1) | async-done | bytes 1048608 | tf_op jit(solution)/shard_map/all_to_all | solution.py:66
  115.6 0.8 own_rows.1
  116.4 0.0 collective-permute-done.9.g_ref
  116.4 1.2 copy-done.9
  117.6 6.5 %attend_backward.3 = (bf16[512,2048]{1,0:T(8,128)(2,1)}, bf16[512,2048]{1,0:T(8,128)(2,1)}, bf16[512,2048]{1,0:T(8,128)(2,1)}) custom-call(s32[1]{0:T(128)} %bitcast.base, bf16[512,2048]{1,0:T(8,128)(2,1)} %q_ref.7, bf16[512,2048]{1,0:T(8,128)(2,1)} %k_ref.7, bf16[512,2048]{1,0:T(8,128)(2,1)} %v_ref.7, ...), custom_call_target="tpu_custom_call", output_to_operand_aliasing={{0}: (7, {}), {1}: (8, {}), {2}: (9, {})} | custom-call | flops 2147483648 | bytes 12582912 | tf_op jit(solution)/shard_map/attend_backward/pallas_call | solution.py:238
  (20 shorter events, 0.0 us)
Async XLA Ops:
  0.6 30.5 %collective-permute-start = (bf16[512,2048]{1,0:T(8,128)(2,1)}, bf16[512,2048]{1,0:T(8,128)(2,1)}, u32[]{:S(2)}, u32[]{:S(2)}) collective-permute-start(bf16[512,2048]{1,0:T(8,128)(2,1)} %up_own_ref.3), channel_id=1, source_target_pairs={{0,1},{1,0},{2,3},{3,2},{4,5},{5,4},{6,7},{7,6},{8,9},{9,8},{10,11... | collective-permute-start | bytes 6291464 | tf_op jit(solution)/shard_map/ppermute | solution.py:470
  2.1 6.7 %copy-start.17 = (bf16[16,2048]{1,0:T(8,128)(2,1)S(1)}, bf16[16,2048]{1,0:T(8,128)(2,1)}, u32[]{:S(2)}) copy-start(bf16[16,2048]{1,0:T(8,128)(2,1)} %own_ref.1) | copy-start | bytes 196612
  8.6 15.8 %copy-start = (bf16[512,2048]{1,0:T(8,128)(2,1)S(1)}, bf16[512,2048]{1,0:T(8,128)(2,1)}, u32[]{:S(2)}) copy-start(bf16[512,2048]{1,0:T(8,128)(2,1)} %q_ref.7) | copy-start | bytes 6291460
  8.6 15.8 %copy-start.16 = (s32[1,512]{1,0:T(1,128)S(1)}, s32[1,512]{1,0:T(1,128)}, u32[]{:S(2)}) copy-start(s32[1,512]{1,0:T(1,128)} %ids_ref.3) | copy-start | bytes 6148
  8.6 22.5 %collective-permute-start.2 = (bf16[512,1024]{1,0:T(8,128)(2,1)}, bf16[512,1024]{1,0:T(8,128)(2,1)}, u32[]{:S(2)}, u32[]{:S(2)}) collective-permute-start(bf16[512,1024]{1,0:T(8,128)(2,1)} %get-tuple-element.27.att_ref), channel_id=1, source_target_pairs={{0,1},{1,0},{2,3},{3,2},{4,5},{5,4},{6,7},{7,6},{8,9},{9,8},{10,11... | collective-permute-start | bytes 3145736 | tf_op jit(solution)/shard_map/ppermute | solution.py:476
  8.7 3.0 %collective-permute-start.1 = (bf16[16,2048]{1,0:T(8,128)(2,1)S(1)}, bf16[16,2048]{1,0:T(8,128)(2,1)S(1)}, u32[]{:S(2)}, u32[]{:S(2)}) collective-permute-start(bf16[16,2048]{1,0:T(8,128)(2,1)S(1)} %copy-done.17), channel_id=1, source_target_pairs={{0,1},{1,0},{2,3},{3,2},{4,5},{5,4},{6,7},{7,6},{8,9},{9,8},{10,11... | collective-permute-start | bytes 196616 | tf_op jit(solution)/shard_map/ppermute | solution.py:471
  11.7 0.6 copy-start.18
  14.2 30.5 %all-to-all-start = ((bf16[16,32,1024]{2,1,0:T(8,128)(2,1)}), bf16[16,32,1024]{2,1,0:T(8,128)(2,1)S(1)}, u32[]{:S(2)}, u32[]{:S(2)}) async-start(bf16[16,32,1024]{2,1,0:T(8,128)(2,1)} %spread.1), calls=%async_computation | async-start | bytes 2097152 | tf_op jit(solution)/shard_map/all_to_all | solution.py:376
  24.5 6.6 %copy-start.1 = (bf16[512,2048]{1,0:T(8,128)(2,1)S(1)}, bf16[512,2048]{1,0:T(8,128)(2,1)}, u32[]{:S(2)}) copy-start(bf16[512,2048]{1,0:T(8,128)(2,1)} %up_own_ref.3) | copy-start | bytes 6291460
  31.1 44.5 %copy-start.2 = (bf16[512,2048]{1,0:T(8,128)(2,1)S(1)}, bf16[512,2048]{1,0:T(8,128)(2,1)}, u32[]{:S(2)}) copy-start(bf16[512,2048]{1,0:T(8,128)(2,1)} %up_own_ref.3) | copy-start | bytes 6291460
  37.9 1.0 copy-start.3
  38.9 1.0 copy-start.5
  39.9 0.8 copy-start.10
  40.7 0.8 copy-start.11
  41.5 0.8 copy-start.12
  42.3 0.8 copy-start.13
  43.1 0.8 copy-start.14
  43.9 0.8 copy-start.15
  44.7 14.5 %collective-permute-start.10 = (bf16[256,1024]{1,0:T(8,128)(2,1)}, bf16[256,1024]{1,0:T(8,128)(2,1)S(1)}, u32[]{:S(2)}, u32[]{:S(2)}) collective-permute-start(bf16[256,1024]{1,0:T(8,128)(2,1)} %copy-done.15), channel_id=1, source_target_pairs={{0,32},{1,33},{2,34},{3,35},{4,36},{5,37},{6,38},{7,39},{8,40},{9,... | collective-permute-start | bytes 1572872 | tf_op jit(solution)/shard_map/ppermute | solution.py:421
  45.1 14.5 %collective-permute-start.7 = (bf16[256,1024]{1,0:T(8,128)(2,1)S(1)}, bf16[256,1024]{1,0:T(8,128)(2,1)S(1)}, u32[]{:S(2)}, u32[]{:S(2)}) collective-permute-start(bf16[256,1024]{1,0:T(8,128)(2,1)S(1)} %get-tuple-element.30), channel_id=1, source_target_pairs={{0,24},{1,25},{2,26},{3,27},{4,28},{5,29},{6,30},{7,31},{8,16},{9,... | collective-permute-start | bytes 1572872 | tf_op jit(solution)/shard_map/ppermute | solution.py:403
  48.7 12.3 %collective-permute-start.5 = (bf16[256,1024]{1,0:T(8,128)(2,1)S(1)}, bf16[256,1024]{1,0:T(8,128)(2,1)S(1)}, u32[]{:S(2)}, u32[]{:S(2)}) collective-permute-start(bf16[256,1024]{1,0:T(8,128)(2,1)S(1)} %get-tuple-element.30), channel_id=1, source_target_pairs={{0,6},{1,7},{2,0},{3,1},{4,2},{5,3},{6,4},{7,5},{8,14},{9,15},{10,... | collective-permute-start | bytes 1572872 | tf_op jit(solution)/shard_map/ppermute | solution.py:403
  51.0 12.0 %collective-permute-start.3 = (bf16[256,1024]{1,0:T(8,128)(2,1)S(1)}, bf16[256,1024]{1,0:T(8,128)(2,1)S(1)}, u32[]{:S(2)}, u32[]{:S(2)}) collective-permute-start(bf16[256,1024]{1,0:T(8,128)(2,1)S(1)} %get-tuple-element.30), channel_id=1, source_target_pairs={{0,96},{1,97},{2,98},{3,99},{4,100},{5,101},{6,102},{7,103},{8,104... | collective-permute-start | bytes 1572872 | tf_op jit(solution)/shard_map/ppermute | solution.py:403
  52.5 12.9 %collective-permute-start.8 = (bf16[256,1024]{1,0:T(8,128)(2,1)S(1)}, bf16[256,1024]{1,0:T(8,128)(2,1)S(1)}, u32[]{:S(2)}, u32[]{:S(2)}) collective-permute-start(bf16[256,1024]{1,0:T(8,128)(2,1)S(1)} %get-tuple-element.31), channel_id=1, source_target_pairs={{0,16},{1,17},{2,18},{3,19},{4,20},{5,21},{6,22},{7,23},{8,24},{9,... | collective-permute-start | bytes 1572872 | tf_op jit(solution)/shard_map/ppermute | solution.py:403
  59.2 13.4 %collective-permute-start.6 = (bf16[256,1024]{1,0:T(8,128)(2,1)S(1)}, bf16[256,1024]{1,0:T(8,128)(2,1)S(1)}, u32[]{:S(2)}, u32[]{:S(2)}) collective-permute-start(bf16[256,1024]{1,0:T(8,128)(2,1)S(1)} %get-tuple-element.31), channel_id=1, source_target_pairs={{0,2},{1,3},{2,4},{3,5},{4,6},{5,7},{6,0},{7,1},{8,10},{9,11},{10,... | collective-permute-start | bytes 1572872 | tf_op jit(solution)/shard_map/ppermute | solution.py:403
  59.6 14.0 %collective-permute-start.4 = (bf16[256,1024]{1,0:T(8,128)(2,1)S(1)}, bf16[256,1024]{1,0:T(8,128)(2,1)S(1)}, u32[]{:S(2)}, u32[]{:S(2)}) collective-permute-start(bf16[256,1024]{1,0:T(8,128)(2,1)S(1)} %get-tuple-element.31), channel_id=1, source_target_pairs={{0,32},{1,33},{2,34},{3,35},{4,36},{5,37},{6,38},{7,39},{8,40},{9,... | collective-permute-start | bytes 1572872 | tf_op jit(solution)/shard_map/ppermute | solution.py:403
  61.0 20.9 %collective-permute-start.11 = (bf16[256,1024]{1,0:T(8,128)(2,1)}, bf16[256,1024]{1,0:T(8,128)(2,1)S(1)}, u32[]{:S(2)}, u32[]{:S(2)}) collective-permute-start(bf16[256,1024]{1,0:T(8,128)(2,1)} %copy-done.14), channel_id=1, source_target_pairs={{0,96},{1,97},{2,98},{3,99},{4,100},{5,101},{6,102},{7,103},{8,104... | collective-permute-start | bytes 1572872 | tf_op jit(solution)/shard_map/ppermute | solution.py:421
  63.0 23.2 %collective-permute-start.12 = (bf16[256,1024]{1,0:T(8,128)(2,1)}, bf16[256,1024]{1,0:T(8,128)(2,1)S(1)}, u32[]{:S(2)}, u32[]{:S(2)}) collective-permute-start(bf16[256,1024]{1,0:T(8,128)(2,1)} %copy-done.13), channel_id=1, source_target_pairs={{0,2},{1,3},{2,4},{3,5},{4,6},{5,7},{6,0},{7,1},{8,10},{9,11},{10,... | collective-permute-start | bytes 1572872 | tf_op jit(solution)/shard_map/ppermute | solution.py:421
  65.4 20.8 %collective-permute-start.13 = (bf16[256,1024]{1,0:T(8,128)(2,1)}, bf16[256,1024]{1,0:T(8,128)(2,1)S(1)}, u32[]{:S(2)}, u32[]{:S(2)}) collective-permute-start(bf16[256,1024]{1,0:T(8,128)(2,1)} %copy-done.12), channel_id=1, source_target_pairs={{0,6},{1,7},{2,0},{3,1},{4,2},{5,3},{6,4},{7,5},{8,14},{9,15},{10,... | collective-permute-start | bytes 1572872 | tf_op jit(solution)/shard_map/ppermute | solution.py:421
  72.6 13.6 %collective-permute-start.14 = (bf16[256,1024]{1,0:T(8,128)(2,1)}, bf16[256,1024]{1,0:T(8,128)(2,1)S(1)}, u32[]{:S(2)}, u32[]{:S(2)}) collective-permute-start(bf16[256,1024]{1,0:T(8,128)(2,1)} %copy-done.11), channel_id=1, source_target_pairs={{0,16},{1,17},{2,18},{3,19},{4,20},{5,21},{6,22},{7,23},{8,24},{9,... | collective-permute-start | bytes 1572872 | tf_op jit(solution)/shard_map/ppermute | solution.py:421
  73.5 12.7 %copy-start.6 = (bf16[512,1024]{1,0:T(8,128)(2,1)S(1)}, bf16[512,1024]{1,0:T(8,128)(2,1)}, u32[]{:S(2)}) copy-start(bf16[512,1024]{1,0:T(8,128)(2,1)} %copy-done.5) | copy-start | bytes 3145732
  73.5 12.7 %collective-permute-start.15 = (bf16[256,1024]{1,0:T(8,128)(2,1)}, bf16[256,1024]{1,0:T(8,128)(2,1)S(1)}, u32[]{:S(2)}, u32[]{:S(2)}) collective-permute-start(bf16[256,1024]{1,0:T(8,128)(2,1)} %copy-done.10), channel_id=1, source_target_pairs={{0,24},{1,25},{2,26},{3,27},{4,28},{5,29},{6,30},{7,31},{8,16},{9,... | collective-permute-start | bytes 1572872 | tf_op jit(solution)/shard_map/ppermute | solution.py:421
  81.9 5.8 %copy-start.7 = (bf16[512,1024]{1,0:T(8,128)(2,1)}, bf16[512,1024]{1,0:T(8,128)(2,1)S(1)}, u32[]{:S(2)}) copy-start(bf16[512,1024]{1,0:T(8,128)(2,1)S(1)} %get-tuple-element.34.g_ref) | copy-start | bytes 3145732
  82.0 34.4 %collective-permute-start.9 = (bf16[512,1024]{1,0:T(8,128)(2,1)}, bf16[512,1024]{1,0:T(8,128)(2,1)}, u32[]{:S(2)}, u32[]{:S(2)}) collective-permute-start(bf16[512,1024]{1,0:T(8,128)(2,1)} %get-tuple-element.32), channel_id=1, source_target_pairs={{0,1},{1,0},{2,3},{3,2},{4,5},{5,4},{6,7},{7,6},{8,9},{9,8},{10,11... | collective-permute-start | bytes 3145736 | tf_op jit(solution)/shard_map/ppermute | solution.py:485
  87.7 8.7 %copy-start.4 = (bf16[512,1024]{1,0:T(8,128)(2,1)S(1)}, bf16[512,1024]{1,0:T(8,128)(2,1)}, u32[]{:S(2)}) copy-start(bf16[512,1024]{1,0:T(8,128)(2,1)} %copy-done.3) | copy-start | bytes 3145732
  87.7 8.7 %copy-start.8 = (bf16[512,1024]{1,0:T(8,128)(2,1)S(1)}, bf16[512,1024]{1,0:T(8,128)(2,1)}, u32[]{:S(2)}) copy-start(bf16[512,1024]{1,0:T(8,128)(2,1)} %copy-done.7) | copy-start | bytes 3145732
  87.7 27.9 %all-to-all-start.1 = ((bf16[32,16,1024]{2,1,0:T(8,128)(2,1)}), bf16[32,16,1024]{2,1,0:T(8,128)(2,1)S(1)}, u32[]{:S(2)}, u32[]{:S(2)}) async-start(bf16[32,16,1024]{2,1,0:T(8,128)(2,1)} %bitcast.6), calls=%async_computation.1 | async-start | bytes 2097152 | tf_op jit(solution)/shard_map/all_to_all | solution.py:66
  116.4 1.2 copy-start.9

commit v3 on v2

--- a/solution.py
+++ b/solution.py
@@ -17,8 +17,8 @@
 LIMIT_A = 60
 LIMIT_BACK = 50
 LIMIT_LAST = 50
-LIMIT_SPREAD = 58
-LIMIT_WHOLE = 20
+LIMIT_PROJECT = 20
+LIMIT_SUMS = 20
 LIMIT_SMALL = 8
 FLOPS_4US = 2 << 30
 FLOPS_6US = 3 << 30
@@ -49,7 +49,6 @@
     for kx in range(2)
     for ky in range(2)
 ]
-CHIPS = [coset[core::2] for coset in COSETS for core in range(2)]
 CORE_SWAP = [(i, i ^ 1) for i in range(128)]
 
 
@@ -76,8 +75,22 @@
     return pltpu.CompilerParams(vmem_limit_bytes=mib * 1024 * 1024)
 
 
-def forward_kernel(base, q_ref, k_ref, v_ref, ids_ref, att_ref, prob_ref, bias_ref):
+BLOCK = 256
+PACKED = 3 * BLOCK
+
+
+def packed(i):
+    return slice(0, BLOCK) if i == 0 else slice(BLOCK, PACKED)
+
+
+def forward_kernel(base, q_ref, k_ref, v_ref, ids_ref, *refs):
+    att_ref, prob_ref, bias_ref = refs[-3 - len(refs) // 4 : -1 - len(refs) // 4] + refs[-1:]
     rows = q_ref.shape[0]
+    if len(refs) > 3:
+        weight_ref, pieces_ref = refs[0], refs[3]
+        cols = pieces_ref.shape[2]
+        for n in range(pieces_ref.shape[0]):
+            pieces_ref[n] = weight_ref[:, cols * (n % 2) : cols * (n % 2 + 1)]
 
     @pl.when(pl.program_id(0) == 0)
     def _():
@@ -87,7 +100,7 @@
         own = jnp.broadcast_to(ids, (DH, rows)).T[:, :1]
         bias_ref[...] = jnp.where(jnp.logical_and(u <= t, own == ids), 0.0, -1e30)
 
-    block = 256
+    block = BLOCK
 
     def cut(h, i):
         return slice(h * DH, (h + 1) * DH), i * block, (i + 1) * block
@@ -107,7 +120,7 @@
         raised = jnp.exp2(scores - jnp.max(scores, axis=1, keepdims=True))
         total = jnp.sum(raised, axis=1, keepdims=True)
         probs = (raised * (1.0 / total)).astype(BF)
-        prob_ref[h, lo:hi, :hi] = probs
+        prob_ref[h, :, packed(i)] = probs
         return probs
 
     def attend(h, i, probs):
@@ -130,37 +143,47 @@
     attend(*waiting)
 
 
-def attend_forward(base, queries, keys, values, ids, mib):
+def attend_forward(base, queries, keys, values, ids, mib, weight=None):
     rows = queries.shape[0]
+    steps = HALF // STEP_HEADS
+    extra, extra_in, extra_out, extra_shape = (), [], [], []
+    if weight is not None:
+        wide = (32, weight.shape[0], weight.shape[1] // 2)
+        extra = (weight,)
+        extra_in = [pl.BlockSpec(weight.shape, lambda i, b: (0, 0))]
+        extra_out = [pl.BlockSpec((wide[0] // steps, *wide[1:]), lambda i, b: (i, 0, 0))]
+        extra_shape = [jax.ShapeDtypeStruct(wide, BF)]
     head = pl.BlockSpec((rows, DH * STEP_HEADS), lambda i, b: (0, b[0] + i))
     return pl.pallas_call(
         forward_kernel,
         grid_spec=pltpu.PrefetchScalarGridSpec(
             num_scalar_prefetch=1,
-            grid=(HALF // STEP_HEADS,),
-            in_specs=[head, head, head, pl.BlockSpec((1, rows), lambda i, b: (0, 0))],
+            grid=(steps,),
+            in_specs=[head, head, head, pl.BlockSpec((1, rows), lambda i, b: (0, 0))] + extra_in,
             out_specs=[
                 pl.BlockSpec((rows, DH * STEP_HEADS), lambda i, b: (0, i)),
-                pl.BlockSpec((STEP_HEADS, rows, rows), lambda i, b: (i, 0, 0)),
-            ],
+                pl.BlockSpec((STEP_HEADS, BLOCK, PACKED), lambda i, b: (i, 0, 0)),
+            ]
+            + extra_out,
             scratch_shapes=[pltpu.VMEM((rows, rows), F32)],
         ),
         out_shape=[
             jax.ShapeDtypeStruct((rows, HALF * DH), BF),
-            jax.ShapeDtypeStruct((HALF, rows, rows), BF),
-        ],
+            jax.ShapeDtypeStruct((HALF, BLOCK, PACKED), BF),
+        ]
+        + extra_shape,
         compiler_params=grid_params(mib),
         cost_estimate=pl.CostEstimate(
             flops=FLOPS_6US, bytes_accessed=9 << 20, transcendentals=1 << 20
         ),
         name="attend_forward",
-    )(base, queries, keys, values, ids)
+    )(base, queries, keys, values, ids, *extra)
 
 
 def backward_kernel(base, q_ref, k_ref, v_ref, g_ref, att_ref, prob_ref, *refs):
     dq_ref, dk_ref, dv_ref = refs[-3:]
     rows = q_ref.shape[0]
-    block = 256
+    block = BLOCK
     count = rows // block
     inner, grad_t, query_t, sums = {}, {}, {}, {}
 
@@ -188,12 +211,12 @@
 
     def grad_scores_of(h, i, grad_probs):
         _, lo, hi = cut(h, i)
-        probs = prob_ref[h, lo:hi, :hi].astype(F32)
+        probs = prob_ref[h, :, packed(i)].astype(F32)
         return (probs * (grad_probs - inner[h][lo:hi, :])).astype(BF)
 
     def finish(h, i, grad_scores):
         cols, lo, hi = cut(h, i)
-        probs = prob_ref[h, lo:hi, :hi]
+        probs = prob_ref[h, :, packed(i)]
         dq_ref[lo:hi, cols] = (
             SCALE * jnp.dot(grad_scores, k_ref[:hi, cols], preferred_element_type=F32)
         ).astype(BF)
@@ -241,7 +264,7 @@
             num_scalar_prefetch=1,
             grid=(HALF // STEP_HEADS,),
             in_specs=[head, head, head, half, half]
-            + [pl.BlockSpec((STEP_HEADS, rows, rows), lambda i, b: (i, 0, 0))]
+            + [pl.BlockSpec((STEP_HEADS, BLOCK, PACKED), lambda i, b: (i, 0, 0))]
             + [pl.BlockSpec(memory_space=pl.ANY)] * len(previous),
             out_specs=[head, head, head],
         ),
@@ -286,6 +309,7 @@
 
 
 SMEM = pl.BlockSpec(memory_space=pltpu.SMEM)
+HBM = pl.BlockSpec(memory_space=pltpu.HBM)
 VMEM = pl.BlockSpec(memory_space=pltpu.VMEM)
 
 
@@ -298,7 +322,7 @@
         out_specs=[VMEM] * 2,
         out_shape=[jax.ShapeDtypeStruct((rows, cols), BF)] * 2,
         scratch_shapes=[pltpu.VMEM((width, cols), BF)],
-        compiler_params=whole_params(LIMIT_WHOLE),
+        compiler_params=whole_params(LIMIT_PROJECT),
         cost_estimate=pl.CostEstimate(
             flops=FLOPS_4US, bytes_accessed=10 << 20, transcendentals=0
         ),
@@ -307,7 +331,7 @@
 
 
 def weight_kernel(kx_ref, ky_ref, up_own_ref, up_other_ref, att_own_ref, att_other_ref, *refs):
-    outs, sums_ref = refs[:7], refs[7]
+    own_ref, outs, stages, (sums_ref, out_sem) = refs[0], refs[1:7], refs[7:13], refs[13:]
     width = up_own_ref.shape[1]
     place = (kx_ref[0], ky_ref[0])
     step, cut = 256, 512
@@ -329,10 +353,17 @@
             sums_ref[lo : lo + step, col : col + cut] = jnp.dot(
                 up_t, attended, preferred_element_type=F32
             ).astype(BF)
-    for ref, (other, lo, hi) in zip(outs, coset_parts()):
+    copies = []
+    for n, (other, lo, hi) in enumerate([*coset_parts()][1:] + [*coset_parts()][:1]):
+        stage = stages[n] if n < len(stages) else own_ref
         for block in range(lo, hi):
             row = pl.multiple_of(row_of(place, other, block), 16)
-            ref[16 * (block - lo) : 16 * (block - lo + 1), :] = sums_ref[pl.ds(row, 16), :]
+            stage[16 * (block - lo) : 16 * (block - lo + 1), :] = sums_ref[pl.ds(row, 16), :]
+        if n < len(stages):
+            copies.append(pltpu.make_async_copy(stage, outs[n], out_sem.at[n]))
+            copies[n].start()
+    for copy in copies:
+        copy.wait()
 
 
 def weight_sums(coset, up_own, up_other, att_own, att_other):
@@ -342,39 +373,16 @@
     return pl.pallas_call(
         weight_kernel,
         in_specs=[SMEM] * 2 + [VMEM] * 4,
-        out_specs=[VMEM] * len(sizes),
+        out_specs=[VMEM] + [HBM] * (len(sizes) - 1),
         out_shape=[jax.ShapeDtypeStruct((size, cols), BF) for size in sizes],
-        scratch_shapes=[pltpu.VMEM((width, cols), BF)],
-        compiler_params=whole_params(LIMIT_WHOLE),
+        scratch_shapes=[pltpu.VMEM((size, cols), BF) for size in sizes[1:]]
+        + [pltpu.VMEM((width, cols), BF), pltpu.SemaphoreType.DMA((len(sizes) - 1,))],
+        compiler_params=whole_params(LIMIT_SUMS),
         cost_estimate=pl.CostEstimate(
             flops=FLOPS_4US, bytes_accessed=10 << 20, transcendentals=0
         ),
         name="weight_sums",
     )(*coset, up_own, up_other, att_own, att_other)
-
-
-def spread_kernel(core_ref, own_ref, other_ref, out_ref):
-    core = core_ref[0]
-    rows, cols = own_ref.shape[0], out_ref.shape[2]
-    mine = pl.ds(pl.multiple_of(core * cols, DH), cols)
-    own, other = own_ref[:, mine], other_ref[:, mine]
-    for n in range(out_ref.shape[0]):
-        out_ref[n, pl.ds(pl.multiple_of(core * rows, rows), rows), :] = own
-        out_ref[n, pl.ds(pl.multiple_of((1 - core) * rows, rows), rows), :] = other
-
-
-def gather_weight(core, weight, other):
-    rows, cols = weight.shape[0], weight.shape[1] // 2
-    pieces = pl.pallas_call(
-        spread_kernel,
-        in_specs=[SMEM, VMEM, VMEM],
-        out_specs=VMEM,
-        out_shape=jax.ShapeDtypeStruct((16, 2 * rows, cols), BF),
-        compiler_params=whole_params(LIMIT_SPREAD),
-        name="spread",
-    )(core, weight, other)
-    block = lax.all_to_all(pieces, "d", 0, 0, axis_index_groups=CHIPS, tiled=True)
-    return block.reshape(32 * rows, cols)
 
 
 def split_kernel(block_ref, low_ref, high_ref):
@@ -468,11 +476,10 @@
     base_other = (steps * (1 - core)).astype(jnp.int32).reshape(1)
 
     up_other = lax.ppermute(upstream, "d", CORE_SWAP)
-    other = lax.ppermute(weight, "d", CORE_SWAP)
-    mine = gather_weight(core.astype(jnp.int32).reshape(1), weight, other)
-    att_a, prob_a = attend_forward(
-        base_other, queries, keys, values, sample_ids, LIMIT_A
+    att_a, prob_a, pieces = attend_forward(
+        base_other, queries, keys, values, sample_ids, LIMIT_A, weight
     )
+    mine = exchange(pieces).reshape(32 * weight.shape[0], -1)
     att_other = lax.ppermute(att_a, "d", CORE_SWAP)
     att_b, prob_b = attend_forward(base_own, queries, keys, values, sample_ids, LIMIT)
     sums = weight_sums(coset, upstream, up_other, att_b, att_other)
@@ -483,9 +490,7 @@
     rows_in = exchange(reduced.reshape(32, -1, reduced.shape[1]))
     grad_own, grad_sent = project(coset, upstream, up_other, gathered)
     grad_other = lax.ppermute(grad_sent, "d", CORE_SWAP)
-    outs = attend_backward(
-        base_own, queries, keys, values, grad_own, att_b, prob_b, (), LIMIT_BACK
-    )
+    outs = attend_backward(base_own, queries, keys, values, grad_own, att_b, prob_b, (), LIMIT_BACK)
     outs = attend_backward(
         base_other, queries, keys, values, grad_other, att_a, prob_a, tuple(outs), LIMIT_LAST
     )

time: 125 us -> 120 us (0.960)
  waiting for transfers between devices: 31.3 us -> 28 us
  Pallas kernels: 43.5 us -> 41.7 us
    all_to_all x1 -> x2, starting transfers between devices: 8.72 us -> 20.5 us  [exchange(): lax.all_to_all(pieces, 'd', 0, 0, axis_index_groups=COSETS, tiled=True)]
    all_to_all x1 -> x0, starting transfers between devices: 10.2 us -> none  [gather_weight(): lax.all_to_all(pieces, 'd', 0, 0, axis_index_groups=CHIPS, tiled=True)]
    ppermute x1 -> x0, waiting for transfers between devices: 2.49 us -> none  [shards(): other = lax.ppermute(weight, 'd', CORE_SWAP)]
    pallas_call x1 -> x0, Pallas kernels: 1.91 us -> none  [gather_weight(): pl.pallas_call(spread_kernel, in_specs=[SMEM, VMEM, VMEM], out_specs=VMEM...]
    all_to_all x1 -> x2, waiting for transfers between devices: 12.7 us -> 11.7 us  [exchange(): lax.all_to_all(pieces, 'd', 0, 0, axis_index_groups=COSETS, tiled=True)]
    unnamed x38 -> x34, local copies, waits for them, and re-layouts: 8.64 us -> 8.03 us
  transfers between devices with their start and end apart: 18 -> 17, of which waited for: 7 -> 6; matrix products, arithmetic and copies ran while one was open for 0% -> 0% of each run, Pallas kernels for 30% -> 30%
where the time goes in v3:
time: 120 us; the launch traced here: 119 us
  Pallas kernels  41.7 us (35%)
  starting transfers between devices  40.8 us (34%)
  waiting for transfers between devices  28 us (23%)
  local copies, waits for them, and re-layouts  8.03 us (7%)
    all_to_all x2, starting transfers between devices, exchange(): lax.all_to_all(pieces, 'd', 0, 0, axis_index_groups=COSETS, tiled=True)  20.5 us
    pallas_call x2, Pallas kernels, attend_forward(): pl.pallas_call(forward_kernel, grid_spec=pltpu.PrefetchScalarGridSpec(num...  13.1 us
    pallas_call x2, Pallas kernels, attend_backward(): pl.pallas_call(backward_kernel, grid_spec=pltpu.PrefetchScalarGridSpec(nu...  12.6 us
    all_to_all x2, waiting for transfers between devices, exchange(): lax.all_to_all(pieces, 'd', 0, 0, axis_index_groups=COSETS, tiled=True)  11.7 us
    ppermute x6, waiting for transfers between devices, gather_cosets(): result.append(lax.ppermute(parts[half], 'd', shift(axis, 2 * half - 1)))  9.48 us
    ppermute x6, starting transfers between devices, gather_cosets(): result.append(lax.ppermute(parts[half], 'd', shift(axis, 2 * half - 1)))  8.3 us
    unnamed x34, local copies, waits for them, and re-layouts  8.03 us
    pallas_call x1, Pallas kernels, weight_sums(): pl.pallas_call(weight_kernel, in_specs=[SMEM] * 2 + [VMEM] * 4, out_specs...  7.15 us
  transfers between devices with their start and end apart: 17, of which 6 were waited for; matrix products, arithmetic and copies ran while one was open for 0% of the time, Pallas kernels for 30%

profile of v3, /device:TPU:1, one launch (start us, length us, event | category | flops | bytes accessed | tf_op | source)
XLA Modules:
  0.0 119.3 jit_solution(14747592684446594709)
XLA Ops:
  0.6 1.5 %collective-permute-start = (bf16[512,2048]{1,0:T(8,128)(2,1)}, bf16[512,2048]{1,0:T(8,128)(2,1)}, u32[]{:S(2)}, u32[]{:S(2)}) collective-permute-start(bf16[512,2048]{1,0:T(8,128)(2,1)} %up_own_ref.3), channel_id=1, source_target_pairs={{0,1},{1,0},{2,3},{3,2},{4,5},{5,4},{6,7},{7,6},{8,9},{9,8},{10,11... | collective-permute-start | bytes 6291464 | tf_op jit(solution)/shard_map/ppermute | solution.py:478
  2.1 6.7 %attend_forward.2 = (bf16[512,1024]{1,0:T(8,128)(2,1)}, bf16[8,256,768]{2,1,0:T(8,128)(2,1)}, bf16[32,16,1024]{2,1,0:T(8,128)(2,1)}) custom-call(s32[1]{0:T(128)} %bitcast.base, bf16[512,2048]{1,0:T(8,128)(2,1)} %q_ref.7, bf16[512,2048]{1,0:T(8,128)(2,1)} %k_ref.7, bf16[512,2048]{1,0:T(8,128)(2,1)} %v_ref.7, s32[1,512]{1,0:T(1,128)} %ids_ref.3, ...), custom_call_target="tpu_custom_call" | custom-call | flops 3221225472 | bytes 9437184 | tf_op jit(solution)/shard_map/attend_forward/pallas_call | solution.py:157
  8.8 0.0 copy-start.16
  8.8 0.1 collective-permute-start.1
  9.0 11.1 %all-to-all-start = ((bf16[32,16,1024]{2,1,0:T(8,128)(2,1)}), bf16[32,16,1024]{2,1,0:T(8,128)(2,1)S(1)}, u32[]{:S(2)}, u32[]{:S(2)}) async-start(bf16[32,16,1024]{2,1,0:T(8,128)(2,1)} %get-tuple-element.27), calls=%async_computation | async-start | bytes 2097152 | tf_op jit(solution)/shard_map/all_to_all | solution.py:65
  20.1 0.0 copy-done
  20.1 0.0 copy-done.16
  20.1 0.0 copy-start.1
  20.1 6.4 %attend_forward.3 = (bf16[512,1024]{1,0:T(8,128)(2,1)S(1)}, bf16[8,256,768]{2,1,0:T(8,128)(2,1)}) custom-call(s32[1]{0:T(128)} %bitcast.4.base, bf16[512,2048]{1,0:T(8,128)(2,1)S(1)} %copy-done, bf16[512,2048]{1,0:T(8,128)(2,1)} %k_ref.7, bf16[512,2048]{1,0:T(8,128)(2,1)} %v_ref.7, s32[1,512]{1,0:T(1,128)S(1)} %copy-done.16), custom_call_target="tpu_custom_call" | custom-call | flops 3221225472 | bytes 9437184 | tf_op jit(solution)/shard_map/attend_forward/pallas_call | solution.py:157
  26.5 0.0 collective-permute-done.1.att_other_ref
  26.5 0.0 collective-permute-done.up_other_ref
  26.5 0.0 copy-done.1
  26.5 0.0 copy-start.2
  26.5 7.2 %weight_sums.1 = (bf16[512,1024]{1,0:T(8,128)(2,1)S(1)}, bf16[256,1024]{1,0:T(8,128)(2,1)S(1)}, bf16[256,1024]{1,0:T(8,128)(2,1)S(1)}, bf16[256,1024]{1,0:T(8,12...) custom-call(s32[1]{0:T(128)} %bitcast.1.kx_ref, ...), custom_call_target="tpu_custom_call" | custom-call | flops 2147483648 | bytes 10485760 | tf_op jit(solution)/shard_map/weight_sums/pallas_call | solution.py:373
  33.7 0.0 copy-start.4
  33.7 1.0 copy-done.4
  34.7 1.0 copy-done.6
  35.6 0.8 copy-done.10
  36.4 0.8 copy-done.11
  37.2 0.8 copy-done.12
  38.0 0.8 copy-done.13
  38.9 0.8 copy-done.14
  39.7 0.8 copy-done.15
  40.5 0.0 all-to-all-done
  40.5 0.3 collective-permute-start.9
  40.8 0.1 split.1
  40.9 3.7 %collective-permute-start.6 = (bf16[256,1024]{1,0:T(8,128)(2,1)S(1)}, bf16[256,1024]{1,0:T(8,128)(2,1)S(1)}, u32[]{:S(2)}, u32[]{:S(2)}) collective-permute-start(bf16[256,1024]{1,0:T(8,128)(2,1)S(1)} %get-tuple-element.32), channel_id=1, source_target_pairs={{0,24},{1,25},{2,26},{3,27},{4,28},{5,29},{6,30},{7,31},{8,16},{9,... | collective-permute-start | bytes 1572872 | tf_op jit(solution)/shard_map/ppermute | solution.py:411
  44.5 2.3 %collective-permute-start.4 = (bf16[256,1024]{1,0:T(8,128)(2,1)S(1)}, bf16[256,1024]{1,0:T(8,128)(2,1)S(1)}, u32[]{:S(2)}, u32[]{:S(2)}) collective-permute-start(bf16[256,1024]{1,0:T(8,128)(2,1)S(1)} %get-tuple-element.32), channel_id=1, source_target_pairs={{0,6},{1,7},{2,0},{3,1},{4,2},{5,3},{6,4},{7,5},{8,14},{9,15},{10,... | collective-permute-start | bytes 1572872 | tf_op jit(solution)/shard_map/ppermute | solution.py:411
  46.8 1.5 %collective-permute-start.2 = (bf16[256,1024]{1,0:T(8,128)(2,1)S(1)}, bf16[256,1024]{1,0:T(8,128)(2,1)S(1)}, u32[]{:S(2)}, u32[]{:S(2)}) collective-permute-start(bf16[256,1024]{1,0:T(8,128)(2,1)S(1)} %get-tuple-element.32), channel_id=1, source_target_pairs={{0,96},{1,97},{2,98},{3,99},{4,100},{5,101},{6,102},{7,103},{8,104... | collective-permute-start | bytes 1572872 | tf_op jit(solution)/shard_map/ppermute | solution.py:411
  48.4 0.0 collective-permute-start.7
  48.4 6.8 %collective-permute-done.9.refs_0_ = bf16[256,1024]{1,0:T(8,128)(2,1)S(1)} collective-permute-done((bf16[256,1024]{1,0:T(8,128)(2,1)}, bf16[256,1024]{1,0:T(8,128)(2,1)S(1)}, u32[]{:S(2)}, u32[]{:S(2)}) %collective-permute-start.9) | collective-permute-done | bytes 524320 | tf_op jit(solution)/shard_map/ppermute | solution.py:429
  55.2 0.4 collective-permute-start.5
  55.6 0.0 collective-permute-done.6.refs_5_
  55.6 0.4 collective-permute-start.3
  56.0 1.2 collective-permute-done.4.refs_3_
  57.2 1.5 %collective-permute-start.10 = (bf16[256,1024]{1,0:T(8,128)(2,1)}, bf16[256,1024]{1,0:T(8,128)(2,1)S(1)}, u32[]{:S(2)}, u32[]{:S(2)}) collective-permute-start(bf16[256,1024]{1,0:T(8,128)(2,1)} %copy-done.14), channel_id=1, source_target_pairs={{0,96},{1,97},{2,98},{3,99},{4,100},{5,101},{6,102},{7,103},{8,104... | collective-permute-start | bytes 1572872 | tf_op jit(solution)/shard_map/ppermute | solution.py:429
  58.7 0.4 collective-permute-done.2.refs_1_
  59.1 1.1 collective-permute-start.11
  60.2 1.3 %collective-permute-done.7.refs_6_ = bf16[256,1024]{1,0:T(8,128)(2,1)S(1)} collective-permute-done((bf16[256,1024]{1,0:T(8,128)(2,1)S(1)}, bf16[256,1024]{1,0:T(8,128)(2,1)S(1)}, u32[]{:S(2)}, u32[]{:S(2)}) %collective-permute-start.7) | collective-permute-done | bytes 524320 | tf_op jit(solution)/shard_map/ppermute | solution.py:411
  61.5 0.6 collective-permute-start.12
  62.2 6.6 %collective-permute-done.5.refs_4_ = bf16[256,1024]{1,0:T(8,128)(2,1)S(1)} collective-permute-done((bf16[256,1024]{1,0:T(8,128)(2,1)S(1)}, bf16[256,1024]{1,0:T(8,128)(2,1)S(1)}, u32[]{:S(2)}, u32[]{:S(2)}) %collective-permute-start.5) | collective-permute-done | bytes 524320 | tf_op jit(solution)/shard_map/ppermute | solution.py:411
  68.8 1.2 collective-permute-start.13
  69.9 0.0 collective-permute-done.3.refs_2_
  69.9 2.1 %collective-permute-start.14 = (bf16[256,1024]{1,0:T(8,128)(2,1)}, bf16[256,1024]{1,0:T(8,128)(2,1)S(1)}, u32[]{:S(2)}, u32[]{:S(2)}) collective-permute-start(bf16[256,1024]{1,0:T(8,128)(2,1)} %copy-done.10), channel_id=1, source_target_pairs={{0,24},{1,25},{2,26},{3,27},{4,28},{5,29},{6,30},{7,31},{8,16},{9,... | collective-permute-start | bytes 1572872 | tf_op jit(solution)/shard_map/ppermute | solution.py:429
  72.0 0.0 copy-done.2
  72.0 6.4 %project.1 = (bf16[512,1024]{1,0:T(8,128)(2,1)S(1)}, bf16[512,1024]{1,0:T(8,128)(2,1)}) custom-call(s32[1]{0:T(128)} %bitcast.1.kx_ref, s32[1]{0:T(128)} %bitcast.2.ky_ref, bf16[512,2048]{1,0:T(8,128)(2,1)S(1)} %copy-done.2, bf16[512,2048]{1,0:T(8,128)(2,1)} %collective-permute-done.up_other_ref, bf16[512,1024]{1,0:T(8,128)(2,1)S(1)} %bitcast.7, ...), custom_call_target="tpu_custom_call" | custom-call | flops 2147483648 | bytes 10485760 | tf_op jit(solution)/shard_map/project/pallas_call | solution.py:319
  78.4 0.0 copy-start.8
  78.4 0.0 collective-permute-done.10.refs_1_
  78.4 3.6 %collective-permute-start.8 = (bf16[512,1024]{1,0:T(8,128)(2,1)}, bf16[512,1024]{1,0:T(8,128)(2,1)}, u32[]{:S(2)}, u32[]{:S(2)}) collective-permute-start(bf16[512,1024]{1,0:T(8,128)(2,1)} %get-tuple-element.34), channel_id=1, source_target_pairs={{0,1},{1,0},{2,3},{3,2},{4,5},{5,4},{6,7},{7,6},{8,9},{9,8},{10,11... | collective-permute-start | bytes 3145736 | tf_op jit(solution)/shard_map/ppermute | solution.py:492
  82.0 0.0 collective-permute-done.11.refs_2_
  82.0 0.0 collective-permute-done.12.refs_3_
  82.0 0.0 collective-permute-done.13.refs_4_
  82.0 0.0 collective-permute-done.14.refs_5_
  82.0 0.0 copy-done.7
  82.0 1.6 %add_received.1 = bf16[512,1024]{1,0:T(8,128)(2,1)} custom-call(bf16[512,1024]{1,0:T(8,128)(2,1)S(1)} %copy-done.7, bf16[256,1024]{1,0:T(8,128)(2,1)S(1)} %collective-permute-done.9.refs_0_, bf16[256,1024]{1,0:T(8,128)(2,1)S(1)} %collective-permute-done.10.refs_1_, bf16[256,1024]{1,0:T(8,128)(2,1)S(1)} %collective-permute-done.11.refs_2_, ...), custom_call_target="tpu_custom_call" | custom-call | flops 268435456 | bytes 5242880 | tf_op jit(solution)/shard_map/add_received/pallas_call | solution.py:434
  83.6 9.4 %all-to-all-start.1 = ((bf16[32,16,1024]{2,1,0:T(8,128)(2,1)}), bf16[32,16,1024]{2,1,0:T(8,128)(2,1)S(1)}, u32[]{:S(2)}, u32[]{:S(2)}) async-start(bf16[32,16,1024]{2,1,0:T(8,128)(2,1)} %bitcast.5), calls=%async_computation.1 | async-start | bytes 2097152 | tf_op jit(solution)/shard_map/all_to_all | solution.py:65
  93.0 0.0 copy-done.5
  93.0 0.0 copy-start.9
  93.0 1.2 %copy-done.9 = bf16[512,1024]{1,0:T(8,128)(2,1)S(1)} copy-done((bf16[512,1024]{1,0:T(8,128)(2,1)S(1)}, bf16[512,1024]{1,0:T(8,128)(2,1)}, u32[]{:S(2)}) %copy-start.9) | copy-done | bytes 1048600
  94.2 6.2 %attend_backward.2 = (bf16[512,2048]{1,0:T(8,128)(2,1)}, bf16[512,2048]{1,0:T(8,128)(2,1)}, bf16[512,2048]{1,0:T(8,128)(2,1)}) custom-call(s32[1]{0:T(128)} %bitcast.4.base, bf16[512,2048]{1,0:T(8,128)(2,1)} %q_ref.7, bf16[512,2048]{1,0:T(8,128)(2,1)} %k_ref.7, bf16[512,2048]{1,0:T(8,128)(2,1)} %v_ref.7, bf16[512,1024]{1,0:T(8,128)(2,1)S(1)} %copy-done.9, ...), custom_call_target="tpu_custom_call" | custom-call | flops 2147483648 | bytes 12582912 | tf_op jit(solution)/shard_map/attend_backward/pallas_call | solution.py:261
  100.5 11.7 %all-to-all-done.1.in_ref = bf16[32,16,1024]{2,1,0:T(8,128)(2,1)S(1)} async-done(((bf16[32,16,1024]{2,1,0:T(8,128)(2,1)}), bf16[32,16,1024]{2,1,0:T(8,128)(2,1)S(1)}, u32[]{:S(2)}, u32[]{:S(2)}) %all-to-all-start.1) | async-done | bytes 1048608 | tf_op jit(solution)/shard_map/all_to_all | solution.py:65
  112.1 0.8 own_rows.1
  112.9 0.0 collective-permute-done.8.g_ref
  112.9 6.3 %attend_backward.3 = (bf16[512,2048]{1,0:T(8,128)(2,1)}, bf16[512,2048]{1,0:T(8,128)(2,1)}, bf16[512,2048]{1,0:T(8,128)(2,1)}) custom-call(s32[1]{0:T(128)} %bitcast.base, bf16[512,2048]{1,0:T(8,128)(2,1)} %q_ref.7, bf16[512,2048]{1,0:T(8,128)(2,1)} %k_ref.7, bf16[512,2048]{1,0:T(8,128)(2,1)} %v_ref.7, ...), custom_call_target="tpu_custom_call", output_to_operand_aliasing={{0}: (7, {}), {1}: (8, {}), {2}: (9, {})} | custom-call | flops 2147483648 | bytes 12582912 | tf_op jit(solution)/shard_map/attend_backward/pallas_call | solution.py:261
  (13 shorter events, 0.0 us)
Async XLA Ops:
  0.6 25.9 %collective-permute-start = (bf16[512,2048]{1,0:T(8,128)(2,1)}, bf16[512,2048]{1,0:T(8,128)(2,1)}, u32[]{:S(2)}, u32[]{:S(2)}) collective-permute-start(bf16[512,2048]{1,0:T(8,128)(2,1)} %up_own_ref.3), channel_id=1, source_target_pairs={{0,1},{1,0},{2,3},{3,2},{4,5},{5,4},{6,7},{7,6},{8,9},{9,8},{10,11... | collective-permute-start | bytes 6291464 | tf_op jit(solution)/shard_map/ppermute | solution.py:478
  8.8 11.3 %copy-start = (bf16[512,2048]{1,0:T(8,128)(2,1)S(1)}, bf16[512,2048]{1,0:T(8,128)(2,1)}, u32[]{:S(2)}) copy-start(bf16[512,2048]{1,0:T(8,128)(2,1)} %q_ref.7) | copy-start | bytes 6291460
  8.8 11.3 %copy-start.16 = (s32[1,512]{1,0:T(1,128)S(1)}, s32[1,512]{1,0:T(1,128)}, u32[]{:S(2)}) copy-start(s32[1,512]{1,0:T(1,128)} %ids_ref.3) | copy-start | bytes 6148
  8.8 17.7 %collective-permute-start.1 = (bf16[512,1024]{1,0:T(8,128)(2,1)}, bf16[512,1024]{1,0:T(8,128)(2,1)}, u32[]{:S(2)}, u32[]{:S(2)}) collective-permute-start(bf16[512,1024]{1,0:T(8,128)(2,1)} %get-tuple-element.29.att_ref), channel_id=1, source_target_pairs={{0,1},{1,0},{2,3},{3,2},{4,5},{5,4},{6,7},{7,6},{8,9},{9,8},{10,11... | collective-permute-start | bytes 3145736 | tf_op jit(solution)/shard_map/ppermute | solution.py:483
  9.0 31.5 %all-to-all-start = ((bf16[32,16,1024]{2,1,0:T(8,128)(2,1)}), bf16[32,16,1024]{2,1,0:T(8,128)(2,1)S(1)}, u32[]{:S(2)}, u32[]{:S(2)}) async-start(bf16[32,16,1024]{2,1,0:T(8,128)(2,1)} %get-tuple-element.27), calls=%async_computation | async-start | bytes 2097152 | tf_op jit(solution)/shard_map/all_to_all | solution.py:65
  20.1 6.4 %copy-start.1 = (bf16[512,2048]{1,0:T(8,128)(2,1)S(1)}, bf16[512,2048]{1,0:T(8,128)(2,1)}, u32[]{:S(2)}) copy-start(bf16[512,2048]{1,0:T(8,128)(2,1)} %up_own_ref.3) | copy-start | bytes 6291460
  26.5 45.5 %copy-start.2 = (bf16[512,2048]{1,0:T(8,128)(2,1)S(1)}, bf16[512,2048]{1,0:T(8,128)(2,1)}, u32[]{:S(2)}) copy-start(bf16[512,2048]{1,0:T(8,128)(2,1)} %up_own_ref.3) | copy-start | bytes 6291460
  33.7 1.0 copy-start.4
  34.7 1.0 copy-start.6
  35.6 0.8 copy-start.10
  36.4 0.8 copy-start.11
  37.2 0.8 copy-start.12
  38.0 0.8 copy-start.13
  38.9 0.8 copy-start.14
  39.7 0.8 copy-start.15
  40.5 14.7 %collective-permute-start.9 = (bf16[256,1024]{1,0:T(8,128)(2,1)}, bf16[256,1024]{1,0:T(8,128)(2,1)S(1)}, u32[]{:S(2)}, u32[]{:S(2)}) collective-permute-start(bf16[256,1024]{1,0:T(8,128)(2,1)} %copy-done.15), channel_id=1, source_target_pairs={{0,32},{1,33},{2,34},{3,35},{4,36},{5,37},{6,38},{7,39},{8,40},{9,... | collective-permute-start | bytes 1572872 | tf_op jit(solution)/shard_map/ppermute | solution.py:429
  40.9 14.7 %collective-permute-start.6 = (bf16[256,1024]{1,0:T(8,128)(2,1)S(1)}, bf16[256,1024]{1,0:T(8,128)(2,1)S(1)}, u32[]{:S(2)}, u32[]{:S(2)}) collective-permute-start(bf16[256,1024]{1,0:T(8,128)(2,1)S(1)} %get-tuple-element.32), channel_id=1, source_target_pairs={{0,24},{1,25},{2,26},{3,27},{4,28},{5,29},{6,30},{7,31},{8,16},{9,... | collective-permute-start | bytes 1572872 | tf_op jit(solution)/shard_map/ppermute | solution.py:411
  44.5 12.6 %collective-permute-start.4 = (bf16[256,1024]{1,0:T(8,128)(2,1)S(1)}, bf16[256,1024]{1,0:T(8,128)(2,1)S(1)}, u32[]{:S(2)}, u32[]{:S(2)}) collective-permute-start(bf16[256,1024]{1,0:T(8,128)(2,1)S(1)} %get-tuple-element.32), channel_id=1, source_target_pairs={{0,6},{1,7},{2,0},{3,1},{4,2},{5,3},{6,4},{7,5},{8,14},{9,15},{10,... | collective-permute-start | bytes 1572872 | tf_op jit(solution)/shard_map/ppermute | solution.py:411
  46.8 12.3 %collective-permute-start.2 = (bf16[256,1024]{1,0:T(8,128)(2,1)S(1)}, bf16[256,1024]{1,0:T(8,128)(2,1)S(1)}, u32[]{:S(2)}, u32[]{:S(2)}) collective-permute-start(bf16[256,1024]{1,0:T(8,128)(2,1)S(1)} %get-tuple-element.32), channel_id=1, source_target_pairs={{0,96},{1,97},{2,98},{3,99},{4,100},{5,101},{6,102},{7,103},{8,104... | collective-permute-start | bytes 1572872 | tf_op jit(solution)/shard_map/ppermute | solution.py:411
  48.4 13.2 %collective-permute-start.7 = (bf16[256,1024]{1,0:T(8,128)(2,1)S(1)}, bf16[256,1024]{1,0:T(8,128)(2,1)S(1)}, u32[]{:S(2)}, u32[]{:S(2)}) collective-permute-start(bf16[256,1024]{1,0:T(8,128)(2,1)S(1)} %get-tuple-element.33), channel_id=1, source_target_pairs={{0,16},{1,17},{2,18},{3,19},{4,20},{5,21},{6,22},{7,23},{8,24},{9,... | collective-permute-start | bytes 1572872 | tf_op jit(solution)/shard_map/ppermute | solution.py:411
  55.2 13.6 %collective-permute-start.5 = (bf16[256,1024]{1,0:T(8,128)(2,1)S(1)}, bf16[256,1024]{1,0:T(8,128)(2,1)S(1)}, u32[]{:S(2)}, u32[]{:S(2)}) collective-permute-start(bf16[256,1024]{1,0:T(8,128)(2,1)S(1)} %get-tuple-element.33), channel_id=1, source_target_pairs={{0,2},{1,3},{2,4},{3,5},{4,6},{5,7},{6,0},{7,1},{8,10},{9,11},{10,... | collective-permute-start | bytes 1572872 | tf_op jit(solution)/shard_map/ppermute | solution.py:411
  55.6 14.4 %collective-permute-start.3 = (bf16[256,1024]{1,0:T(8,128)(2,1)S(1)}, bf16[256,1024]{1,0:T(8,128)(2,1)S(1)}, u32[]{:S(2)}, u32[]{:S(2)}) collective-permute-start(bf16[256,1024]{1,0:T(8,128)(2,1)S(1)} %get-tuple-element.33), channel_id=1, source_target_pairs={{0,32},{1,33},{2,34},{3,35},{4,36},{5,37},{6,38},{7,39},{8,40},{9,... | collective-permute-start | bytes 1572872 | tf_op jit(solution)/shard_map/ppermute | solution.py:411
  57.2 21.2 %collective-permute-start.10 = (bf16[256,1024]{1,0:T(8,128)(2,1)}, bf16[256,1024]{1,0:T(8,128)(2,1)S(1)}, u32[]{:S(2)}, u32[]{:S(2)}) collective-permute-start(bf16[256,1024]{1,0:T(8,128)(2,1)} %copy-done.14), channel_id=1, source_target_pairs={{0,96},{1,97},{2,98},{3,99},{4,100},{5,101},{6,102},{7,103},{8,104... | collective-permute-start | bytes 1572872 | tf_op jit(solution)/shard_map/ppermute | solution.py:429
  59.1 22.9 %collective-permute-start.11 = (bf16[256,1024]{1,0:T(8,128)(2,1)}, bf16[256,1024]{1,0:T(8,128)(2,1)S(1)}, u32[]{:S(2)}, u32[]{:S(2)}) collective-permute-start(bf16[256,1024]{1,0:T(8,128)(2,1)} %copy-done.13), channel_id=1, source_target_pairs={{0,2},{1,3},{2,4},{3,5},{4,6},{5,7},{6,0},{7,1},{8,10},{9,11},{10,... | collective-permute-start | bytes 1572872 | tf_op jit(solution)/shard_map/ppermute | solution.py:429
  61.5 20.4 %collective-permute-start.12 = (bf16[256,1024]{1,0:T(8,128)(2,1)}, bf16[256,1024]{1,0:T(8,128)(2,1)S(1)}, u32[]{:S(2)}, u32[]{:S(2)}) collective-permute-start(bf16[256,1024]{1,0:T(8,128)(2,1)} %copy-done.12), channel_id=1, source_target_pairs={{0,6},{1,7},{2,0},{3,1},{4,2},{5,3},{6,4},{7,5},{8,14},{9,15},{10,... | collective-permute-start | bytes 1572872 | tf_op jit(solution)/shard_map/ppermute | solution.py:429
  68.8 13.2 %collective-permute-start.13 = (bf16[256,1024]{1,0:T(8,128)(2,1)}, bf16[256,1024]{1,0:T(8,128)(2,1)S(1)}, u32[]{:S(2)}, u32[]{:S(2)}) collective-permute-start(bf16[256,1024]{1,0:T(8,128)(2,1)} %copy-done.11), channel_id=1, source_target_pairs={{0,16},{1,17},{2,18},{3,19},{4,20},{5,21},{6,22},{7,23},{8,24},{9,... | collective-permute-start | bytes 1572872 | tf_op jit(solution)/shard_map/ppermute | solution.py:429
  69.9 12.1 %copy-start.7 = (bf16[512,1024]{1,0:T(8,128)(2,1)S(1)}, bf16[512,1024]{1,0:T(8,128)(2,1)}, u32[]{:S(2)}) copy-start(bf16[512,1024]{1,0:T(8,128)(2,1)} %copy-done.6) | copy-start | bytes 3145732
  69.9 12.0 %collective-permute-start.14 = (bf16[256,1024]{1,0:T(8,128)(2,1)}, bf16[256,1024]{1,0:T(8,128)(2,1)S(1)}, u32[]{:S(2)}, u32[]{:S(2)}) collective-permute-start(bf16[256,1024]{1,0:T(8,128)(2,1)} %copy-done.10), channel_id=1, source_target_pairs={{0,24},{1,25},{2,26},{3,27},{4,28},{5,29},{6,30},{7,31},{8,16},{9,... | collective-permute-start | bytes 1572872 | tf_op jit(solution)/shard_map/ppermute | solution.py:429
  78.4 5.2 %copy-start.8 = (bf16[512,1024]{1,0:T(8,128)(2,1)}, bf16[512,1024]{1,0:T(8,128)(2,1)S(1)}, u32[]{:S(2)}) copy-start(bf16[512,1024]{1,0:T(8,128)(2,1)S(1)} %get-tuple-element.36.g_ref) | copy-start | bytes 3145732
  78.4 34.5 %collective-permute-start.8 = (bf16[512,1024]{1,0:T(8,128)(2,1)}, bf16[512,1024]{1,0:T(8,128)(2,1)}, u32[]{:S(2)}, u32[]{:S(2)}) collective-permute-start(bf16[512,1024]{1,0:T(8,128)(2,1)} %get-tuple-element.34), channel_id=1, source_target_pairs={{0,1},{1,0},{2,3},{3,2},{4,5},{5,4},{6,7},{7,6},{8,9},{9,8},{10,11... | collective-permute-start | bytes 3145736 | tf_op jit(solution)/shard_map/ppermute | solution.py:492
  83.6 9.4 %copy-start.5 = (bf16[512,1024]{1,0:T(8,128)(2,1)S(1)}, bf16[512,1024]{1,0:T(8,128)(2,1)}, u32[]{:S(2)}) copy-start(bf16[512,1024]{1,0:T(8,128)(2,1)} %copy-done.4) | copy-start | bytes 3145732
  83.6 28.5 %all-to-all-start.1 = ((bf16[32,16,1024]{2,1,0:T(8,128)(2,1)}), bf16[32,16,1024]{2,1,0:T(8,128)(2,1)S(1)}, u32[]{:S(2)}, u32[]{:S(2)}) async-start(bf16[32,16,1024]{2,1,0:T(8,128)(2,1)} %bitcast.5), calls=%async_computation.1 | async-start | bytes 2097152 | tf_op jit(solution)/shard_map/all_to_all | solution.py:65
  93.0 1.2 %copy-start.9 = (bf16[512,1024]{1,0:T(8,128)(2,1)S(1)}, bf16[512,1024]{1,0:T(8,128)(2,1)}, u32[]{:S(2)}) copy-start(bf16[512,1024]{1,0:T(8,128)(2,1)} %copy-done.8) | copy-start | bytes 3145732
  94.2 18.7 %copy-start.3 = (bf16[512,1024]{1,0:T(8,128)(2,1)S(1)}, bf16[512,1024]{1,0:T(8,128)(2,1)}, u32[]{:S(2)}) copy-start(bf16[512,1024]{1,0:T(8,128)(2,1)} %get-tuple-element.29.att_ref) | copy-start | bytes 3145732

commit v4 on v3

--- a/solution.py
+++ b/solution.py
@@ -15,9 +15,10 @@
 STEP_HEADS = 4
 LIMIT = 50
 LIMIT_A = 60
-LIMIT_BACK = 50
+LIMIT_BACK = 60
 LIMIT_LAST = 50
-LIMIT_PROJECT = 20
+LIMIT_PROJECT = 50
+LIMIT_ADD = 8
 LIMIT_SUMS = 20
 LIMIT_SMALL = 8
 FLOPS_4US = 2 << 30
@@ -293,8 +294,10 @@
         yield other, 16, 32
 
 
-def project_kernel(kx_ref, ky_ref, up_own_ref, up_other_ref, *refs):
-    pieces, (own_ref, other_ref, weight_ref) = refs[:7], refs[7:]
+def project_kernel(kx_ref, ky_ref, up_own_hbm, up_other_ref, *refs):
+    pieces, (own_ref, other_ref, weight_ref, up_own_ref, sem) = refs[:7], refs[7:]
+    load = pltpu.make_async_copy(up_own_hbm, up_own_ref, sem)
+    load.start()
     place = (kx_ref[0], ky_ref[0])
     for ref, (other, lo, hi) in zip(pieces, coset_parts()):
         for block in range(lo, hi):
@@ -302,6 +305,8 @@
             weight_ref[pl.ds(row, 16), :] = ref[16 * (block - lo) : 16 * (block - lo + 1), :]
     step = 512
     for up_ref, out_ref in ((up_other_ref, other_ref), (up_own_ref, own_ref)):
+        if up_ref is up_own_ref:
+            load.wait()
         for lo in range(0, out_ref.shape[1], step):
             out_ref[:, lo : lo + step] = jnp.dot(
                 up_ref[...], weight_ref[:, lo : lo + step], preferred_element_type=F32
@@ -318,10 +323,14 @@
     cols = pieces[0].shape[1]
     return pl.pallas_call(
         project_kernel,
-        in_specs=[SMEM] * 2 + [VMEM] * (2 + len(pieces)),
+        in_specs=[SMEM, SMEM, HBM] + [VMEM] * (1 + len(pieces)),
         out_specs=[VMEM] * 2,
         out_shape=[jax.ShapeDtypeStruct((rows, cols), BF)] * 2,
-        scratch_shapes=[pltpu.VMEM((width, cols), BF)],
+        scratch_shapes=[
+            pltpu.VMEM((width, cols), BF),
+            pltpu.VMEM((rows, width), BF),
+            pltpu.SemaphoreType.DMA,
+        ],
         compiler_params=whole_params(LIMIT_PROJECT),
         cost_estimate=pl.CostEstimate(
             flops=FLOPS_4US, bytes_accessed=10 << 20, transcendentals=0
@@ -412,15 +421,22 @@
     return result
 
 
+ADD_STEPS = 4
+
+
 def add_kernel(own_ref, *refs):
     received, out_ref = refs[:6], refs[6]
-    rows = received[0].shape[0]
+
+    def add(half):
+        for lo in range(0, out_ref.shape[0], 16):
+            rows = slice(lo, lo + 16)
+            total = own_ref[rows, :].astype(F32)
+            for axis in range(3):
+                total = total + received[2 * axis + half][rows, :].astype(F32)
+            out_ref[rows, :] = total.astype(BF)
+
     for half in range(2):
-        for lo in range(0, rows, 16):
-            total = own_ref[rows * half + lo : rows * half + lo + 16, :].astype(F32)
-            for axis in range(3):
-                total = total + received[2 * axis + half][lo : lo + 16, :].astype(F32)
-            out_ref[rows * half + lo : rows * half + lo + 16, :] = total.astype(BF)
+        pl.when(pl.program_id(0) // (ADD_STEPS // 2) == half)(functools.partial(add, half))
 
 
 def reduce_cosets(pieces):
@@ -431,12 +447,20 @@
 
 
 def add_received(own, received):
+    size = (own.shape[0] // ADD_STEPS, own.shape[1])
+    last = ADD_STEPS // 2 - 1
     return pl.pallas_call(
         add_kernel,
-        in_specs=[VMEM] * 7,
-        out_specs=VMEM,
+        grid=(ADD_STEPS,),
+        in_specs=[pl.BlockSpec(size, lambda i: (i, 0))]
+        + [
+            pl.BlockSpec(size, lambda i: (jnp.minimum(i, last), 0)),
+            pl.BlockSpec(size, lambda i: (jnp.maximum(i - last - 1, 0), 0)),
+        ]
+        * 3,
+        out_specs=pl.BlockSpec(size, lambda i: (i, 0)),
         out_shape=jax.ShapeDtypeStruct(own.shape, BF),
-        compiler_params=whole_params(LIMIT_SMALL),
+        compiler_params=grid_params(LIMIT_ADD),
         cost_estimate=pl.CostEstimate(flops=1 << 28, bytes_accessed=5 << 20, transcendentals=0),
         name="add_received",
     )(own, *received)

time: 120 us -> 115 us (0.958)
  local copies, waits for them, and re-layouts: 8.03 us -> 1.01 us
  starting transfers between devices: 40.8 us -> 34.5 us
  waiting for transfers between devices: 28 us -> 34.2 us
  Pallas kernels: 41.7 us -> 44.4 us
    unnamed x34 -> x12, local copies, waits for them, and re-layouts: 8.03 us -> 1.01 us
    ppermute x6, starting transfers between devices: 8.3 us -> 4.66 us  [gather_cosets(): result.append(lax.ppermute(parts[half], 'd', shift(axis, 2 * half - 1)))]
    all_to_all x2, waiting for transfers between devices: 11.7 us -> 15.2 us  [exchange(): lax.all_to_all(pieces, 'd', 0, 0, axis_index_groups=COSETS, tiled=True)]
    ppermute x6, waiting for transfers between devices: 6.82 us -> 10.3 us  [reduce_cosets(): received.append(lax.ppermute(piece, 'd', shift(n // 2, 1 - 2 * (n % 2))))]
    all_to_all x2, starting transfers between devices: 20.5 us -> 17.1 us  [exchange(): lax.all_to_all(pieces, 'd', 0, 0, axis_index_groups=COSETS, tiled=True)]
    pallas_call x2, Pallas kernels: 7.95 us -> 9.65 us  [the longest x1 7.78 us: project(): pl.pallas_call(project_kernel, in_specs=[SMEM, SMEM, HBM] + [VMEM] * (1 +...]
    ppermute x6, starting transfers between devices: 6.84 us -> 8.08 us  [reduce_cosets(): received.append(lax.ppermute(piece, 'd', shift(n // 2, 1 - 2 * (n % 2))))]
  transfers between devices with their start and end apart: 17 -> 17, of which waited for: 6 -> 4; matrix products, arithmetic and copies ran while one was open for 0% -> 0% of each run, Pallas kernels for 30% -> 33%
where the time goes in v4:
time: 115 us
  Pallas kernels  44.4 us (39%)
  starting transfers between devices  34.5 us (30%)
  waiting for transfers between devices  34.2 us (30%)
    all_to_all x2, starting transfers between devices, exchange(): lax.all_to_all(pieces, 'd', 0, 0, axis_index_groups=COSETS, tiled=True)  17.1 us
    all_to_all x2, waiting for transfers between devices, exchange(): lax.all_to_all(pieces, 'd', 0, 0, axis_index_groups=COSETS, tiled=True)  15.2 us
    pallas_call x2, Pallas kernels, attend_forward(): pl.pallas_call(forward_kernel, grid_spec=pltpu.PrefetchScalarGridSpec(num...  13.1 us
    pallas_call x2, Pallas kernels, attend_backward(): pl.pallas_call(backward_kernel, grid_spec=pltpu.PrefetchScalarGridSpec(nu...  12.8 us
    ppermute x6, waiting for transfers between devices, reduce_cosets(): received.append(lax.ppermute(piece, 'd', shift(n // 2, 1 - 2 * (n % 2))))  10.3 us
    ppermute x6, waiting for transfers between devices, gather_cosets(): result.append(lax.ppermute(parts[half], 'd', shift(axis, 2 * half - 1)))  8.7 us
    ppermute x6, starting transfers between devices, reduce_cosets(): received.append(lax.ppermute(piece, 'd', shift(n // 2, 1 - 2 * (n % 2))))  8.08 us
    pallas_call x1, Pallas kernels, weight_sums(): pl.pallas_call(weight_kernel, in_specs=[SMEM] * 2 + [VMEM] * 4, out_specs...  7.95 us
  transfers between devices with their start and end apart: 17, of which 4 were waited for; matrix products, arithmetic and copies ran while one was open for 0% of the time, Pallas kernels for 33%

profile of v4, /device:TPU:1, one launch (start us, length us, event | category | flops | bytes accessed | tf_op | source)
XLA Modules:
  0.0 114.9 jit_solution(4346123225945788770)
XLA Ops:
  0.6 1.5 %collective-permute-start = (bf16[512,2048]{1,0:T(8,128)(2,1)}, bf16[512,2048]{1,0:T(8,128)(2,1)}, u32[]{:S(2)}, u32[]{:S(2)}) collective-permute-start(bf16[512,2048]{1,0:T(8,128)(2,1)} %up_own_hbm.1), channel_id=1, source_target_pairs={{0,1},{1,0},{2,3},{3,2},{4,5},{5,4},{6,7},{7,6},{8,9},{9,8},{10,11... | collective-permute-start | bytes 6291464 | tf_op jit(solution)/shard_map/ppermute | solution.py:502
  2.1 6.7 %attend_forward.2 = (bf16[512,1024]{1,0:T(8,128)(2,1)}, bf16[8,256,768]{2,1,0:T(8,128)(2,1)}, bf16[32,16,1024]{2,1,0:T(8,128)(2,1)}) custom-call(s32[1]{0:T(128)} %bitcast.base, bf16[512,2048]{1,0:T(8,128)(2,1)} %q_ref.7, bf16[512,2048]{1,0:T(8,128)(2,1)} %k_ref.7, bf16[512,2048]{1,0:T(8,128)(2,1)} %v_ref.7, s32[1,512]{1,0:T(1,128)} %ids_ref.3, ...), custom_call_target="tpu_custom_call" | custom-call | flops 3221225472 | bytes 9437184 | tf_op jit(solution)/shard_map/attend_forward/pallas_call | solution.py:158
  8.8 0.0 copy-start.1
  8.8 0.0 copy-start.5
  8.8 0.1 collective-permute-start.1
  8.9 11.1 %all-to-all-start = ((bf16[32,16,1024]{2,1,0:T(8,128)(2,1)}), bf16[32,16,1024]{2,1,0:T(8,128)(2,1)S(1)}, u32[]{:S(2)}, u32[]{:S(2)}) async-start(bf16[32,16,1024]{2,1,0:T(8,128)(2,1)} %get-tuple-element.27), calls=%async_computation | async-start | bytes 2097152 | tf_op jit(solution)/shard_map/all_to_all | solution.py:66
  20.0 0.0 copy-done.1
  20.1 0.0 copy-done.5
  20.1 0.0 copy-start.2
  20.1 6.4 %attend_forward.3 = (bf16[512,1024]{1,0:T(8,128)(2,1)S(1)}, bf16[8,256,768]{2,1,0:T(8,128)(2,1)}) custom-call(s32[1]{0:T(128)} %bitcast.4.base, bf16[512,2048]{1,0:T(8,128)(2,1)S(1)} %copy-done.1, bf16[512,2048]{1,0:T(8,128)(2,1)} %k_ref.7, bf16[512,2048]{1,0:T(8,128)(2,1)} %v_ref.7, s32[1,512]{1,0:T(1,128)S(1)} %copy-done.5), custom_call_target="tpu_custom_call" | custom-call | flops 3221225472 | bytes 9437184 | tf_op jit(solution)/shard_map/attend_forward/pallas_call | solution.py:158
  26.5 0.0 collective-permute-done.1.att_other_ref
  26.5 0.0 collective-permute-done.up_other_ref
  26.5 0.0 copy-done.2
  26.5 8.0 %weight_sums.1 = (bf16[512,1024]{1,0:T(8,128)(2,1)S(1)}, bf16[256,1024]{1,0:T(8,128)(2,1)S(1)}, bf16[256,1024]{1,0:T(8,128)(2,1)S(1)}, bf16[256,1024]{1,0:T(8,12...) custom-call(s32[1]{0:T(128)} %bitcast.1.kx_ref, s32[1]{0:T(128)} %bitcast.2.ky_ref, ...), custom_call_target="tpu_custom_call" | custom-call | flops 2147483648 | bytes 10485760 | tf_op jit(solution)/shard_map/weight_sums/pallas_call | solution.py:382
  34.5 0.0 copy-start.4
  34.5 1.0 copy-done.4
  35.5 3.4 %all-to-all-done = bf16[32,16,1024]{2,1,0:T(8,128)(2,1)S(1)} async-done(((bf16[32,16,1024]{2,1,0:T(8,128)(2,1)}), bf16[32,16,1024]{2,1,0:T(8,128)(2,1)S(1)}, u32[]{:S(2)}, u32[]{:S(2)}) %all-to-all-start) | async-done | bytes 1048608 | tf_op jit(solution)/shard_map/all_to_all | solution.py:66
  38.8 0.0 copy-start
  38.8 0.0 collective-permute-start.9
  38.8 0.1 split.1
  38.9 1.2 %collective-permute-start.6 = (bf16[256,1024]{1,0:T(8,128)(2,1)S(1)}, bf16[256,1024]{1,0:T(8,128)(2,1)S(1)}, u32[]{:S(2)}, u32[]{:S(2)}) collective-permute-start(bf16[256,1024]{1,0:T(8,128)(2,1)S(1)} %get-tuple-element.32), channel_id=1, source_target_pairs={{0,24},{1,25},{2,26},{3,27},{4,28},{5,29},{6,30},{7,31},{8,16},{9,... | collective-permute-start | bytes 1572872 | tf_op jit(solution)/shard_map/ppermute | solution.py:420
  40.1 1.7 %collective-permute-start.4 = (bf16[256,1024]{1,0:T(8,128)(2,1)S(1)}, bf16[256,1024]{1,0:T(8,128)(2,1)S(1)}, u32[]{:S(2)}, u32[]{:S(2)}) collective-permute-start(bf16[256,1024]{1,0:T(8,128)(2,1)S(1)} %get-tuple-element.32), channel_id=1, source_target_pairs={{0,6},{1,7},{2,0},{3,1},{4,2},{5,3},{6,4},{7,5},{8,14},{9,15},{10,... | collective-permute-start | bytes 1572872 | tf_op jit(solution)/shard_map/ppermute | solution.py:420
  41.8 1.5 %collective-permute-start.2 = (bf16[256,1024]{1,0:T(8,128)(2,1)S(1)}, bf16[256,1024]{1,0:T(8,128)(2,1)S(1)}, u32[]{:S(2)}, u32[]{:S(2)}) collective-permute-start(bf16[256,1024]{1,0:T(8,128)(2,1)S(1)} %get-tuple-element.32), channel_id=1, source_target_pairs={{0,96},{1,97},{2,98},{3,99},{4,100},{5,101},{6,102},{7,103},{8,104... | collective-permute-start | bytes 1572872 | tf_op jit(solution)/shard_map/ppermute | solution.py:420
  43.3 0.2 collective-permute-start.7
  43.6 10.3 %collective-permute-done.9.refs_0_ = bf16[256,1024]{1,0:T(8,128)(2,1)S(1)} collective-permute-done((bf16[256,1024]{1,0:T(8,128)(2,1)S(1)}, bf16[256,1024]{1,0:T(8,128)(2,1)S(1)}, u32[]{:S(2)}, u32[]{:S(2)}) %collective-permute-start.9) | collective-permute-done | bytes 524320 | tf_op jit(solution)/shard_map/ppermute | solution.py:445
  53.8 0.0 collective-permute-start.5
  53.8 0.0 collective-permute-done.6.refs_5_
  53.8 0.0 collective-permute-start.3
  53.8 0.0 collective-permute-done.4.refs_3_
  53.8 2.7 %collective-permute-start.10 = (bf16[256,1024]{1,0:T(8,128)(2,1)S(1)}, bf16[256,1024]{1,0:T(8,128)(2,1)S(1)}, u32[]{:S(2)}, u32[]{:S(2)}) collective-permute-start(bf16[256,1024]{1,0:T(8,128)(2,1)S(1)} %get-tuple-element.45), channel_id=1, source_target_pairs={{0,96},{1,97},{2,98},{3,99},{4,100},{5,101},{6,102},{7,103},{8,104... | collective-permute-start | bytes 1572872 | tf_op jit(solution)/shard_map/ppermute | solution.py:445
  56.5 0.0 collective-permute-done.2.refs_1_
  56.5 0.0 collective-permute-start.11
  56.5 0.0 collective-permute-done.7.refs_6_
  56.5 2.7 %collective-permute-start.12 = (bf16[256,1024]{1,0:T(8,128)(2,1)}, bf16[256,1024]{1,0:T(8,128)(2,1)S(1)}, u32[]{:S(2)}, u32[]{:S(2)}) collective-permute-start(bf16[256,1024]{1,0:T(8,128)(2,1)} %get-tuple-element.47), channel_id=1, source_target_pairs={{0,6},{1,7},{2,0},{3,1},{4,2},{5,3},{6,4},{7,5},{8,14},{9,15},{10,... | collective-permute-start | bytes 1572872 | tf_op jit(solution)/shard_map/ppermute | solution.py:445
  59.3 8.7 %collective-permute-done.5.refs_4_ = bf16[256,1024]{1,0:T(8,128)(2,1)S(1)} collective-permute-done((bf16[256,1024]{1,0:T(8,128)(2,1)S(1)}, bf16[256,1024]{1,0:T(8,128)(2,1)S(1)}, u32[]{:S(2)}, u32[]{:S(2)}) %collective-permute-start.5) | collective-permute-done | bytes 524320 | tf_op jit(solution)/shard_map/ppermute | solution.py:420
  68.0 0.0 collective-permute-start.13
  68.0 0.0 collective-permute-done.3.refs_2_
  68.0 2.7 %collective-permute-start.14 = (bf16[256,1024]{1,0:T(8,128)(2,1)}, bf16[256,1024]{1,0:T(8,128)(2,1)S(1)}, u32[]{:S(2)}, u32[]{:S(2)}) collective-permute-start(bf16[256,1024]{1,0:T(8,128)(2,1)} %get-tuple-element.49), channel_id=1, source_target_pairs={{0,24},{1,25},{2,26},{3,27},{4,28},{5,29},{6,30},{7,31},{8,16},{9,... | collective-permute-start | bytes 1572872 | tf_op jit(solution)/shard_map/ppermute | solution.py:445
  70.6 0.0 copy-done
  70.6 7.8 %project.1 = (bf16[512,1024]{1,0:T(8,128)(2,1)}, bf16[512,1024]{1,0:T(8,128)(2,1)}) custom-call(s32[1]{0:T(128)} %bitcast.1.kx_ref, s32[1]{0:T(128)} %bitcast.2.ky_ref, bf16[512,2048]{1,0:T(8,128)(2,1)} %up_own_hbm.1, bf16[512,2048]{1,0:T(8,128)(2,1)} %collective-permute-done.up_other_ref, bf16[512,1024]{1,0:T(8,128)(2,1)} %bitcast.7, ...), custom_call_target="tpu_custom_call" | custom-call | flops 2147483648 | bytes 10485760 | tf_op jit(solution)/shard_map/project/pallas_call | solution.py:324
  78.4 0.0 collective-permute-done.10.refs_1_
  78.4 3.1 %collective-permute-start.8 = (bf16[512,1024]{1,0:T(8,128)(2,1)}, bf16[512,1024]{1,0:T(8,128)(2,1)S(1)}, u32[]{:S(2)}, u32[]{:S(2)}) collective-permute-start(bf16[512,1024]{1,0:T(8,128)(2,1)} %get-tuple-element.34), channel_id=1, source_target_pairs={{0,1},{1,0},{2,3},{3,2},{4,5},{5,4},{6,7},{7,6},{8,9},{9,8},{10,11... | collective-permute-start | bytes 3145736 | tf_op jit(solution)/shard_map/ppermute | solution.py:516
  81.5 0.0 collective-permute-done.11.refs_2_
  81.5 0.0 collective-permute-done.12.refs_3_
  81.5 0.0 collective-permute-done.13.refs_4_
  81.5 0.0 collective-permute-done.14.refs_5_
  81.5 1.9 %add_received.1 = bf16[512,1024]{1,0:T(8,128)(2,1)} custom-call(bf16[512,1024]{1,0:T(8,128)(2,1)S(1)} %get-tuple-element.30.own_ref, bf16[256,1024]{1,0:T(8,128)(2,1)S(1)} %collective-permute-done.9.refs_0_, bf16[256,1024]{1,0:T(8,128)(2,1)S(1)} %collective-permute-done.10.refs_1_, bf16[256,1024]{1,0:T(8,128)(2,1)S(1)} %collective-permute-done.11.refs_2_, ...), custom_call_target="tpu_custom_call" | custom-call | flops 268435456 | bytes 5242880 | tf_op jit(solution)/shard_map/add_received/pallas_call | solution.py:452
  83.4 6.0 %all-to-all-start.1 = ((bf16[32,16,1024]{2,1,0:T(8,128)(2,1)}), bf16[32,16,1024]{2,1,0:T(8,128)(2,1)S(1)}, u32[]{:S(2)}, u32[]{:S(2)}) async-start(bf16[32,16,1024]{2,1,0:T(8,128)(2,1)} %bitcast.5), calls=%async_computation.1 | async-start | bytes 2097152 | tf_op jit(solution)/shard_map/all_to_all | solution.py:66
  89.4 0.0 copy-start.3
  89.4 6.6 %attend_backward.2 = (bf16[512,2048]{1,0:T(8,128)(2,1)}, bf16[512,2048]{1,0:T(8,128)(2,1)}, bf16[512,2048]{1,0:T(8,128)(2,1)}) custom-call(s32[1]{0:T(128)} %bitcast.4.base, bf16[512,2048]{1,0:T(8,128)(2,1)} %q_ref.7, bf16[512,2048]{1,0:T(8,128)(2,1)} %k_ref.7, bf16[512,2048]{1,0:T(8,128)(2,1)} %v_ref.7, bf16[512,1024]{1,0:T(8,128)(2,1)} %get-tuple-element.36.g_ref, ...), custom_call_target="tpu_custom_call" | custom-call | flops 2147483648 | bytes 12582912 | tf_op jit(solution)/shard_map/attend_backward/pallas_call | solution.py:262
  96.0 11.9 %all-to-all-done.1.in_ref = bf16[32,16,1024]{2,1,0:T(8,128)(2,1)S(1)} async-done(((bf16[32,16,1024]{2,1,0:T(8,128)(2,1)}), bf16[32,16,1024]{2,1,0:T(8,128)(2,1)S(1)}, u32[]{:S(2)}, u32[]{:S(2)}) %all-to-all-start.1) | async-done | bytes 1048608 | tf_op jit(solution)/shard_map/all_to_all | solution.py:66
  107.9 0.8 own_rows.1
  108.7 0.0 collective-permute-done.8.g_ref
  108.7 0.0 copy-done.3
  108.7 6.2 %attend_backward.3 = (bf16[512,2048]{1,0:T(8,128)(2,1)}, bf16[512,2048]{1,0:T(8,128)(2,1)}, bf16[512,2048]{1,0:T(8,128)(2,1)}) custom-call(s32[1]{0:T(128)} %bitcast.base, bf16[512,2048]{1,0:T(8,128)(2,1)} %q_ref.7, bf16[512,2048]{1,0:T(8,128)(2,1)} %k_ref.7, bf16[512,2048]{1,0:T(8,128)(2,1)} %v_ref.7, ...), custom_call_target="tpu_custom_call", output_to_operand_aliasing={{0}: (7, {}), {1}: (8, {}), {2}: (9, {})} | custom-call | flops 2147483648 | bytes 12582912 | tf_op jit(solution)/shard_map/attend_backward/pallas_call | solution.py:262
Async XLA Ops:
  0.6 25.9 %collective-permute-start = (bf16[512,2048]{1,0:T(8,128)(2,1)}, bf16[512,2048]{1,0:T(8,128)(2,1)}, u32[]{:S(2)}, u32[]{:S(2)}) collective-permute-start(bf16[512,2048]{1,0:T(8,128)(2,1)} %up_own_hbm.1), channel_id=1, source_target_pairs={{0,1},{1,0},{2,3},{3,2},{4,5},{5,4},{6,7},{7,6},{8,9},{9,8},{10,11... | collective-permute-start | bytes 6291464 | tf_op jit(solution)/shard_map/ppermute | solution.py:502
  8.8 11.3 %copy-start.1 = (bf16[512,2048]{1,0:T(8,128)(2,1)S(1)}, bf16[512,2048]{1,0:T(8,128)(2,1)}, u32[]{:S(2)}) copy-start(bf16[512,2048]{1,0:T(8,128)(2,1)} %q_ref.7) | copy-start | bytes 6291460
  8.8 11.3 %copy-start.5 = (s32[1,512]{1,0:T(1,128)S(1)}, s32[1,512]{1,0:T(1,128)}, u32[]{:S(2)}) copy-start(s32[1,512]{1,0:T(1,128)} %ids_ref.3) | copy-start | bytes 6148
  8.8 17.7 %collective-permute-start.1 = (bf16[512,1024]{1,0:T(8,128)(2,1)}, bf16[512,1024]{1,0:T(8,128)(2,1)}, u32[]{:S(2)}, u32[]{:S(2)}) collective-permute-start(bf16[512,1024]{1,0:T(8,128)(2,1)} %get-tuple-element.29.att_ref), channel_id=1, source_target_pairs={{0,1},{1,0},{2,3},{3,2},{4,5},{5,4},{6,7},{7,6},{8,9},{9,8},{10,11... | collective-permute-start | bytes 3145736 | tf_op jit(solution)/shard_map/ppermute | solution.py:507
  8.9 29.9 %all-to-all-start = ((bf16[32,16,1024]{2,1,0:T(8,128)(2,1)}), bf16[32,16,1024]{2,1,0:T(8,128)(2,1)S(1)}, u32[]{:S(2)}, u32[]{:S(2)}) async-start(bf16[32,16,1024]{2,1,0:T(8,128)(2,1)} %get-tuple-element.27), calls=%async_computation | async-start | bytes 2097152 | tf_op jit(solution)/shard_map/all_to_all | solution.py:66
  20.1 6.4 %copy-start.2 = (bf16[512,2048]{1,0:T(8,128)(2,1)S(1)}, bf16[512,2048]{1,0:T(8,128)(2,1)}, u32[]{:S(2)}) copy-start(bf16[512,2048]{1,0:T(8,128)(2,1)} %up_own_hbm.1) | copy-start | bytes 6291460
  34.5 1.0 copy-start.4
  38.8 31.8 %copy-start = (bf16[32,16,1024]{2,1,0:T(8,128)(2,1)}, bf16[32,16,1024]{2,1,0:T(8,128)(2,1)S(1)}, u32[]{:S(2)}) copy-start(bf16[32,16,1024]{2,1,0:T(8,128)(2,1)S(1)} %all-to-all-done) | copy-start | bytes 3145732
  38.8 15.0 %collective-permute-start.9 = (bf16[256,1024]{1,0:T(8,128)(2,1)S(1)}, bf16[256,1024]{1,0:T(8,128)(2,1)S(1)}, u32[]{:S(2)}, u32[]{:S(2)}) collective-permute-start(bf16[256,1024]{1,0:T(8,128)(2,1)S(1)} %get-tuple-element.44), channel_id=1, source_target_pairs={{0,32},{1,33},{2,34},{3,35},{4,36},{5,37},{6,38},{7,39},{8,40},{9,... | collective-permute-start | bytes 1572872 | tf_op jit(solution)/shard_map/ppermute | solution.py:445
  38.9 14.9 %collective-permute-start.6 = (bf16[256,1024]{1,0:T(8,128)(2,1)S(1)}, bf16[256,1024]{1,0:T(8,128)(2,1)S(1)}, u32[]{:S(2)}, u32[]{:S(2)}) collective-permute-start(bf16[256,1024]{1,0:T(8,128)(2,1)S(1)} %get-tuple-element.32), channel_id=1, source_target_pairs={{0,24},{1,25},{2,26},{3,27},{4,28},{5,29},{6,30},{7,31},{8,16},{9,... | collective-permute-start | bytes 1572872 | tf_op jit(solution)/shard_map/ppermute | solution.py:420
  40.1 13.8 %collective-permute-start.4 = (bf16[256,1024]{1,0:T(8,128)(2,1)S(1)}, bf16[256,1024]{1,0:T(8,128)(2,1)S(1)}, u32[]{:S(2)}, u32[]{:S(2)}) collective-permute-start(bf16[256,1024]{1,0:T(8,128)(2,1)S(1)} %get-tuple-element.32), channel_id=1, source_target_pairs={{0,6},{1,7},{2,0},{3,1},{4,2},{5,3},{6,4},{7,5},{8,14},{9,15},{10,... | collective-permute-start | bytes 1572872 | tf_op jit(solution)/shard_map/ppermute | solution.py:420
  41.8 14.7 %collective-permute-start.2 = (bf16[256,1024]{1,0:T(8,128)(2,1)S(1)}, bf16[256,1024]{1,0:T(8,128)(2,1)S(1)}, u32[]{:S(2)}, u32[]{:S(2)}) collective-permute-start(bf16[256,1024]{1,0:T(8,128)(2,1)S(1)} %get-tuple-element.32), channel_id=1, source_target_pairs={{0,96},{1,97},{2,98},{3,99},{4,100},{5,101},{6,102},{7,103},{8,104... | collective-permute-start | bytes 1572872 | tf_op jit(solution)/shard_map/ppermute | solution.py:420
  43.3 13.2 %collective-permute-start.7 = (bf16[256,1024]{1,0:T(8,128)(2,1)S(1)}, bf16[256,1024]{1,0:T(8,128)(2,1)S(1)}, u32[]{:S(2)}, u32[]{:S(2)}) collective-permute-start(bf16[256,1024]{1,0:T(8,128)(2,1)S(1)} %get-tuple-element.33), channel_id=1, source_target_pairs={{0,16},{1,17},{2,18},{3,19},{4,20},{5,21},{6,22},{7,23},{8,24},{9,... | collective-permute-start | bytes 1572872 | tf_op jit(solution)/shard_map/ppermute | solution.py:420
  53.8 14.1 %collective-permute-start.5 = (bf16[256,1024]{1,0:T(8,128)(2,1)S(1)}, bf16[256,1024]{1,0:T(8,128)(2,1)S(1)}, u32[]{:S(2)}, u32[]{:S(2)}) collective-permute-start(bf16[256,1024]{1,0:T(8,128)(2,1)S(1)} %get-tuple-element.33), channel_id=1, source_target_pairs={{0,2},{1,3},{2,4},{3,5},{4,6},{5,7},{6,0},{7,1},{8,10},{9,11},{10,... | collective-permute-start | bytes 1572872 | tf_op jit(solution)/shard_map/ppermute | solution.py:420
  53.8 14.1 %collective-permute-start.3 = (bf16[256,1024]{1,0:T(8,128)(2,1)S(1)}, bf16[256,1024]{1,0:T(8,128)(2,1)S(1)}, u32[]{:S(2)}, u32[]{:S(2)}) collective-permute-start(bf16[256,1024]{1,0:T(8,128)(2,1)S(1)} %get-tuple-element.33), channel_id=1, source_target_pairs={{0,32},{1,33},{2,34},{3,35},{4,36},{5,37},{6,38},{7,39},{8,40},{9,... | collective-permute-start | bytes 1572872 | tf_op jit(solution)/shard_map/ppermute | solution.py:420
  53.8 24.6 %collective-permute-start.10 = (bf16[256,1024]{1,0:T(8,128)(2,1)S(1)}, bf16[256,1024]{1,0:T(8,128)(2,1)S(1)}, u32[]{:S(2)}, u32[]{:S(2)}) collective-permute-start(bf16[256,1024]{1,0:T(8,128)(2,1)S(1)} %get-tuple-element.45), channel_id=1, source_target_pairs={{0,96},{1,97},{2,98},{3,99},{4,100},{5,101},{6,102},{7,103},{8,104... | collective-permute-start | bytes 1572872 | tf_op jit(solution)/shard_map/ppermute | solution.py:445
  56.5 25.0 %collective-permute-start.11 = (bf16[256,1024]{1,0:T(8,128)(2,1)}, bf16[256,1024]{1,0:T(8,128)(2,1)S(1)}, u32[]{:S(2)}, u32[]{:S(2)}) collective-permute-start(bf16[256,1024]{1,0:T(8,128)(2,1)} %get-tuple-element.46), channel_id=1, source_target_pairs={{0,2},{1,3},{2,4},{3,5},{4,6},{5,7},{6,0},{7,1},{8,10},{9,11},{10,... | collective-permute-start | bytes 1572872 | tf_op jit(solution)/shard_map/ppermute | solution.py:445
  56.5 25.0 %collective-permute-start.12 = (bf16[256,1024]{1,0:T(8,128)(2,1)}, bf16[256,1024]{1,0:T(8,128)(2,1)S(1)}, u32[]{:S(2)}, u32[]{:S(2)}) collective-permute-start(bf16[256,1024]{1,0:T(8,128)(2,1)} %get-tuple-element.47), channel_id=1, source_target_pairs={{0,6},{1,7},{2,0},{3,1},{4,2},{5,3},{6,4},{7,5},{8,14},{9,15},{10,... | collective-permute-start | bytes 1572872 | tf_op jit(solution)/shard_map/ppermute | solution.py:445
  68.0 13.6 %collective-permute-start.13 = (bf16[256,1024]{1,0:T(8,128)(2,1)}, bf16[256,1024]{1,0:T(8,128)(2,1)S(1)}, u32[]{:S(2)}, u32[]{:S(2)}) collective-permute-start(bf16[256,1024]{1,0:T(8,128)(2,1)} %get-tuple-element.48), channel_id=1, source_target_pairs={{0,16},{1,17},{2,18},{3,19},{4,20},{5,21},{6,22},{7,23},{8,24},{9,... | collective-permute-start | bytes 1572872 | tf_op jit(solution)/shard_map/ppermute | solution.py:445
  68.0 13.6 %collective-permute-start.14 = (bf16[256,1024]{1,0:T(8,128)(2,1)}, bf16[256,1024]{1,0:T(8,128)(2,1)S(1)}, u32[]{:S(2)}, u32[]{:S(2)}) collective-permute-start(bf16[256,1024]{1,0:T(8,128)(2,1)} %get-tuple-element.49), channel_id=1, source_target_pairs={{0,24},{1,25},{2,26},{3,27},{4,28},{5,29},{6,30},{7,31},{8,16},{9,... | collective-permute-start | bytes 1572872 | tf_op jit(solution)/shard_map/ppermute | solution.py:445
  78.4 30.2 %collective-permute-start.8 = (bf16[512,1024]{1,0:T(8,128)(2,1)}, bf16[512,1024]{1,0:T(8,128)(2,1)S(1)}, u32[]{:S(2)}, u32[]{:S(2)}) collective-permute-start(bf16[512,1024]{1,0:T(8,128)(2,1)} %get-tuple-element.34), channel_id=1, source_target_pairs={{0,1},{1,0},{2,3},{3,2},{4,5},{5,4},{6,7},{7,6},{8,9},{9,8},{10,11... | collective-permute-start | bytes 3145736 | tf_op jit(solution)/shard_map/ppermute | solution.py:516
  83.4 24.5 %all-to-all-start.1 = ((bf16[32,16,1024]{2,1,0:T(8,128)(2,1)}), bf16[32,16,1024]{2,1,0:T(8,128)(2,1)S(1)}, u32[]{:S(2)}, u32[]{:S(2)}) async-start(bf16[32,16,1024]{2,1,0:T(8,128)(2,1)} %bitcast.5), calls=%async_computation.1 | async-start | bytes 2097152 | tf_op jit(solution)/shard_map/all_to_all | solution.py:66
  89.4 19.3 %copy-start.3 = (bf16[512,1024]{1,0:T(8,128)(2,1)S(1)}, bf16[512,1024]{1,0:T(8,128)(2,1)}, u32[]{:S(2)}) copy-start(bf16[512,1024]{1,0:T(8,128)(2,1)} %get-tuple-element.29.att_ref) | copy-start | bytes 3145732

commit v5 on v3

--- a/solution.py
+++ b/solution.py
@@ -15,9 +15,9 @@
 STEP_HEADS = 4
 LIMIT = 50
 LIMIT_A = 60
-LIMIT_BACK = 50
+LIMIT_BACK = 60
 LIMIT_LAST = 50
-LIMIT_PROJECT = 20
+LIMIT_PROJECT = 54
 LIMIT_SUMS = 20
 LIMIT_SMALL = 8
 FLOPS_4US = 2 << 30
@@ -293,8 +293,10 @@
         yield other, 16, 32
 
 
-def project_kernel(kx_ref, ky_ref, up_own_ref, up_other_ref, *refs):
-    pieces, (own_ref, other_ref, weight_ref) = refs[:7], refs[7:]
+def project_kernel(kx_ref, ky_ref, up_own_hbm, up_other_ref, *refs):
+    pieces, (own_ref, other_ref, weight_ref, up_own_ref, sem) = refs[:7], refs[7:]
+    load = pltpu.make_async_copy(up_own_hbm, up_own_ref, sem)
+    load.start()
     place = (kx_ref[0], ky_ref[0])
     for ref, (other, lo, hi) in zip(pieces, coset_parts()):
         for block in range(lo, hi):
@@ -302,6 +304,8 @@
             weight_ref[pl.ds(row, 16), :] = ref[16 * (block - lo) : 16 * (block - lo + 1), :]
     step = 512
     for up_ref, out_ref in ((up_other_ref, other_ref), (up_own_ref, own_ref)):
+        if up_ref is up_own_ref:
+            load.wait()
         for lo in range(0, out_ref.shape[1], step):
             out_ref[:, lo : lo + step] = jnp.dot(
                 up_ref[...], weight_ref[:, lo : lo + step], preferred_element_type=F32
@@ -318,10 +322,14 @@
     cols = pieces[0].shape[1]
     return pl.pallas_call(
         project_kernel,
-        in_specs=[SMEM] * 2 + [VMEM] * (2 + len(pieces)),
+        in_specs=[SMEM, SMEM, HBM] + [VMEM] * (1 + len(pieces)),
         out_specs=[VMEM] * 2,
         out_shape=[jax.ShapeDtypeStruct((rows, cols), BF)] * 2,
-        scratch_shapes=[pltpu.VMEM((width, cols), BF)],
+        scratch_shapes=[
+            pltpu.VMEM((width, cols), BF),
+            pltpu.VMEM((rows, width), BF),
+            pltpu.SemaphoreType.DMA,
+        ],
         compiler_params=whole_params(LIMIT_PROJECT),
         cost_estimate=pl.CostEstimate(
             flops=FLOPS_4US, bytes_accessed=10 << 20, transcendentals=0

time: 120 us -> 115 us (0.958)
  starting transfers between devices: 40.8 us -> 33.5 us
  local copies, waits for them, and re-layouts: 8.03 us -> 1.03 us
  waiting for transfers between devices: 28 us -> 34.2 us
  Pallas kernels: 41.7 us -> 44.9 us
    unnamed x34 -> x24, local copies, waits for them, and re-layouts: 8.03 us -> 1.03 us
    all_to_all x2, starting transfers between devices: 20.5 us -> 16.1 us  [exchange(): lax.all_to_all(pieces, 'd', 0, 0, axis_index_groups=COSETS, tiled=True)]
    ppermute x6, starting transfers between devices: 8.3 us -> 4.73 us  [gather_cosets(): result.append(lax.ppermute(parts[half], 'd', shift(axis, 2 * half - 1)))]
    all_to_all x2, waiting for transfers between devices: 11.7 us -> 15.2 us  [exchange(): lax.all_to_all(pieces, 'd', 0, 0, axis_index_groups=COSETS, tiled=True)]
    ppermute x6, waiting for transfers between devices: 6.82 us -> 10.3 us  [reduce_cosets(): received.append(lax.ppermute(piece, 'd', shift(n // 2, 1 - 2 * (n % 2))))]
    pallas_call x1, Pallas kernels: 6.35 us -> 8.74 us  [project(): pl.pallas_call(project_kernel, in_specs=[SMEM, SMEM, HBM] + [VMEM] * (1 +...]
  transfers between devices with their start and end apart: 17 -> 17, of which waited for: 6 -> 5; matrix products, arithmetic and copies ran while one was open for 0% -> 0% of each run, Pallas kernels for 30% -> 34%
where the time goes in v5:
time: 115 us
  Pallas kernels  44.9 us (39%)
  waiting for transfers between devices  34.2 us (30%)
  starting transfers between devices  33.5 us (29%)
    all_to_all x2, starting transfers between devices, exchange(): lax.all_to_all(pieces, 'd', 0, 0, axis_index_groups=COSETS, tiled=True)  16.1 us
    all_to_all x2, waiting for transfers between devices, exchange(): lax.all_to_all(pieces, 'd', 0, 0, axis_index_groups=COSETS, tiled=True)  15.2 us
    pallas_call x2, Pallas kernels, attend_forward(): pl.pallas_call(forward_kernel, grid_spec=pltpu.PrefetchScalarGridSpec(num...  13.1 us
    pallas_call x2, Pallas kernels, attend_backward(): pl.pallas_call(backward_kernel, grid_spec=pltpu.PrefetchScalarGridSpec(nu...  12.8 us
    ppermute x6, waiting for transfers between devices, reduce_cosets(): received.append(lax.ppermute(piece, 'd', shift(n // 2, 1 - 2 * (n % 2))))  10.3 us
    ppermute x6, waiting for transfers between devices, gather_cosets(): result.append(lax.ppermute(parts[half], 'd', shift(axis, 2 * half - 1)))  8.75 us
    pallas_call x1, Pallas kernels, project(): pl.pallas_call(project_kernel, in_specs=[SMEM, SMEM, HBM] + [VMEM] * (1 +...  8.74 us
    pallas_call x1, Pallas kernels, weight_sums(): pl.pallas_call(weight_kernel, in_specs=[SMEM] * 2 + [VMEM] * 4, out_specs...  7.96 us
  transfers between devices with their start and end apart: 17, of which 5 were waited for; matrix products, arithmetic and copies ran while one was open for 0% of the time, Pallas kernels for 34%

profile of v5, /device:TPU:1, one launch (start us, length us, event | category | flops | bytes accessed | tf_op | source)
XLA Modules:
  0.0 114.5 jit_solution(15537837197816564256)
XLA Ops:
  0.6 1.5 %collective-permute-start = (bf16[512,2048]{1,0:T(8,128)(2,1)}, bf16[512,2048]{1,0:T(8,128)(2,1)}, u32[]{:S(2)}, u32[]{:S(2)}) collective-permute-start(bf16[512,2048]{1,0:T(8,128)(2,1)} %up_own_hbm.1), channel_id=1, source_target_pairs={{0,1},{1,0},{2,3},{3,2},{4,5},{5,4},{6,7},{7,6},{8,9},{9,8},{10,11... | collective-permute-start | bytes 6291464 | tf_op jit(solution)/shard_map/ppermute | solution.py:486
  2.1 6.7 %attend_forward.2 = (bf16[512,1024]{1,0:T(8,128)(2,1)}, bf16[8,256,768]{2,1,0:T(8,128)(2,1)}, bf16[32,16,1024]{2,1,0:T(8,128)(2,1)}) custom-call(s32[1]{0:T(128)} %bitcast.base, bf16[512,2048]{1,0:T(8,128)(2,1)} %q_ref.7, bf16[512,2048]{1,0:T(8,128)(2,1)} %k_ref.7, bf16[512,2048]{1,0:T(8,128)(2,1)} %v_ref.7, s32[1,512]{1,0:T(1,128)} %ids_ref.3, ...), custom_call_target="tpu_custom_call" | custom-call | flops 3221225472 | bytes 9437184 | tf_op jit(solution)/shard_map/attend_forward/pallas_call | solution.py:157
  8.8 0.0 copy-start.1
  8.8 0.0 copy-start.5
  8.8 0.1 collective-permute-start.1
  8.9 11.1 %all-to-all-start = ((bf16[32,16,1024]{2,1,0:T(8,128)(2,1)}), bf16[32,16,1024]{2,1,0:T(8,128)(2,1)S(1)}, u32[]{:S(2)}, u32[]{:S(2)}) async-start(bf16[32,16,1024]{2,1,0:T(8,128)(2,1)} %get-tuple-element.27), calls=%async_computation | async-start | bytes 2097152 | tf_op jit(solution)/shard_map/all_to_all | solution.py:65
  20.0 0.0 copy-done.1
  20.1 0.0 copy-done.5
  20.1 0.0 copy-start.2
  20.1 6.4 %attend_forward.3 = (bf16[512,1024]{1,0:T(8,128)(2,1)S(1)}, bf16[8,256,768]{2,1,0:T(8,128)(2,1)}) custom-call(s32[1]{0:T(128)} %bitcast.4.base, bf16[512,2048]{1,0:T(8,128)(2,1)S(1)} %copy-done.1, bf16[512,2048]{1,0:T(8,128)(2,1)} %k_ref.7, bf16[512,2048]{1,0:T(8,128)(2,1)} %v_ref.7, s32[1,512]{1,0:T(1,128)S(1)} %copy-done.5), custom_call_target="tpu_custom_call" | custom-call | flops 3221225472 | bytes 9437184 | tf_op jit(solution)/shard_map/attend_forward/pallas_call | solution.py:157
  26.5 0.0 collective-permute-done.1.att_other_ref
  26.5 0.0 collective-permute-done.up_other_ref
  26.5 0.0 copy-done.2
  26.5 8.0 %weight_sums.1 = (bf16[512,1024]{1,0:T(8,128)(2,1)S(1)}, bf16[256,1024]{1,0:T(8,128)(2,1)S(1)}, bf16[256,1024]{1,0:T(8,128)(2,1)S(1)}, bf16[256,1024]{1,0:T(8,12...) custom-call(s32[1]{0:T(128)} %bitcast.1.kx_ref, s32[1]{0:T(128)} %bitcast.2.ky_ref, ...), custom_call_target="tpu_custom_call" | custom-call | flops 2147483648 | bytes 10485760 | tf_op jit(solution)/shard_map/weight_sums/pallas_call | solution.py:381
  34.5 0.0 copy-start.4
  34.5 1.0 copy-done.4
  35.5 3.4 %all-to-all-done = bf16[32,16,1024]{2,1,0:T(8,128)(2,1)S(1)} async-done(((bf16[32,16,1024]{2,1,0:T(8,128)(2,1)}), bf16[32,16,1024]{2,1,0:T(8,128)(2,1)S(1)}, u32[]{:S(2)}, u32[]{:S(2)}) %all-to-all-start) | async-done | bytes 1048608 | tf_op jit(solution)/shard_map/all_to_all | solution.py:65
  38.8 0.0 copy-start
  38.8 0.0 collective-permute-start.9
  38.8 0.1 split.1
  38.9 1.2 %collective-permute-start.6 = (bf16[256,1024]{1,0:T(8,128)(2,1)S(1)}, bf16[256,1024]{1,0:T(8,128)(2,1)S(1)}, u32[]{:S(2)}, u32[]{:S(2)}) collective-permute-start(bf16[256,1024]{1,0:T(8,128)(2,1)S(1)} %get-tuple-element.32), channel_id=1, source_target_pairs={{0,24},{1,25},{2,26},{3,27},{4,28},{5,29},{6,30},{7,31},{8,16},{9,... | collective-permute-start | bytes 1572872 | tf_op jit(solution)/shard_map/ppermute | solution.py:419
  40.1 1.7 %collective-permute-start.4 = (bf16[256,1024]{1,0:T(8,128)(2,1)S(1)}, bf16[256,1024]{1,0:T(8,128)(2,1)S(1)}, u32[]{:S(2)}, u32[]{:S(2)}) collective-permute-start(bf16[256,1024]{1,0:T(8,128)(2,1)S(1)} %get-tuple-element.32), channel_id=1, source_target_pairs={{0,6},{1,7},{2,0},{3,1},{4,2},{5,3},{6,4},{7,5},{8,14},{9,15},{10,... | collective-permute-start | bytes 1572872 | tf_op jit(solution)/shard_map/ppermute | solution.py:419
  41.8 1.5 %collective-permute-start.2 = (bf16[256,1024]{1,0:T(8,128)(2,1)S(1)}, bf16[256,1024]{1,0:T(8,128)(2,1)S(1)}, u32[]{:S(2)}, u32[]{:S(2)}) collective-permute-start(bf16[256,1024]{1,0:T(8,128)(2,1)S(1)} %get-tuple-element.32), channel_id=1, source_target_pairs={{0,96},{1,97},{2,98},{3,99},{4,100},{5,101},{6,102},{7,103},{8,104... | collective-permute-start | bytes 1572872 | tf_op jit(solution)/shard_map/ppermute | solution.py:419
  43.3 0.2 collective-permute-start.7
  43.6 10.3 %collective-permute-done.9.refs_0_ = bf16[256,1024]{1,0:T(8,128)(2,1)S(1)} collective-permute-done((bf16[256,1024]{1,0:T(8,128)(2,1)S(1)}, bf16[256,1024]{1,0:T(8,128)(2,1)S(1)}, u32[]{:S(2)}, u32[]{:S(2)}) %collective-permute-start.9) | collective-permute-done | bytes 524320 | tf_op jit(solution)/shard_map/ppermute | solution.py:437
  53.8 0.0 collective-permute-start.5
  53.8 0.0 collective-permute-done.6.refs_5_
  53.8 0.0 copy-start.6
  53.8 0.1 collective-permute-start.3
  53.9 0.0 collective-permute-done.4.refs_3_
  53.9 0.0 copy-start.7
  53.9 2.6 %collective-permute-start.10 = (bf16[256,1024]{1,0:T(8,128)(2,1)S(1)}, bf16[256,1024]{1,0:T(8,128)(2,1)S(1)}, u32[]{:S(2)}, u32[]{:S(2)}) collective-permute-start(bf16[256,1024]{1,0:T(8,128)(2,1)S(1)} %get-tuple-element.45), channel_id=1, source_target_pairs={{0,96},{1,97},{2,98},{3,99},{4,100},{5,101},{6,102},{7,103},{8,104... | collective-permute-start | bytes 1572872 | tf_op jit(solution)/shard_map/ppermute | solution.py:437
  56.6 0.0 collective-permute-done.2.refs_1_
  56.6 0.0 collective-permute-start.11
  56.6 0.0 collective-permute-done.7.refs_6_
  56.6 0.0 copy-start.9
  56.6 2.7 %collective-permute-start.12 = (bf16[256,1024]{1,0:T(8,128)(2,1)}, bf16[256,1024]{1,0:T(8,128)(2,1)S(1)}, u32[]{:S(2)}, u32[]{:S(2)}) collective-permute-start(bf16[256,1024]{1,0:T(8,128)(2,1)} %get-tuple-element.47), channel_id=1, source_target_pairs={{0,6},{1,7},{2,0},{3,1},{4,2},{5,3},{6,4},{7,5},{8,14},{9,15},{10,... | collective-permute-start | bytes 1572872 | tf_op jit(solution)/shard_map/ppermute | solution.py:437
  59.3 8.7 %collective-permute-done.5.refs_4_ = bf16[256,1024]{1,0:T(8,128)(2,1)S(1)} collective-permute-done((bf16[256,1024]{1,0:T(8,128)(2,1)S(1)}, bf16[256,1024]{1,0:T(8,128)(2,1)S(1)}, u32[]{:S(2)}, u32[]{:S(2)}) %collective-permute-start.5) | collective-permute-done | bytes 524320 | tf_op jit(solution)/shard_map/ppermute | solution.py:419
  68.0 0.0 collective-permute-start.13
  68.0 0.1 collective-permute-done.3.refs_2_
  68.0 2.6 %collective-permute-start.14 = (bf16[256,1024]{1,0:T(8,128)(2,1)}, bf16[256,1024]{1,0:T(8,128)(2,1)S(1)}, u32[]{:S(2)}, u32[]{:S(2)}) collective-permute-start(bf16[256,1024]{1,0:T(8,128)(2,1)} %get-tuple-element.49), channel_id=1, source_target_pairs={{0,24},{1,25},{2,26},{3,27},{4,28},{5,29},{6,30},{7,31},{8,16},{9,... | collective-permute-start | bytes 1572872 | tf_op jit(solution)/shard_map/ppermute | solution.py:437
  70.6 0.0 copy-done
  70.6 0.0 copy-done.6
  70.6 0.0 copy-done.7
  70.6 0.0 copy-done.8
  70.7 0.0 copy-done.9
  70.7 0.0 copy-done.10
  70.7 0.0 copy-done.11
  70.7 8.7 %project.1 = (bf16[512,1024]{1,0:T(8,128)(2,1)}, bf16[512,1024]{1,0:T(8,128)(2,1)}) custom-call(s32[1]{0:T(128)} %bitcast.1.kx_ref, s32[1]{0:T(128)} %bitcast.2.ky_ref, bf16[512,2048]{1,0:T(8,128)(2,1)} %up_own_hbm.1, bf16[512,2048]{1,0:T(8,128)(2,1)} %collective-permute-done.up_other_ref, bf16[512,1024]{1,0:T(8,128)(2,1)} %bitcast.7, ...), custom_call_target="tpu_custom_call" | custom-call | flops 2147483648 | bytes 10485760 | tf_op jit(solution)/shard_map/project/pallas_call | solution.py:323
  79.4 0.0 collective-permute-done.10.refs_1_
  79.4 3.1 %collective-permute-start.8 = (bf16[512,1024]{1,0:T(8,128)(2,1)}, bf16[512,1024]{1,0:T(8,128)(2,1)S(1)}, u32[]{:S(2)}, u32[]{:S(2)}) collective-permute-start(bf16[512,1024]{1,0:T(8,128)(2,1)} %get-tuple-element.34), channel_id=1, source_target_pairs={{0,1},{1,0},{2,3},{3,2},{4,5},{5,4},{6,7},{7,6},{8,9},{9,8},{10,11... | collective-permute-start | bytes 3145736 | tf_op jit(solution)/shard_map/ppermute | solution.py:500
  82.5 0.0 collective-permute-done.11.refs_2_
  82.5 0.0 collective-permute-done.12.refs_3_
  82.5 0.0 collective-permute-done.13.refs_4_
  82.5 0.0 collective-permute-done.14.refs_5_
  82.5 1.5 %add_received.1 = bf16[512,1024]{1,0:T(8,128)(2,1)} custom-call(bf16[512,1024]{1,0:T(8,128)(2,1)S(1)} %get-tuple-element.30.own_ref, bf16[256,1024]{1,0:T(8,128)(2,1)S(1)} %collective-permute-done.9.refs_0_, bf16[256,1024]{1,0:T(8,128)(2,1)S(1)} %collective-permute-done.10.refs_1_, bf16[256,1024]{1,0:T(8,128)(2,1)S(1)} %collective-permute-done.11.refs_2_, ...), custom_call_target="tpu_custom_call" | custom-call | flops 268435456 | bytes 5242880 | tf_op jit(solution)/shard_map/add_received/pallas_call | solution.py:442
  84.0 5.0 %all-to-all-start.1 = ((bf16[32,16,1024]{2,1,0:T(8,128)(2,1)}), bf16[32,16,1024]{2,1,0:T(8,128)(2,1)S(1)}, u32[]{:S(2)}, u32[]{:S(2)}) async-start(bf16[32,16,1024]{2,1,0:T(8,128)(2,1)} %bitcast.5), calls=%async_computation.1 | async-start | bytes 2097152 | tf_op jit(solution)/shard_map/all_to_all | solution.py:65
  89.1 0.0 copy-start.3
  89.1 6.6 %attend_backward.2 = (bf16[512,2048]{1,0:T(8,128)(2,1)}, bf16[512,2048]{1,0:T(8,128)(2,1)}, bf16[512,2048]{1,0:T(8,128)(2,1)}) custom-call(s32[1]{0:T(128)} %bitcast.4.base, bf16[512,2048]{1,0:T(8,128)(2,1)} %q_ref.7, bf16[512,2048]{1,0:T(8,128)(2,1)} %k_ref.7, bf16[512,2048]{1,0:T(8,128)(2,1)} %v_ref.7, bf16[512,1024]{1,0:T(8,128)(2,1)} %get-tuple-element.36.g_ref, ...), custom_call_target="tpu_custom_call" | custom-call | flops 2147483648 | bytes 12582912 | tf_op jit(solution)/shard_map/attend_backward/pallas_call | solution.py:261
  95.7 11.9 %all-to-all-done.1.in_ref = bf16[32,16,1024]{2,1,0:T(8,128)(2,1)S(1)} async-done(((bf16[32,16,1024]{2,1,0:T(8,128)(2,1)}), bf16[32,16,1024]{2,1,0:T(8,128)(2,1)S(1)}, u32[]{:S(2)}, u32[]{:S(2)}) %all-to-all-start.1) | async-done | bytes 1048608 | tf_op jit(solution)/shard_map/all_to_all | solution.py:65
  107.5 0.8 own_rows.1
  108.3 0.0 collective-permute-done.8.g_ref
  108.3 0.0 copy-done.3
  108.3 6.2 %attend_backward.3 = (bf16[512,2048]{1,0:T(8,128)(2,1)}, bf16[512,2048]{1,0:T(8,128)(2,1)}, bf16[512,2048]{1,0:T(8,128)(2,1)}) custom-call(s32[1]{0:T(128)} %bitcast.base, bf16[512,2048]{1,0:T(8,128)(2,1)} %q_ref.7, bf16[512,2048]{1,0:T(8,128)(2,1)} %k_ref.7, bf16[512,2048]{1,0:T(8,128)(2,1)} %v_ref.7, ...), custom_call_target="tpu_custom_call", output_to_operand_aliasing={{0}: (7, {}), {1}: (8, {}), {2}: (9, {})} | custom-call | flops 2147483648 | bytes 12582912 | tf_op jit(solution)/shard_map/attend_backward/pallas_call | solution.py:261
  (3 shorter events, 0.0 us)
Async XLA Ops:
  0.6 25.9 %collective-permute-start = (bf16[512,2048]{1,0:T(8,128)(2,1)}, bf16[512,2048]{1,0:T(8,128)(2,1)}, u32[]{:S(2)}, u32[]{:S(2)}) collective-permute-start(bf16[512,2048]{1,0:T(8,128)(2,1)} %up_own_hbm.1), channel_id=1, source_target_pairs={{0,1},{1,0},{2,3},{3,2},{4,5},{5,4},{6,7},{7,6},{8,9},{9,8},{10,11... | collective-permute-start | bytes 6291464 | tf_op jit(solution)/shard_map/ppermute | solution.py:486
  8.8 11.3 %copy-start.1 = (bf16[512,2048]{1,0:T(8,128)(2,1)S(1)}, bf16[512,2048]{1,0:T(8,128)(2,1)}, u32[]{:S(2)}) copy-start(bf16[512,2048]{1,0:T(8,128)(2,1)} %q_ref.7) | copy-start | bytes 6291460
  8.8 11.3 %copy-start.5 = (s32[1,512]{1,0:T(1,128)S(1)}, s32[1,512]{1,0:T(1,128)}, u32[]{:S(2)}) copy-start(s32[1,512]{1,0:T(1,128)} %ids_ref.3) | copy-start | bytes 6148
  8.8 17.7 %collective-permute-start.1 = (bf16[512,1024]{1,0:T(8,128)(2,1)}, bf16[512,1024]{1,0:T(8,128)(2,1)}, u32[]{:S(2)}, u32[]{:S(2)}) collective-permute-start(bf16[512,1024]{1,0:T(8,128)(2,1)} %get-tuple-element.29.att_ref), channel_id=1, source_target_pairs={{0,1},{1,0},{2,3},{3,2},{4,5},{5,4},{6,7},{7,6},{8,9},{9,8},{10,11... | collective-permute-start | bytes 3145736 | tf_op jit(solution)/shard_map/ppermute | solution.py:491
  8.9 29.9 %all-to-all-start = ((bf16[32,16,1024]{2,1,0:T(8,128)(2,1)}), bf16[32,16,1024]{2,1,0:T(8,128)(2,1)S(1)}, u32[]{:S(2)}, u32[]{:S(2)}) async-start(bf16[32,16,1024]{2,1,0:T(8,128)(2,1)} %get-tuple-element.27), calls=%async_computation | async-start | bytes 2097152 | tf_op jit(solution)/shard_map/all_to_all | solution.py:65
  20.1 6.4 %copy-start.2 = (bf16[512,2048]{1,0:T(8,128)(2,1)S(1)}, bf16[512,2048]{1,0:T(8,128)(2,1)}, u32[]{:S(2)}) copy-start(bf16[512,2048]{1,0:T(8,128)(2,1)} %up_own_hbm.1) | copy-start | bytes 6291460
  34.5 1.0 copy-start.4
  38.8 31.8 %copy-start = (bf16[32,16,1024]{2,1,0:T(8,128)(2,1)}, bf16[32,16,1024]{2,1,0:T(8,128)(2,1)S(1)}, u32[]{:S(2)}) copy-start(bf16[32,16,1024]{2,1,0:T(8,128)(2,1)S(1)} %all-to-all-done) | copy-start | bytes 3145732
  38.8 15.0 %collective-permute-start.9 = (bf16[256,1024]{1,0:T(8,128)(2,1)S(1)}, bf16[256,1024]{1,0:T(8,128)(2,1)S(1)}, u32[]{:S(2)}, u32[]{:S(2)}) collective-permute-start(bf16[256,1024]{1,0:T(8,128)(2,1)S(1)} %get-tuple-element.44), channel_id=1, source_target_pairs={{0,32},{1,33},{2,34},{3,35},{4,36},{5,37},{6,38},{7,39},{8,40},{9,... | collective-permute-start | bytes 1572872 | tf_op jit(solution)/shard_map/ppermute | solution.py:437
  38.9 14.9 %collective-permute-start.6 = (bf16[256,1024]{1,0:T(8,128)(2,1)S(1)}, bf16[256,1024]{1,0:T(8,128)(2,1)S(1)}, u32[]{:S(2)}, u32[]{:S(2)}) collective-permute-start(bf16[256,1024]{1,0:T(8,128)(2,1)S(1)} %get-tuple-element.32), channel_id=1, source_target_pairs={{0,24},{1,25},{2,26},{3,27},{4,28},{5,29},{6,30},{7,31},{8,16},{9,... | collective-permute-start | bytes 1572872 | tf_op jit(solution)/shard_map/ppermute | solution.py:419
  40.1 13.8 %collective-permute-start.4 = (bf16[256,1024]{1,0:T(8,128)(2,1)S(1)}, bf16[256,1024]{1,0:T(8,128)(2,1)S(1)}, u32[]{:S(2)}, u32[]{:S(2)}) collective-permute-start(bf16[256,1024]{1,0:T(8,128)(2,1)S(1)} %get-tuple-element.32), channel_id=1, source_target_pairs={{0,6},{1,7},{2,0},{3,1},{4,2},{5,3},{6,4},{7,5},{8,14},{9,15},{10,... | collective-permute-start | bytes 1572872 | tf_op jit(solution)/shard_map/ppermute | solution.py:419
  41.8 14.8 %collective-permute-start.2 = (bf16[256,1024]{1,0:T(8,128)(2,1)S(1)}, bf16[256,1024]{1,0:T(8,128)(2,1)S(1)}, u32[]{:S(2)}, u32[]{:S(2)}) collective-permute-start(bf16[256,1024]{1,0:T(8,128)(2,1)S(1)} %get-tuple-element.32), channel_id=1, source_target_pairs={{0,96},{1,97},{2,98},{3,99},{4,100},{5,101},{6,102},{7,103},{8,104... | collective-permute-start | bytes 1572872 | tf_op jit(solution)/shard_map/ppermute | solution.py:419
  43.3 13.3 %collective-permute-start.7 = (bf16[256,1024]{1,0:T(8,128)(2,1)S(1)}, bf16[256,1024]{1,0:T(8,128)(2,1)S(1)}, u32[]{:S(2)}, u32[]{:S(2)}) collective-permute-start(bf16[256,1024]{1,0:T(8,128)(2,1)S(1)} %get-tuple-element.33), channel_id=1, source_target_pairs={{0,16},{1,17},{2,18},{3,19},{4,20},{5,21},{6,22},{7,23},{8,24},{9,... | collective-permute-start | bytes 1572872 | tf_op jit(solution)/shard_map/ppermute | solution.py:419
  53.8 14.1 %collective-permute-start.5 = (bf16[256,1024]{1,0:T(8,128)(2,1)S(1)}, bf16[256,1024]{1,0:T(8,128)(2,1)S(1)}, u32[]{:S(2)}, u32[]{:S(2)}) collective-permute-start(bf16[256,1024]{1,0:T(8,128)(2,1)S(1)} %get-tuple-element.33), channel_id=1, source_target_pairs={{0,2},{1,3},{2,4},{3,5},{4,6},{5,7},{6,0},{7,1},{8,10},{9,11},{10,... | collective-permute-start | bytes 1572872 | tf_op jit(solution)/shard_map/ppermute | solution.py:419
  53.8 16.8 %copy-start.6 = (bf16[256,1024]{1,0:T(8,128)(2,1)}, bf16[256,1024]{1,0:T(8,128)(2,1)S(1)}, u32[]{:S(2)}) copy-start(bf16[256,1024]{1,0:T(8,128)(2,1)S(1)} %collective-permute-done.6.refs_5_) | copy-start | bytes 1572868
  53.8 14.2 %collective-permute-start.3 = (bf16[256,1024]{1,0:T(8,128)(2,1)S(1)}, bf16[256,1024]{1,0:T(8,128)(2,1)S(1)}, u32[]{:S(2)}, u32[]{:S(2)}) collective-permute-start(bf16[256,1024]{1,0:T(8,128)(2,1)S(1)} %get-tuple-element.33), channel_id=1, source_target_pairs={{0,32},{1,33},{2,34},{3,35},{4,36},{5,37},{6,38},{7,39},{8,40},{9,... | collective-permute-start | bytes 1572872 | tf_op jit(solution)/shard_map/ppermute | solution.py:419
  53.9 16.7 %copy-start.7 = (bf16[256,1024]{1,0:T(8,128)(2,1)}, bf16[256,1024]{1,0:T(8,128)(2,1)S(1)}, u32[]{:S(2)}) copy-start(bf16[256,1024]{1,0:T(8,128)(2,1)S(1)} %collective-permute-done.4.refs_3_) | copy-start | bytes 1572868
  53.9 25.5 %collective-permute-start.10 = (bf16[256,1024]{1,0:T(8,128)(2,1)S(1)}, bf16[256,1024]{1,0:T(8,128)(2,1)S(1)}, u32[]{:S(2)}, u32[]{:S(2)}) collective-permute-start(bf16[256,1024]{1,0:T(8,128)(2,1)S(1)} %get-tuple-element.45), channel_id=1, source_target_pairs={{0,96},{1,97},{2,98},{3,99},{4,100},{5,101},{6,102},{7,103},{8,104... | collective-permute-start | bytes 1572872 | tf_op jit(solution)/shard_map/ppermute | solution.py:437
  56.6 14.1 %copy-start.8 = (bf16[256,1024]{1,0:T(8,128)(2,1)}, bf16[256,1024]{1,0:T(8,128)(2,1)S(1)}, u32[]{:S(2)}) copy-start(bf16[256,1024]{1,0:T(8,128)(2,1)S(1)} %collective-permute-done.2.refs_1_) | copy-start | bytes 1572868
  56.6 25.9 %collective-permute-start.11 = (bf16[256,1024]{1,0:T(8,128)(2,1)}, bf16[256,1024]{1,0:T(8,128)(2,1)S(1)}, u32[]{:S(2)}, u32[]{:S(2)}) collective-permute-start(bf16[256,1024]{1,0:T(8,128)(2,1)} %get-tuple-element.46), channel_id=1, source_target_pairs={{0,2},{1,3},{2,4},{3,5},{4,6},{5,7},{6,0},{7,1},{8,10},{9,11},{10,... | collective-permute-start | bytes 1572872 | tf_op jit(solution)/shard_map/ppermute | solution.py:437
  56.6 14.0 %copy-start.9 = (bf16[256,1024]{1,0:T(8,128)(2,1)}, bf16[256,1024]{1,0:T(8,128)(2,1)S(1)}, u32[]{:S(2)}) copy-start(bf16[256,1024]{1,0:T(8,128)(2,1)S(1)} %collective-permute-done.7.refs_6_) | copy-start | bytes 1572868
  56.6 25.9 %collective-permute-start.12 = (bf16[256,1024]{1,0:T(8,128)(2,1)}, bf16[256,1024]{1,0:T(8,128)(2,1)S(1)}, u32[]{:S(2)}, u32[]{:S(2)}) collective-permute-start(bf16[256,1024]{1,0:T(8,128)(2,1)} %get-tuple-element.47), channel_id=1, source_target_pairs={{0,6},{1,7},{2,0},{3,1},{4,2},{5,3},{6,4},{7,5},{8,14},{9,15},{10,... | collective-permute-start | bytes 1572872 | tf_op jit(solution)/shard_map/ppermute | solution.py:437
  68.0 2.7 %copy-start.10 = (bf16[256,1024]{1,0:T(8,128)(2,1)}, bf16[256,1024]{1,0:T(8,128)(2,1)S(1)}, u32[]{:S(2)}) copy-start(bf16[256,1024]{1,0:T(8,128)(2,1)S(1)} %collective-permute-done.5.refs_4_) | copy-start | bytes 1572868
  68.0 14.6 %collective-permute-start.13 = (bf16[256,1024]{1,0:T(8,128)(2,1)}, bf16[256,1024]{1,0:T(8,128)(2,1)S(1)}, u32[]{:S(2)}, u32[]{:S(2)}) collective-permute-start(bf16[256,1024]{1,0:T(8,128)(2,1)} %get-tuple-element.48), channel_id=1, source_target_pairs={{0,16},{1,17},{2,18},{3,19},{4,20},{5,21},{6,22},{7,23},{8,24},{9,... | collective-permute-start | bytes 1572872 | tf_op jit(solution)/shard_map/ppermute | solution.py:437
  68.0 2.6 %copy-start.11 = (bf16[256,1024]{1,0:T(8,128)(2,1)}, bf16[256,1024]{1,0:T(8,128)(2,1)S(1)}, u32[]{:S(2)}) copy-start(bf16[256,1024]{1,0:T(8,128)(2,1)S(1)} %collective-permute-done.3.refs_2_) | copy-start | bytes 1572868
  68.0 14.5 %collective-permute-start.14 = (bf16[256,1024]{1,0:T(8,128)(2,1)}, bf16[256,1024]{1,0:T(8,128)(2,1)S(1)}, u32[]{:S(2)}, u32[]{:S(2)}) collective-permute-start(bf16[256,1024]{1,0:T(8,128)(2,1)} %get-tuple-element.49), channel_id=1, source_target_pairs={{0,24},{1,25},{2,26},{3,27},{4,28},{5,29},{6,30},{7,31},{8,16},{9,... | collective-permute-start | bytes 1572872 | tf_op jit(solution)/shard_map/ppermute | solution.py:437
  79.4 28.9 %collective-permute-start.8 = (bf16[512,1024]{1,0:T(8,128)(2,1)}, bf16[512,1024]{1,0:T(8,128)(2,1)S(1)}, u32[]{:S(2)}, u32[]{:S(2)}) collective-permute-start(bf16[512,1024]{1,0:T(8,128)(2,1)} %get-tuple-element.34), channel_id=1, source_target_pairs={{0,1},{1,0},{2,3},{3,2},{4,5},{5,4},{6,7},{7,6},{8,9},{9,8},{10,11... | collective-permute-start | bytes 3145736 | tf_op jit(solution)/shard_map/ppermute | solution.py:500
  84.0 23.5 %all-to-all-start.1 = ((bf16[32,16,1024]{2,1,0:T(8,128)(2,1)}), bf16[32,16,1024]{2,1,0:T(8,128)(2,1)S(1)}, u32[]{:S(2)}, u32[]{:S(2)}) async-start(bf16[32,16,1024]{2,1,0:T(8,128)(2,1)} %bitcast.5), calls=%async_computation.1 | async-start | bytes 2097152 | tf_op jit(solution)/shard_map/all_to_all | solution.py:65
  89.1 19.3 %copy-start.3 = (bf16[512,1024]{1,0:T(8,128)(2,1)S(1)}, bf16[512,1024]{1,0:T(8,128)(2,1)}, u32[]{:S(2)}) copy-start(bf16[512,1024]{1,0:T(8,128)(2,1)} %get-tuple-element.29.att_ref) | copy-start | bytes 3145732
